TPU v7x, 256 devices: a whole 4x4x8 slice. The times are simulated.
256 devices in a mesh: group: 4 (over z_hi, core), fsdp: 64 (over x, z_lo, y).
Axes of the slice: x: 4, y: 4, z: 8 (z_hi: 2, z_lo: 4; z = z_hi * 4 + z_lo), core: 2. Of those that a mesh axis runs over, the one named last changes fastest.
Arguments:
- tokens: bfloat16 [4, 40960, 8192], P('group', 'fsdp'), may hold values from -16 to 16
- keys_grad: bfloat16 [4, 40960, 512], P('group', 'fsdp'), may hold values from -6 to 6
- norm_gain: float32 [8192], replicated, may hold values from 0.5 to 1.5
- weight: bfloat16 [8192, 512], P('fsdp'), may hold values from -6 to 6
- momentum: float32 [8192, 512], P('fsdp', 'group'), may hold values from -6 to 6
Outputs:
- new_weight: bfloat16 [8192, 512], P('fsdp')
- new_momentum: float32 [8192, 512], P('fsdp', 'group')
All inputs are finite; a program needn't handle non-finite values. Where the computation divides by a largest or mean magnitude, that divisor is 1e-20 or more.
Results may differ from a plain program's by a relative error of at most 0.0066.
Values may be sent and summed in bfloat16 or wider, within the bound.
No kernel may reach another device: no remote copies, remote signals or barrier semaphores. Data moves between devices by JAX's collectives and lax.ppermute only.
A program may use at most 128 MiB of HBM per device.

v0:
```python
import functools
import math

import jax
import jax.numpy as jnp
from jax import lax
from jax.experimental import pallas as pl
from jax.experimental.pallas import tpu as pltpu
from jax.sharding import Mesh
from jax.sharding import PartitionSpec as P


BLOCK = 128
ROWS_AT_A_TIME = 64
FSDP = ("x", "zl", "y")
GROUP = ("zh", "core")

norm_epsilon = 1e-05
inner_rate = 0.5
outer_rate = 0.7
momentum_decay = 0.9


def shift(block, axis, step):
    count = lax.axis_size(axis)
    return lax.ppermute(block, axis, [(i, (i + step) % count) for i in range(count)])


def onward(block, axis, step):
    route = [(i, (i + step) % 4) for i in range(4)] + [(4 + i, 4 + (i - step) % 4) for i in range(4)]
    return lax.ppermute(block, ("core", axis), route)


def swap(block, axis):
    return lax.ppermute(block, axis, [(0, 1), (1, 0)])


def wide(array):
    return array.astype(jnp.float32)


def narrow(array):
    return array.astype(jnp.bfloat16)


class Tiles:
    def __init__(self, place, distances):
        self.x, self.zl, self.y, self.core = (place[i] for i in range(4))
        self.distances = distances
        self.count = 4 * len(distances)

    def parts(self, turn):
        return turn // 4, (turn // 2) % 2, turn % 2

    def column(self, turn, block):
        at, colour, low = self.parts(turn)
        distance = self.distances[0] + 2 * at
        along = jnp.where(colour == 0, self.x, self.y)
        along = lax.rem(along + 4 + jnp.where(self.core == 0, distance, -distance), 4)
        line = lax.rem(self.zl + 2 * colour + low, 4)
        x, y = jnp.where(colour == 0, along, block), jnp.where(colour == 0, block, along)
        return pl.multiple_of(((x * 4 + line) * 4 + y) * BLOCK, BLOCK)

    def second(self, colour, block):
        across = jnp.where(colour == 0, self.y, self.x)
        return lax.rem(jnp.where(self.core == 0, block - across, across - block) + 4, 4)

    def products(self, grads, gain, tile_of, send, own, stage, sems):
        def out(turn, half):
            at, colour, low = self.parts(turn)
            if half == 0:
                at = len(self.distances) - 1 - at
            ref = (send, own)[half]
            return pltpu.make_async_copy(
                stage.at[half, at, colour, :, low], ref.at[at, colour, :, low], sems.at[half]
            )

        def body(turn, carry):
            at, colour, low = self.parts(turn)
            tile = tile_of(turn)
            full = jnp.dot(grads[...], tile, preferred_element_type=jnp.float32)
            rows = full.shape[0] // 2
            for k in range(4):
                scale = gain[:, pl.ds(self.column(turn, k), BLOCK)]
                block = (full[:, k * BLOCK : (k + 1) * BLOCK] * scale).astype(jnp.bfloat16)
                there = self.second(colour, k)
                stage[0, len(self.distances) - 1 - at, colour, lax.rem(4 - there, 4), low] = block[:rows]
                stage[1, at, colour, there, low] = block[rows:]
            out(turn, 0).start()
            out(turn, 1).start()
            return carry

        lax.fori_loop(0, self.count, body, 0)

        def drain(turn, carry):
            out(turn, 0).wait()
            out(turn, 1).wait()
            return carry

        lax.fori_loop(0, self.count, drain, 0)


def first_kernel(factor, place, tokens, keys, gain, send, own, grads, held, scaled, stage, load, sems):
    count = held.shape[0] // ROWS_AT_A_TIME

    def rows(i):
        return pl.ds(pl.multiple_of(i * ROWS_AT_A_TIME, ROWS_AT_A_TIME), ROWS_AT_A_TIME)

    def read(i):
        return pltpu.make_async_copy(tokens.at[rows(i)], held.at[rows(i)], load.at[i])

    for i in range(count):
        read(i).start()

    def squares(i, carry):
        read(i).wait()
        total = jnp.zeros((ROWS_AT_A_TIME, BLOCK), jnp.float32)

        def add(j, total):
            for k in range(8):
                part = held[rows(i), pl.ds(pl.multiple_of((j * 8 + k) * BLOCK, BLOCK), BLOCK)].astype(jnp.float32)
                total = total + part * part
            return total

        total = lax.fori_loop(0, held.shape[1] // (8 * BLOCK), add, total)
        meansq = jnp.sum(total, axis=1, keepdims=True) / held.shape[1]
        scale = lax.rsqrt(meansq + norm_epsilon) * factor
        scaled[rows(i)] = keys[rows(i)].astype(jnp.float32) * scale
        return carry

    lax.fori_loop(0, count, squares, 0)

    core = place[3]
    for group in range(4):
        mine = jnp.where(core == group % 2, 2, 0)
        at = pl.ds(pl.multiple_of((mine + group // 2) * BLOCK, BLOCK), BLOCK)
        for t in range(held.shape[0] // BLOCK):
            square = scaled[t * BLOCK : (t + 1) * BLOCK, group * BLOCK : (group + 1) * BLOCK]
            grads[at, t * BLOCK : (t + 1) * BLOCK] = square.T.astype(jnp.bfloat16)

    tiles = Tiles(place, (2,))

    def tile_of(turn):
        return jnp.concatenate([held[:, pl.ds(tiles.column(turn, k), BLOCK)] for k in range(4)], axis=1)

    tiles.products(grads, gain, tile_of, send, own, stage, sems)


def later_kernel(distances, place, tokens, grads, gain, send, own, held, stage, load, sems):
    tiles = Tiles(place, distances)

    def read(turn, k):
        return pltpu.make_async_copy(
            tokens.at[:, pl.ds(tiles.column(turn, k), BLOCK)],
            held.at[turn, :, k * BLOCK : (k + 1) * BLOCK],
            load.at[turn, k],
        )

    for turn in range(tiles.count):
        for k in range(4):
            read(turn, k).start()

    def tile_of(turn):
        for k in range(4):
            read(turn, k).wait()
        return held[turn]

    tiles.products(grads, gain, tile_of, send, own, stage, sems)


def first_terms(place, tokens, keys, gain, factor):
    count, width = tokens.shape
    cols = keys.shape[1]
    part = jax.ShapeDtypeStruct((1, 2, 4, 2, cols // 2, BLOCK), jnp.bfloat16)
    any_space = pl.BlockSpec(memory_space=pl.ANY)
    in_vmem = pl.BlockSpec(memory_space=pltpu.VMEM)
    in_smem = pl.BlockSpec(memory_space=pltpu.SMEM)
    return pl.pallas_call(
        functools.partial(first_kernel, factor),
        out_shape=[part, part, jax.ShapeDtypeStruct((cols, count), jnp.bfloat16)],
        in_specs=[in_smem, any_space, in_vmem, in_vmem],
        out_specs=[any_space, any_space, in_vmem],
        scratch_shapes=[
            pltpu.VMEM((count, width), jnp.bfloat16),
            pltpu.VMEM((count, cols), jnp.float32),
            pltpu.VMEM((2,) + part.shape, jnp.bfloat16),
            pltpu.SemaphoreType.DMA((count // ROWS_AT_A_TIME,)),
            pltpu.SemaphoreType.DMA((2,)),
        ],
        cost_estimate=pl.CostEstimate(
            flops=count * width * cols // 2, bytes_accessed=2 * count * width, transcendentals=0
        ),
        compiler_params=pltpu.CompilerParams(vmem_limit_bytes=56 * 2**20),
    )(place, tokens, keys, gain)


def later_terms(distances, place, tokens, grads, gain):
    count, width = tokens.shape
    cols = grads.shape[0]
    part = jax.ShapeDtypeStruct((len(distances), 2, 4, 2, cols // 2, BLOCK), jnp.bfloat16)
    any_space = pl.BlockSpec(memory_space=pl.ANY)
    in_vmem = pl.BlockSpec(memory_space=pltpu.VMEM)
    in_smem = pl.BlockSpec(memory_space=pltpu.SMEM)
    turns = 4 * len(distances)
    return pl.pallas_call(
        functools.partial(later_kernel, distances),
        out_shape=[part, part],
        in_specs=[in_smem, any_space, in_vmem, in_vmem],
        out_specs=[any_space, any_space],
        scratch_shapes=[
            pltpu.VMEM((turns, count, 4 * BLOCK), jnp.bfloat16),
            pltpu.VMEM((2,) + part.shape, jnp.bfloat16),
            pltpu.SemaphoreType.DMA((turns, 4)),
            pltpu.SemaphoreType.DMA((2,)),
        ],
        cost_estimate=pl.CostEstimate(
            flops=2 * turns * count * cols * 4 * BLOCK, bytes_accessed=2 * count * width, transcendentals=0
        ),
        compiler_params=pltpu.CompilerParams(vmem_limit_bytes=52 * 2**20),
    )(place, tokens, grads, gain)


def ring_sum(terms, axis):
    far = onward(narrow(terms[2]), axis, 1)
    back = onward(narrow(terms[3]), axis, -1)
    front = onward(narrow(terms[1] + wide(far)), axis, 1)
    return terms[0] + wide(back) + wide(front)


def per_device(tokens, keys_grad, norm_gain, weight, momentum):
    x, zl, y, zh, core = (lax.axis_index(a) for a in FSDP + GROUP)
    rows, cols = momentum.shape
    groups = lax.axis_size(GROUP)
    factor = inner_rate / math.sqrt(lax.axis_size(FSDP) * tokens.shape[1]) / groups
    place = jnp.stack([x, zl, y, core]).astype(jnp.int32)
    gain = norm_gain[None, :]
    axes = ("x", "y")

    send, own, grads = first_terms(place, tokens[0], keys_grad[0], gain, factor)
    received = swap(send, "core")
    far = [None, None]
    for c in (0, 1):
        far[c] = onward(narrow(wide(own[0, c]) + wide(received[0, c])), axes[c], 1)

    send, own = later_terms((1, 3), place, tokens[0], grads, gain)
    received = swap(send, "core")
    sides = [[wide(own[i, c]) + wide(received[i, c]) for i in (0, 1)] for c in (0, 1)]
    back = [None, None]
    for c in (0, 1):
        back[c] = onward(narrow(sides[c][1]), axes[c], -1)

    send, own = later_terms((0,), place, tokens[0], grads, gain)
    received = swap(send, "core")
    front = [onward(narrow(sides[c][0] + wide(far[c])), axes[c], 1) for c in (0, 1)]
    sums = [wide(own[0, c]) + wide(received[0, c]) + wide(back[c]) + wide(front[c]) for c in (0, 1)]

    sums = [ring_sum(sums[0], "y"), ring_sum(sums[1], "x")]
    lines = [sums[0][0], sums[0][1], sums[1][0], sums[1][1]]
    partial = lines[0]
    for step in (1, 2, 3):
        partial += wide(shift(narrow(lines[step]), "zl", step))

    partial = partial.reshape(2, cols, rows)
    both_rate = 1 + momentum_decay
    mine = (jnp.arange(2) == zh)[:, None, None]
    joined = narrow(partial + jnp.where(mine, momentum.T * (momentum_decay**2 / both_rate), 0.0))
    received = swap(joined, "zh")
    update = wide(joined) + wide(received)
    updates = jnp.stack([update, swap(update, "core")])
    updates = jnp.where(core == 0, updates, updates[::-1])
    average = jnp.where(zh == 0, partial[0] + wide(received[0]), partial[1] + wide(received[1]))

    new_momentum = momentum_decay * momentum + average.T
    updates = updates.transpose(3, 1, 0, 2).reshape(rows, 4 * cols)
    new_weight = narrow(wide(weight) - outer_rate * both_rate * updates)
    return (new_weight, new_momentum)


def solution(mesh):
    finer = Mesh(mesh.devices.reshape(2, 2, 4, 4, 4), GROUP + FSDP)
    in_specs = (
        P(GROUP, FSDP, None),
        P(GROUP, FSDP, None),
        P(),
        P(FSDP, None),
        P(FSDP, GROUP),
    )
    out_specs = (P(FSDP, None), P(FSDP, GROUP))
    return jax.shard_map(per_device, mesh=finer, in_specs=in_specs, out_specs=out_specs, check_vma=False)
```

profile of v0, /device:TPU:1, one launch (start us, length us, event | category | flops | bytes accessed | tf_op | source)
XLA Modules:
  0.0 100.7 jit_solution(5815099793879426120)
XLA Ops:
  0.6 0.6 pad_add_fusion.place
  1.3 11.3 %shard_map.68 = (bf16[1,2,4,2,256,128]{5,4,3,2,1,0:T(8,128)(2,1)}, bf16[1,2,4,2,256,128]{5,4,3,2,1,0:T(8,128)(2,1)}, bf16[512,640]{1,0:T(8,128)(2,1)}) custom-call(s32[4]{0:T(128)} %pad_add_fusion.place, bf16[640,8192]{1,0:T(8,128)(2,1)} %bitcast.110, bf16[640,512]{1,0:T(8,128)(2,1)} %bitcast.115, f32[1,8192]{1,0:T(1,128)} %bitcast.107), custom_call_target="tpu_custom_call" | custom-call | flops 1342177280 | bytes 10485760 | tf_op jit(solution)/shard_map/pallas_call | solution.py:178
  12.6 1.1 %copy-done = bf16[512,640]{1,0:T(8,128)(2,1)S(1)} copy-done((bf16[512,640]{1,0:T(8,128)(2,1)S(1)}, bf16[512,640]{1,0:T(8,128)(2,1)}, u32[]{:S(2)}) %copy-start) | copy-done | bytes 655384
  13.7 8.0 %shard_map.70 = (bf16[2,2,4,2,256,128]{5,4,3,2,1,0:T(8,128)(2,1)}, bf16[2,2,4,2,256,128]{5,4,3,2,1,0:T(8,128)(2,1)}) custom-call(s32[4]{0:T(128)S(1)} %copy-done.2, bf16[640,8192]{1,0:T(8,128)(2,1)} %bitcast.111, bf16[512,640]{1,0:T(8,128)(2,1)S(1)} %copy-done, f32[1,8192]{1,0:T(1,128)S(1)} %bitcast.108), custom_call_target="tpu_custom_call" | custom-call | flops 2684354560 | bytes 10485760 | tf_op jit(solution)/shard_map/pallas_call | solution.py:205
  21.8 3.3 %collective-permute-start.1 = (bf16[2,2,4,2,256,128]{5,4,3,2,1,0:T(8,128)(2,1)}, bf16[2,2,4,2,256,128]{5,4,3,2,1,0:T(8,128)(2,1)S(1)}, u32[]{:S(2)}, u32[]{:S(2)}) collective-permute-start(bf16[2,2,4,2,256,128]{5,4,3,2,1,0:T(8,128)(2,1)} %get-tuple-element.13), channel_id=1, source_target_pairs={{0,64},{64,0},{1,65},{65,1},{2,66},{66,2},{3,67},{67,3},{4,68},{68... | collective-permute-start | bytes 6291464 | tf_op jit(solution)/shard_map/ppermute | solution.py:35
  25.2 5.4 %collective-permute-done.3 = bf16[1,2,4,2,256,128]{5,4,3,2,1,0:T(8,128)(2,1)S(1)} collective-permute-done((bf16[1,2,4,2,256,128]{5,4,3,2,1,0:T(8,128)(2,1)S(1)}, bf16[1,2,4,2,256,128]{5,4,3,2,1,0:T(8,128)(2,1)S(1)}, u32[]{:S(2)}, u32[]{:S(2)}) %collective-permute-start.3) | collective-permute-done | bytes 1048608 | tf_op jit(solution)/shard_map/ppermute | solution.py:35
  30.8 1.1 %collective-permute-start.11 = (bf16[4,2,256,128]{3,2,1,0:T(8,128)(2,1)S(1)}, bf16[4,2,256,128]{3,2,1,0:T(8,128)(2,1)S(1)}, u32[]{:S(2)}, u32[]{:S(2)}) collective-permute-start(bf16[4,2,256,128]{3,2,1,0:T(8,128)(2,1)S(1)} %get-tuple-element.30), channel_id=1, source_target_pairs={{0,1},{1,2},{2,3},{3,0},{64,67},{65,64},{66,65},{67,66},{4,5},{5,6... | collective-permute-start | bytes 1572872 | tf_op jit(solution)/shard_map/ppermute | solution.py:31
  31.9 2.5 %collective-permute-start.4 = (bf16[4,2,256,128]{3,2,1,0:T(8,128)(2,1)S(1)}, bf16[4,2,256,128]{3,2,1,0:T(8,128)(2,1)S(1)}, u32[]{:S(2)}, u32[]{:S(2)}) collective-permute-start(bf16[4,2,256,128]{3,2,1,0:T(8,128)(2,1)S(1)} %get-tuple-element.31), channel_id=1, source_target_pairs={{0,16},{16,32},{32,48},{48,0},{64,112},{80,64},{96,80},{112,96},{1... | collective-permute-start | bytes 1572872 | tf_op jit(solution)/shard_map/ppermute | solution.py:31
  34.4 5.2 %shard_map.69 = (bf16[1,2,4,2,256,128]{5,4,3,2,1,0:T(8,128)(2,1)S(1)}, bf16[1,2,4,2,256,128]{5,4,3,2,1,0:T(8,128)(2,1)}) custom-call(s32[4]{0:T(128)S(1)} %copy-done.2, bf16[640,8192]{1,0:T(8,128)(2,1)} %bitcast.112, bf16[512,640]{1,0:T(8,128)(2,1)S(1)} %copy-done, f32[1,8192]{1,0:T(1,128)S(1)} %bitcast.109), custom_call_target="tpu_custom_call" | custom-call | flops 1342177280 | bytes 10485760 | tf_op jit(solution)/shard_map/pallas_call | solution.py:205
  39.8 0.8 collective-permute-done.4
  40.5 1.4 %fusion = (bf16[4,2,256,128]{3,2,1,0:T(8,128)(2,1)}, bf16[4,2,256,128]{3,2,1,0:T(8,128)(2,1)}) fusion(bf16[4,2,256,128]{3,2,1,0:T(8,128)(2,1)S(1)} %collective-permute-done.11, bf16[2,2,4,2,256,128]{5,4,3,2,1,0:T(8,128)(2,1)S(1)} %collective-permute-done.1, bf16[2,2,4,2,256,128]{5,4,3,2,1,0:T(8,128)(2,1)S(1)} %copy-done.3, ...), kind=kLoop, calls=%fused_computation.1 | loop fusion | flops 3145728 | bytes 4194304 | tf_op jit(solution)/shard_map/convert_element_type | solution.py:43
  41.9 0.9 collective-permute-start.12
  42.9 1.3 %fusion.6 = (bf16[4,2,256,128]{3,2,1,0:T(8,128)(2,1)}, bf16[4,2,256,128]{3,2,1,0:T(8,128)(2,1)}) fusion(bf16[2,2,4,2,256,128]{5,4,3,2,1,0:T(8,128)(2,1)S(1)} %collective-permute-done.1, bf16[2,2,4,2,256,128]{5,4,3,2,1,0:T(8,128)(2,1)S(1)} %copy-done.3), kind=kLoop, calls=%fused_computation.14 | loop fusion | flops 2097152 | bytes 3145728 | tf_op jit(solution)/shard_map/convert_element_type | solution.py:43
  44.7 3.1 %collective-permute-start.5 = (bf16[4,2,256,128]{3,2,1,0:T(8,128)(2,1)}, bf16[4,2,256,128]{3,2,1,0:T(8,128)(2,1)}, u32[]{:S(2)}, u32[]{:S(2)}) collective-permute-start(bf16[4,2,256,128]{3,2,1,0:T(8,128)(2,1)} %get-tuple-element.27), channel_id=1, source_target_pairs={{0,16},{16,32},{32,48},{48,0},{64,112},{80,64},{96,80},{112,96},{1... | collective-permute-start | bytes 1572872 | tf_op jit(solution)/shard_map/ppermute | solution.py:31
  47.9 4.0 %collective-permute-done.12 = bf16[4,2,256,128]{3,2,1,0:T(8,128)(2,1)} collective-permute-done((bf16[4,2,256,128]{3,2,1,0:T(8,128)(2,1)}, bf16[4,2,256,128]{3,2,1,0:T(8,128)(2,1)}, u32[]{:S(2)}, u32[]{:S(2)}) %collective-permute-start.12) | collective-permute-done | bytes 524320 | tf_op jit(solution)/shard_map/ppermute | solution.py:31
  51.9 7.2 %collective-permute-done.10 = bf16[4,2,256,128]{3,2,1,0:T(8,128)(2,1)} collective-permute-done((bf16[4,2,256,128]{3,2,1,0:T(8,128)(2,1)}, bf16[4,2,256,128]{3,2,1,0:T(8,128)(2,1)}, u32[]{:S(2)}, u32[]{:S(2)}) %collective-permute-start.10) | collective-permute-done | bytes 524320 | tf_op jit(solution)/shard_map/ppermute | solution.py:31
  59.1 3.8 %collective-permute-done.2 = bf16[4,2,256,128]{3,2,1,0:T(8,128)(2,1)} collective-permute-done((bf16[4,2,256,128]{3,2,1,0:T(8,128)(2,1)}, bf16[4,2,256,128]{3,2,1,0:T(8,128)(2,1)}, u32[]{:S(2)}, u32[]{:S(2)}) %collective-permute-start.2) | collective-permute-done | bytes 524320 | tf_op jit(solution)/shard_map/ppermute | solution.py:31
  62.9 2.2 %fusion.28 = (bf16[4,2,256,128]{3,2,1,0:T(8,128)(2,1)S(1)}, f32[4,2,256,128]{3,2,1,0:T(8,128)S(1)}, bf16[4,2,256,128]{3,2,1,0:T(8,128)(2,1)S(1)}, f32[4,2,256,128]{3,2,1,0:T(8,128)S(1)}) fusion(bf16[4,2,256,128]{3,2,1,0:T(8,128)(2,1)} %collective-permute-done.12, bf16[4,2,256,128]{3,2,1,0:T(8,128)(2,1)} %collective-permute-done.10, ...), kind=kLoop, calls=%fused_computation.60 | loop fusion | flops 4194304 | bytes 7340032 | tf_op jit(solution)/shard_map/convert.5
  65.2 1.9 %collective-permute-start.7 = (bf16[2,256,128]{2,1,0:T(8,128)(2,1)S(1)}, bf16[2,256,128]{2,1,0:T(8,128)(2,1)S(1)}, u32[]{:S(2)}, u32[]{:S(2)}) collective-permute-start(bf16[2,256,128]{2,1,0:T(8,128)(2,1)S(1)} %get-tuple-element.35), channel_id=1, source_target_pairs={{0,1},{1,2},{2,3},{3,0},{64,67},{65,64},{66,65},{67,66},{4,5},{5,6... | collective-permute-start | bytes 393224 | tf_op jit(solution)/shard_map/ppermute | solution.py:31
  67.1 1.4 %collective-permute-start.13 = (bf16[2,256,128]{2,1,0:T(8,128)(2,1)S(1)}, bf16[2,256,128]{2,1,0:T(8,128)(2,1)S(1)}, u32[]{:S(2)}, u32[]{:S(2)}) collective-permute-start(bf16[2,256,128]{2,1,0:T(8,128)(2,1)S(1)} %get-tuple-element.32), channel_id=1, source_target_pairs={{0,48},{16,0},{32,16},{48,32},{64,80},{80,96},{96,112},{112,64},{1... | collective-permute-start | bytes 393224 | tf_op jit(solution)/shard_map/ppermute | solution.py:31
  69.0 1.3 %collective-permute-start.15 = (bf16[2,256,128]{2,1,0:T(8,128)(2,1)S(1)}, bf16[2,256,128]{2,1,0:T(8,128)(2,1)S(1)}, u32[]{:S(2)}, u32[]{:S(2)}) collective-permute-start(bf16[2,256,128]{2,1,0:T(8,128)(2,1)S(1)} %fusion.11), channel_id=1, source_target_pairs={{0,16},{16,32},{32,48},{48,0},{64,112},{80,64},{96,80},{112,96},{1... | collective-permute-start | bytes 393224 | tf_op jit(solution)/shard_map/ppermute | solution.py:31
  70.4 2.3 %collective-permute-start.8 = (bf16[2,256,128]{2,1,0:T(8,128)(2,1)S(1)}, bf16[2,256,128]{2,1,0:T(8,128)(2,1)S(1)}, u32[]{:S(2)}, u32[]{:S(2)}) collective-permute-start(bf16[2,256,128]{2,1,0:T(8,128)(2,1)S(1)} %fusion.16), channel_id=1, source_target_pairs={{0,1},{1,2},{2,3},{3,0},{64,67},{65,64},{66,65},{67,66},{4,5},{5,6... | collective-permute-start | bytes 393224 | tf_op jit(solution)/shard_map/ppermute | solution.py:31
  72.9 1.1 %collective-permute-done.15 = bf16[2,256,128]{2,1,0:T(8,128)(2,1)S(1)} collective-permute-done((bf16[2,256,128]{2,1,0:T(8,128)(2,1)S(1)}, bf16[2,256,128]{2,1,0:T(8,128)(2,1)S(1)}, u32[]{:S(2)}, u32[]{:S(2)}) %collective-permute-start.15) | collective-permute-done | bytes 131104 | tf_op jit(solution)/shard_map/ppermute | solution.py:31
  74.1 5.6 %collective-permute-start.17 = (bf16[256,128]{1,0:T(8,128)(2,1)S(1)}, bf16[256,128]{1,0:T(8,128)(2,1)S(1)}, u32[]{:S(2)}, u32[]{:S(2)}) collective-permute-start(bf16[256,128]{1,0:T(8,128)(2,1)S(1)} %get-tuple-element.39), channel_id=1, source_target_pairs={{0,12},{4,0},{8,4},{12,8},{1,13},{5,1},{9,5},{13,9},{2,14},{6,2},{... | collective-permute-start | bytes 196616 | tf_op jit(solution)/shard_map/ppermute | solution.py:26
  80.2 0.8 collective-permute-done.17
  81.0 2.7 %collective-permute-done.16 = bf16[256,128]{1,0:T(8,128)(2,1)S(1)} collective-permute-done((bf16[256,128]{1,0:T(8,128)(2,1)S(1)}, bf16[256,128]{1,0:T(8,128)(2,1)S(1)}, u32[]{:S(2)}, u32[]{:S(2)}) %collective-permute-start.16) | collective-permute-done | bytes 65568 | tf_op jit(solution)/shard_map/ppermute | solution.py:26
  83.6 1.2 %collective-permute-done.9 = bf16[256,128]{1,0:T(8,128)(2,1)S(1)} collective-permute-done((bf16[256,128]{1,0:T(8,128)(2,1)S(1)}, bf16[256,128]{1,0:T(8,128)(2,1)S(1)}, u32[]{:S(2)}, u32[]{:S(2)}) %collective-permute-start.9) | collective-permute-done | bytes 65568 | tf_op jit(solution)/shard_map/ppermute | solution.py:26
  84.9 4.1 %collective-permute-start.18 = (bf16[2,128,128]{2,1,0:T(8,128)(2,1)S(1)}, bf16[2,128,128]{2,1,0:T(8,128)(2,1)S(1)}, u32[]{:S(2)}, u32[]{:S(2)}) collective-permute-start(bf16[2,128,128]{2,1,0:T(8,128)(2,1)S(1)} %add_convert_fusion.4), channel_id=1, source_target_pairs={{0,128},{128,0},{1,129},{129,1},{2,130},{130,2},{3,131},{131,3},{4... | collective-permute-start | bytes 196616 | tf_op jit(solution)/shard_map/ppermute | solution.py:35
  89.3 3.3 %collective-permute-done.18 = bf16[2,128,128]{2,1,0:T(8,128)(2,1)S(1)} collective-permute-done((bf16[2,128,128]{2,1,0:T(8,128)(2,1)S(1)}, bf16[2,128,128]{2,1,0:T(8,128)(2,1)S(1)}, u32[]{:S(2)}, u32[]{:S(2)}) %collective-permute-start.18) | collective-permute-done | bytes 65568 | tf_op jit(solution)/shard_map/ppermute | solution.py:35
  92.7 6.1 %collective-permute-start.19 = (f32[2,128,128]{2,1,0:T(8,128)S(1)}, f32[2,128,128]{2,1,0:T(8,128)S(1)}, u32[]{:S(2)}, u32[]{:S(2)}) collective-permute-start(f32[2,128,128]{2,1,0:T(8,128)S(1)} %get-tuple-element.37), channel_id=1, source_target_pairs={{0,64},{64,0},{1,65},{65,1},{2,66},{66,2},{3,67},{67,3},{4,68},{68... | collective-permute-start | bytes 393224 | tf_op jit(solution)/shard_map/ppermute | solution.py:35
  98.8 0.7 copy.15
  99.9 0.8 copy.14
  (57 shorter events, 3.3 us)
Async XLA Ops:
  1.3 11.4 %copy-start.1 = (f32[8192]{0:T(1024)S(1)}, f32[8192]{0:T(1024)}, u32[]{:S(2)}) copy-start(f32[8192]{0:T(1024)} %param.7) | copy-start | bytes 98308
  1.3 11.4 %copy-start.2 = (s32[4]{0:T(128)S(1)}, s32[4]{0:T(128)}, u32[]{:S(2)}) copy-start(s32[4]{0:T(128)} %pad_add_fusion.place) | copy-start | bytes 52
  12.6 1.1 %copy-start = (bf16[512,640]{1,0:T(8,128)(2,1)S(1)}, bf16[512,640]{1,0:T(8,128)(2,1)}, u32[]{:S(2)}) copy-start(bf16[512,640]{1,0:T(8,128)(2,1)} %get-tuple-element.9.grads) | copy-start | bytes 1966084
  13.7 11.3 %copy-start.8 = (bf16[1,2,4,2,256,128]{5,4,3,2,1,0:T(8,128)(2,1)S(1)}, bf16[1,2,4,2,256,128]{5,4,3,2,1,0:T(8,128)(2,1)}, u32[]{:S(2)}) copy-start(bf16[1,2,4,2,256,128]{5,4,3,2,1,0:T(8,128)(2,1)} %get-tuple-element.15) | copy-start | bytes 3145732
  13.7 16.8 %copy-start.5 = (bf16[1,2,4,2,256,128]{5,4,3,2,1,0:T(8,128)(2,1)S(1)}, bf16[1,2,4,2,256,128]{5,4,3,2,1,0:T(8,128)(2,1)}, u32[]{:S(2)}) copy-start(bf16[1,2,4,2,256,128]{5,4,3,2,1,0:T(8,128)(2,1)} %get-tuple-element.14) | copy-start | bytes 3145732
  21.8 18.8 %collective-permute-start.1 = (bf16[2,2,4,2,256,128]{5,4,3,2,1,0:T(8,128)(2,1)}, bf16[2,2,4,2,256,128]{5,4,3,2,1,0:T(8,128)(2,1)S(1)}, u32[]{:S(2)}, u32[]{:S(2)}) collective-permute-start(bf16[2,2,4,2,256,128]{5,4,3,2,1,0:T(8,128)(2,1)} %get-tuple-element.13), channel_id=1, source_target_pairs={{0,64},{64,0},{1,65},{65,1},{2,66},{66,2},{3,67},{67,3},{4,68},{68... | collective-permute-start | bytes 6291464 | tf_op jit(solution)/shard_map/ppermute | solution.py:35
  25.1 5.5 %collective-permute-start.3 = (bf16[1,2,4,2,256,128]{5,4,3,2,1,0:T(8,128)(2,1)S(1)}, bf16[1,2,4,2,256,128]{5,4,3,2,1,0:T(8,128)(2,1)S(1)}, u32[]{:S(2)}, u32[]{:S(2)}) collective-permute-start(bf16[1,2,4,2,256,128]{5,4,3,2,1,0:T(8,128)(2,1)S(1)} %copy-done.8), channel_id=1, source_target_pairs={{0,64},{64,0},{1,65},{65,1},{2,66},{66,2},{3,67},{67,3},{4,68},{68... | collective-permute-start | bytes 3145736 | tf_op jit(solution)/shard_map/ppermute | solution.py:35
  30.8 8.9 %collective-permute-start.11 = (bf16[4,2,256,128]{3,2,1,0:T(8,128)(2,1)S(1)}, bf16[4,2,256,128]{3,2,1,0:T(8,128)(2,1)S(1)}, u32[]{:S(2)}, u32[]{:S(2)}) collective-permute-start(bf16[4,2,256,128]{3,2,1,0:T(8,128)(2,1)S(1)} %get-tuple-element.30), channel_id=1, source_target_pairs={{0,1},{1,2},{2,3},{3,0},{64,67},{65,64},{66,65},{67,66},{4,5},{5,6... | collective-permute-start | bytes 1572872 | tf_op jit(solution)/shard_map/ppermute | solution.py:31
  31.9 8.6 %copy-start.3 = (bf16[2,2,4,2,256,128]{5,4,3,2,1,0:T(8,128)(2,1)S(1)}, bf16[2,2,4,2,256,128]{5,4,3,2,1,0:T(8,128)(2,1)}, u32[]{:S(2)}) copy-start(bf16[2,2,4,2,256,128]{5,4,3,2,1,0:T(8,128)(2,1)} %get-tuple-element.12) | copy-start | bytes 6291460
  31.9 8.6 %collective-permute-start.4 = (bf16[4,2,256,128]{3,2,1,0:T(8,128)(2,1)S(1)}, bf16[4,2,256,128]{3,2,1,0:T(8,128)(2,1)S(1)}, u32[]{:S(2)}, u32[]{:S(2)}) collective-permute-start(bf16[4,2,256,128]{3,2,1,0:T(8,128)(2,1)S(1)} %get-tuple-element.31), channel_id=1, source_target_pairs={{0,16},{16,32},{32,48},{48,0},{64,112},{80,64},{96,80},{112,96},{1... | collective-permute-start | bytes 1572872 | tf_op jit(solution)/shard_map/ppermute | solution.py:31
  39.7 8.3 %collective-permute-start = (bf16[1,2,4,2,256,128]{5,4,3,2,1,0:T(8,128)(2,1)S(1)}, bf16[1,2,4,2,256,128]{5,4,3,2,1,0:T(8,128)(2,1)S(1)}, u32[]{:S(2)}, u32[]{:S(2)}) collective-permute-start(bf16[1,2,4,2,256,128]{5,4,3,2,1,0:T(8,128)(2,1)S(1)} %get-tuple-element.11), channel_id=1, source_target_pairs={{0,64},{64,0},{1,65},{65,1},{2,66},{66,2},{3,67},{67,3},{4,68},{68... | collective-permute-start | bytes 3145736 | tf_op jit(solution)/shard_map/ppermute | solution.py:35
  41.9 5.9 %copy-start.6 = (f32[128,128]{1,0:T(8,128)S(1)}, f32[128,128]{1,0:T(8,128)}, u32[]{:S(2)}) copy-start(f32[128,128]{1,0:T(8,128)} %param.9) | copy-start | bytes 196612
  41.9 21.0 %copy-start.4 = (bf16[1,2,4,2,256,128]{5,4,3,2,1,0:T(8,128)(2,1)S(1)}, bf16[1,2,4,2,256,128]{5,4,3,2,1,0:T(8,128)(2,1)}, u32[]{:S(2)}) copy-start(bf16[1,2,4,2,256,128]{5,4,3,2,1,0:T(8,128)(2,1)} %get-tuple-element.10) | copy-start | bytes 3145732
  41.9 9.9 %collective-permute-start.12 = (bf16[4,2,256,128]{3,2,1,0:T(8,128)(2,1)}, bf16[4,2,256,128]{3,2,1,0:T(8,128)(2,1)}, u32[]{:S(2)}, u32[]{:S(2)}) collective-permute-start(bf16[4,2,256,128]{3,2,1,0:T(8,128)(2,1)} %get-tuple-element.26), channel_id=1, source_target_pairs={{0,1},{1,2},{2,3},{3,0},{64,67},{65,64},{66,65},{67,66},{4,5},{5,6... | collective-permute-start | bytes 1572872 | tf_op jit(solution)/shard_map/ppermute | solution.py:31
  44.2 15.0 %collective-permute-start.10 = (bf16[4,2,256,128]{3,2,1,0:T(8,128)(2,1)}, bf16[4,2,256,128]{3,2,1,0:T(8,128)(2,1)}, u32[]{:S(2)}, u32[]{:S(2)}) collective-permute-start(bf16[4,2,256,128]{3,2,1,0:T(8,128)(2,1)} %get-tuple-element.24), channel_id=1, source_target_pairs={{0,3},{1,0},{2,1},{3,2},{64,65},{65,66},{66,67},{67,64},{4,7},{5,4... | collective-permute-start | bytes 1572872 | tf_op jit(solution)/shard_map/ppermute | solution.py:31
  44.7 14.4 %collective-permute-start.5 = (bf16[4,2,256,128]{3,2,1,0:T(8,128)(2,1)}, bf16[4,2,256,128]{3,2,1,0:T(8,128)(2,1)}, u32[]{:S(2)}, u32[]{:S(2)}) collective-permute-start(bf16[4,2,256,128]{3,2,1,0:T(8,128)(2,1)} %get-tuple-element.27), channel_id=1, source_target_pairs={{0,16},{16,32},{32,48},{48,0},{64,112},{80,64},{96,80},{112,96},{1... | collective-permute-start | bytes 1572872 | tf_op jit(solution)/shard_map/ppermute | solution.py:31
  47.8 15.1 %collective-permute-start.2 = (bf16[4,2,256,128]{3,2,1,0:T(8,128)(2,1)}, bf16[4,2,256,128]{3,2,1,0:T(8,128)(2,1)}, u32[]{:S(2)}, u32[]{:S(2)}) collective-permute-start(bf16[4,2,256,128]{3,2,1,0:T(8,128)(2,1)} %get-tuple-element.25), channel_id=1, source_target_pairs={{0,48},{16,0},{32,16},{48,32},{64,80},{80,96},{96,112},{112,64},{1... | collective-permute-start | bytes 1572872 | tf_op jit(solution)/shard_map/ppermute | solution.py:31
  65.1 3.9 %collective-permute-start.14 = (bf16[2,256,128]{2,1,0:T(8,128)(2,1)S(1)}, bf16[2,256,128]{2,1,0:T(8,128)(2,1)S(1)}, u32[]{:S(2)}, u32[]{:S(2)}) collective-permute-start(bf16[2,256,128]{2,1,0:T(8,128)(2,1)S(1)} %get-tuple-element.33), channel_id=1, source_target_pairs={{0,16},{16,32},{32,48},{48,0},{64,112},{80,64},{96,80},{112,96},{1... | collective-permute-start | bytes 393224 | tf_op jit(solution)/shard_map/ppermute | solution.py:31
  65.2 24.0 %copy-start.7 = (bf16[128,512]{1,0:T(8,128)(2,1)S(1)}, bf16[128,512]{1,0:T(8,128)(2,1)}, u32[]{:S(2)}) copy-start(bf16[128,512]{1,0:T(8,128)(2,1)} %param.8) | copy-start | bytes 393220
  65.2 5.1 %collective-permute-start.7 = (bf16[2,256,128]{2,1,0:T(8,128)(2,1)S(1)}, bf16[2,256,128]{2,1,0:T(8,128)(2,1)S(1)}, u32[]{:S(2)}, u32[]{:S(2)}) collective-permute-start(bf16[2,256,128]{2,1,0:T(8,128)(2,1)S(1)} %get-tuple-element.35), channel_id=1, source_target_pairs={{0,1},{1,2},{2,3},{3,0},{64,67},{65,64},{66,65},{67,66},{4,5},{5,6... | collective-permute-start | bytes 393224 | tf_op jit(solution)/shard_map/ppermute | solution.py:31
  67.1 12.5 %collective-permute-start.6 = (bf16[2,256,128]{2,1,0:T(8,128)(2,1)S(1)}, bf16[2,256,128]{2,1,0:T(8,128)(2,1)S(1)}, u32[]{:S(2)}, u32[]{:S(2)}) collective-permute-start(bf16[2,256,128]{2,1,0:T(8,128)(2,1)S(1)} %get-tuple-element.34), channel_id=1, source_target_pairs={{0,3},{1,0},{2,1},{3,2},{64,65},{65,66},{66,67},{67,64},{4,7},{5,4... | collective-permute-start | bytes 393224 | tf_op jit(solution)/shard_map/ppermute | solution.py:31
  67.1 5.7 %collective-permute-start.13 = (bf16[2,256,128]{2,1,0:T(8,128)(2,1)S(1)}, bf16[2,256,128]{2,1,0:T(8,128)(2,1)S(1)}, u32[]{:S(2)}, u32[]{:S(2)}) collective-permute-start(bf16[2,256,128]{2,1,0:T(8,128)(2,1)S(1)} %get-tuple-element.32), channel_id=1, source_target_pairs={{0,48},{16,0},{32,16},{48,32},{64,80},{80,96},{96,112},{112,64},{1... | collective-permute-start | bytes 393224 | tf_op jit(solution)/shard_map/ppermute | solution.py:31
  69.0 4.9 %collective-permute-start.15 = (bf16[2,256,128]{2,1,0:T(8,128)(2,1)S(1)}, bf16[2,256,128]{2,1,0:T(8,128)(2,1)S(1)}, u32[]{:S(2)}, u32[]{:S(2)}) collective-permute-start(bf16[2,256,128]{2,1,0:T(8,128)(2,1)S(1)} %fusion.11), channel_id=1, source_target_pairs={{0,16},{16,32},{32,48},{48,0},{64,112},{80,64},{96,80},{112,96},{1... | collective-permute-start | bytes 393224 | tf_op jit(solution)/shard_map/ppermute | solution.py:31
  70.4 9.2 %collective-permute-start.8 = (bf16[2,256,128]{2,1,0:T(8,128)(2,1)S(1)}, bf16[2,256,128]{2,1,0:T(8,128)(2,1)S(1)}, u32[]{:S(2)}, u32[]{:S(2)}) collective-permute-start(bf16[2,256,128]{2,1,0:T(8,128)(2,1)S(1)} %fusion.16), channel_id=1, source_target_pairs={{0,1},{1,2},{2,3},{3,0},{64,67},{65,64},{66,65},{67,66},{4,5},{5,6... | collective-permute-start | bytes 393224 | tf_op jit(solution)/shard_map/ppermute | solution.py:31
  74.1 6.9 %collective-permute-start.17 = (bf16[256,128]{1,0:T(8,128)(2,1)S(1)}, bf16[256,128]{1,0:T(8,128)(2,1)S(1)}, u32[]{:S(2)}, u32[]{:S(2)}) collective-permute-start(bf16[256,128]{1,0:T(8,128)(2,1)S(1)} %get-tuple-element.39), channel_id=1, source_target_pairs={{0,12},{4,0},{8,4},{12,8},{1,13},{5,1},{9,5},{13,9},{2,14},{6,2},{... | collective-permute-start | bytes 196616 | tf_op jit(solution)/shard_map/ppermute | solution.py:26
  79.6 4.0 %collective-permute-start.16 = (bf16[256,128]{1,0:T(8,128)(2,1)S(1)}, bf16[256,128]{1,0:T(8,128)(2,1)S(1)}, u32[]{:S(2)}, u32[]{:S(2)}) collective-permute-start(bf16[256,128]{1,0:T(8,128)(2,1)S(1)} %get-tuple-element.38), channel_id=1, source_target_pairs={{0,8},{4,12},{8,0},{12,4},{1,9},{5,13},{9,1},{13,5},{2,10},{6,14},... | collective-permute-start | bytes 196616 | tf_op jit(solution)/shard_map/ppermute | solution.py:26
  79.7 5.1 %collective-permute-start.9 = (bf16[256,128]{1,0:T(8,128)(2,1)S(1)}, bf16[256,128]{1,0:T(8,128)(2,1)S(1)}, u32[]{:S(2)}, u32[]{:S(2)}) collective-permute-start(bf16[256,128]{1,0:T(8,128)(2,1)S(1)} %fusion.23), channel_id=1, source_target_pairs={{0,4},{4,8},{8,12},{12,0},{1,5},{5,9},{9,13},{13,1},{2,6},{6,10},{... | collective-permute-start | bytes 196616 | tf_op jit(solution)/shard_map/ppermute | solution.py:26
  84.9 7.7 %collective-permute-start.18 = (bf16[2,128,128]{2,1,0:T(8,128)(2,1)S(1)}, bf16[2,128,128]{2,1,0:T(8,128)(2,1)S(1)}, u32[]{:S(2)}, u32[]{:S(2)}) collective-permute-start(bf16[2,128,128]{2,1,0:T(8,128)(2,1)S(1)} %add_convert_fusion.4), channel_id=1, source_target_pairs={{0,128},{128,0},{1,129},{129,1},{2,130},{130,2},{3,131},{131,3},{4... | collective-permute-start | bytes 196616 | tf_op jit(solution)/shard_map/ppermute | solution.py:35
  92.7 7.1 %collective-permute-start.19 = (f32[2,128,128]{2,1,0:T(8,128)S(1)}, f32[2,128,128]{2,1,0:T(8,128)S(1)}, u32[]{:S(2)}, u32[]{:S(2)}) collective-permute-start(f32[2,128,128]{2,1,0:T(8,128)S(1)} %get-tuple-element.37), channel_id=1, source_target_pairs={{0,64},{64,0},{1,65},{65,1},{2,66},{66,2},{3,67},{67,3},{4,68},{68... | collective-permute-start | bytes 393224 | tf_op jit(solution)/shard_map/ppermute | solution.py:35
where the time goes:
time: 101 us
  starting transfers between devices  34.9 us (35%)
  waiting for transfers between devices  31 us (31%)
  Pallas kernels  24.6 us (24%)
  other arithmetic  6.23 us (6%)
  local copies, waits for them, and re-layouts  2.98 us (3%)
    ppermute x12, waiting for transfers between devices, onward(): return lax.ppermute(block, ('core', axis), route)  17.5 us
    ppermute x12, starting transfers between devices, onward(): return lax.ppermute(block, ('core', axis), route)  15.1 us
    ppermute x5, starting transfers between devices, swap(): return lax.ppermute(block, axis, [(0, 1), (1, 0)])  13.7 us
    pallas_call x2, Pallas kernels, later_terms(): pl.pallas_call(functools.partial(later_kernel, distances), out_shape=[par...  13.3 us
    pallas_call x1, Pallas kernels, first_terms(): pl.pallas_call(functools.partial(first_kernel, factor), out_shape=[part,...  11.3 us
    ppermute x5, waiting for transfers between devices, swap(): return lax.ppermute(block, axis, [(0, 1), (1, 0)])  8.92 us
    ppermute x3, starting transfers between devices, shift(): lax.ppermute(block, axis, [(i, (i + step) % count) for i in range(count)])  6.02 us
    ppermute x3, waiting for transfers between devices, shift(): lax.ppermute(block, axis, [(i, (i + step) % count) for i in range(count)])  4.63 us
  transfers between devices with their start and end apart: 20, of which 13 were waited for; matrix products, arithmetic and copies ran while one was open for 4% of the time, Pallas kernels for 5%

commit v1 on v0

v1 whole, which is shorter than its diff:
```python
import functools
import math

import jax
import jax.numpy as jnp
from jax import lax
from jax.experimental import pallas as pl
from jax.experimental.pallas import tpu as pltpu
from jax.sharding import Mesh
from jax.sharding import PartitionSpec as P


BLOCK = 128
ROWS_AT_A_TIME = 64
VMEM_LIMIT = 24 * 2**20
FSDP = ("x", "zl", "y")
GROUP = ("zh", "core")

norm_epsilon = 1e-05
inner_rate = 0.5
outer_rate = 0.7
momentum_decay = 0.9


def shift(block, axis, step):
    count = lax.axis_size(axis)
    return lax.ppermute(block, axis, [(i, (i + step) % count) for i in range(count)])


def onward(block, axis, step):
    route = [(i, (i + step) % 4) for i in range(4)] + [(4 + i, 4 + (i - step) % 4) for i in range(4)]
    return lax.ppermute(block, ("core", axis), route)


def swap(block, axis):
    return lax.ppermute(block, axis, [(0, 1), (1, 0)])


def wide(array):
    return array.astype(jnp.float32)


def narrow(array):
    return array.astype(jnp.bfloat16)


class Tiles:
    def __init__(self, place, distances):
        self.x, self.zl, self.y, self.core = (place[i] for i in range(4))
        self.distances = distances
        self.count = 4 * len(distances)

    def parts(self, turn):
        return turn // 4, (turn // 2) % 2, turn % 2

    def column(self, turn, block):
        at, colour, low = self.parts(turn)
        distance = self.distances[0] + 2 * at
        along = jnp.where(colour == 0, self.x, self.y)
        along = lax.rem(along + 4 + jnp.where(self.core == 0, distance, -distance), 4)
        line = lax.rem(self.zl + 2 * colour + low, 4)
        x, y = jnp.where(colour == 0, along, block), jnp.where(colour == 0, block, along)
        return pl.multiple_of(((x * 4 + line) * 4 + y) * BLOCK, BLOCK)

    def second(self, colour, block):
        across = jnp.where(colour == 0, self.y, self.x)
        return lax.rem(jnp.where(self.core == 0, block - across, across - block) + 4, 4)

    def products(self, tokens, grads, gain, send, own):
        def body(turn, carry):
            at, colour, low = self.parts(turn)
            columns = [pl.ds(self.column(turn, k), BLOCK) for k in range(4)]
            tile = jnp.concatenate([tokens[:, c] for c in columns], axis=1)
            full = jnp.dot(grads[...], tile, preferred_element_type=jnp.float32)
            rows = full.shape[0] // 2
            for k in range(4):
                block = (full[:, k * BLOCK : (k + 1) * BLOCK] * gain[:, columns[k]]).astype(jnp.bfloat16)
                there = self.second(colour, k)
                send[len(self.distances) - 1 - at, colour, lax.rem(4 - there, 4), low] = block[:rows]
                own[at, colour, there, low] = block[rows:]
            return carry

        lax.fori_loop(0, self.count, body, 0)


def first_kernel(factor, place, tokens, keys, gain, send, own, grads, scaled):
    count, width = tokens.shape

    def squares(i, carry):
        rows = pl.ds(pl.multiple_of(i * ROWS_AT_A_TIME, ROWS_AT_A_TIME), ROWS_AT_A_TIME)

        def add(j, total):
            for k in range(8):
                part = tokens[rows, pl.ds(pl.multiple_of((j * 8 + k) * BLOCK, BLOCK), BLOCK)].astype(jnp.float32)
                total = total + part * part
            return total

        total = jnp.zeros((ROWS_AT_A_TIME, BLOCK), jnp.float32)
        total = lax.fori_loop(0, width // (8 * BLOCK), add, total)
        meansq = jnp.sum(total, axis=1, keepdims=True) / width
        scale = lax.rsqrt(meansq + norm_epsilon) * factor
        scaled[rows] = keys[rows].astype(jnp.float32) * scale
        return carry

    lax.fori_loop(0, count // ROWS_AT_A_TIME, squares, 0)

    core = place[3]
    for group in range(4):
        mine = jnp.where(core == group % 2, 2, 0)
        at = pl.ds(pl.multiple_of((mine + group // 2) * BLOCK, BLOCK), BLOCK)
        for t in range(count // BLOCK):
            square = scaled[t * BLOCK : (t + 1) * BLOCK, group * BLOCK : (group + 1) * BLOCK]
            grads[at, t * BLOCK : (t + 1) * BLOCK] = square.T.astype(jnp.bfloat16)

    Tiles(place, (2,)).products(tokens, grads, gain, send, own)


def later_kernel(distances, place, tokens, grads, gain, send, own):
    Tiles(place, distances).products(tokens, grads, gain, send, own)


def terms(kernel, distances, outs, scratch, place, tokens, grads, gain):
    count = tokens.shape[0]
    cols = 4 * BLOCK
    part = jax.ShapeDtypeStruct((len(distances), 2, 4, 2, cols // 2, BLOCK), jnp.bfloat16)
    in_vmem = pl.BlockSpec(memory_space=pltpu.VMEM)
    in_smem = pl.BlockSpec(memory_space=pltpu.SMEM)
    outs = [part, part] + outs
    flops = 2 * len(distances) * 16 * BLOCK * count * cols
    return pl.pallas_call(
        kernel,
        out_shape=outs,
        in_specs=[in_smem, in_vmem, in_vmem, in_vmem],
        out_specs=[in_vmem] * len(outs),
        scratch_shapes=scratch,
        cost_estimate=pl.CostEstimate(flops=flops, bytes_accessed=2**20, transcendentals=0),
        compiler_params=pltpu.CompilerParams(vmem_limit_bytes=VMEM_LIMIT),
    )(place, tokens, grads, gain)


def first_terms(place, tokens, keys, gain, factor):
    count, cols = keys.shape
    grads = jax.ShapeDtypeStruct((cols, count), jnp.bfloat16)
    scratch = [pltpu.VMEM((count, cols), jnp.float32)]
    return terms(functools.partial(first_kernel, factor), (2,), [grads], scratch, place, tokens, keys, gain)


def later_terms(distances, place, tokens, grads, gain):
    return terms(functools.partial(later_kernel, distances), distances, [], [], place, tokens, grads, gain)


def ring_sum(terms, axis):
    far = onward(narrow(terms[2]), axis, 1)
    back = onward(narrow(terms[3]), axis, -1)
    front = onward(narrow(terms[1] + wide(far)), axis, 1)
    return terms[0] + wide(back) + wide(front)


def per_device(tokens, keys_grad, norm_gain, weight, momentum):
    x, zl, y, zh, core = (lax.axis_index(a) for a in FSDP + GROUP)
    rows, cols = momentum.shape
    groups = lax.axis_size(GROUP)
    factor = inner_rate / math.sqrt(lax.axis_size(FSDP) * tokens.shape[1]) / groups
    place = jnp.stack([x, zl, y, core]).astype(jnp.int32)
    gain = norm_gain[None, :]
    axes = ("x", "y")

    send, own, grads = first_terms(place, tokens[0], keys_grad[0], gain, factor)
    received = swap(send, "core")
    far = [None, None]
    for c in (0, 1):
        far[c] = onward(narrow(wide(own[0, c]) + wide(received[0, c])), axes[c], 1)

    send, own = later_terms((1, 3), place, tokens[0], grads, gain)
    received = swap(send, "core")
    sides = [[wide(own[i, c]) + wide(received[i, c]) for i in (0, 1)] for c in (0, 1)]
    back = [None, None]
    for c in (0, 1):
        back[c] = onward(narrow(sides[c][1]), axes[c], -1)

    front = [None, None]
    for c in (0, 1):
        front[c] = onward(narrow(sides[c][0] + wide(far[c])), axes[c], 1)

    send, own = later_terms((0,), place, tokens[0], grads, gain)
    received = swap(send, "core")
    sums = [wide(own[0, c]) + wide(received[0, c]) + wide(back[c]) + wide(front[c]) for c in (0, 1)]

    sums = [ring_sum(sums[0], "y"), ring_sum(sums[1], "x")]
    lines = [sums[0][0], sums[0][1], sums[1][0], sums[1][1]]
    partial = lines[0]
    for step in (1, 2, 3):
        partial += wide(shift(narrow(lines[step]), "zl", step))

    partial = partial.reshape(2, cols, rows)
    both_rate = 1 + momentum_decay
    mine = (jnp.arange(2) == zh)[:, None, None]
    joined = narrow(partial + jnp.where(mine, momentum.T * (momentum_decay**2 / both_rate), 0.0))
    received = swap(joined, "zh")
    update = wide(joined) + wide(received)
    updates = jnp.stack([update, swap(update, "core")])
    updates = jnp.where(core == 0, updates, updates[::-1])
    average = jnp.where(zh == 0, partial[0] + wide(received[0]), partial[1] + wide(received[1]))

    new_momentum = momentum_decay * momentum + average.T
    updates = updates.transpose(3, 1, 0, 2).reshape(rows, 4 * cols)
    new_weight = narrow(wide(weight) - outer_rate * both_rate * updates)
    return (new_weight, new_momentum)


def solution(mesh):
    finer = Mesh(mesh.devices.reshape(2, 2, 4, 4, 4), GROUP + FSDP)
    in_specs = (
        P(GROUP, FSDP, None),
        P(GROUP, FSDP, None),
        P(),
        P(FSDP, None),
        P(FSDP, GROUP),
    )
    out_specs = (P(FSDP, None), P(FSDP, GROUP))
    return jax.shard_map(per_device, mesh=finer, in_specs=in_specs, out_specs=out_specs, check_vma=False)
```

time: 101 us -> 99.1 us (0.981)
  Pallas kernels: 24.6 us -> 16.8 us
  local copies, waits for them, and re-layouts: 2.98 us -> 7.71 us
    pallas_call x3, Pallas kernels: 24.6 us -> 16.8 us  [terms(): pl.pallas_call(kernel, out_shape=outs, in_specs=[in_smem, in_vmem, in_vme...]
    unnamed x22 -> x14, local copies, waits for them, and re-layouts: 2.82 us -> 7.54 us
    ppermute x12, waiting for transfers between devices: 17.5 us -> 19.7 us  [onward(): return lax.ppermute(block, ('core', axis), route)]
    ppermute x5, starting transfers between devices: 13.7 us -> 15.2 us  [swap(): return lax.ppermute(block, axis, [(0, 1), (1, 0)])]
  transfers between devices with their start and end apart: 20 -> 20, of which waited for: 13 -> 14; matrix products, arithmetic and copies ran while one was open for 4% -> 4% of each run, Pallas kernels for 5% -> 3%
where the time goes in v1:
time: 99.1 us; the launch traced here: 98.9 us
  starting transfers between devices  35.9 us (36%)
  waiting for transfers between devices  31.8 us (32%)
  Pallas kernels  16.8 us (17%)
  local copies, waits for them, and re-layouts  7.71 us (8%)
  other arithmetic  5.72 us (6%)
    ppermute x12, waiting for transfers between devices, onward(): return lax.ppermute(block, ('core', axis), route)  19.7 us
    pallas_call x3, Pallas kernels, terms(): pl.pallas_call(kernel, out_shape=outs, in_specs=[in_smem, in_vmem, in_vme...  16.8 us
    ppermute x5, starting transfers between devices, swap(): return lax.ppermute(block, axis, [(0, 1), (1, 0)])  15.2 us
    ppermute x12, starting transfers between devices, onward(): return lax.ppermute(block, ('core', axis), route)  15 us
    ppermute x5, waiting for transfers between devices, swap(): return lax.ppermute(block, axis, [(0, 1), (1, 0)])  7.98 us
    unnamed x14, local copies, waits for them, and re-layouts  7.54 us
    ppermute x3, starting transfers between devices, shift(): lax.ppermute(block, axis, [(i, (i + step) % count) for i in range(count)])  5.67 us
    ppermute x3, waiting for transfers between devices, shift(): lax.ppermute(block, axis, [(i, (i + step) % count) for i in range(count)])  4.18 us
  transfers between devices with their start and end apart: 20, of which 14 were waited for; matrix products, arithmetic and copies ran while one was open for 4% of the time, Pallas kernels for 3%

profile of v1, /device:TPU:1, one launch (start us, length us, event | category | flops | bytes accessed | tf_op | source)
XLA Modules:
  0.0 98.9 jit_solution(10832301508956688724)
XLA Ops:
  0.7 4.0 %copy-done = bf16[1,640,8192]{2,1,0:T(8,128)(2,1)S(1)} copy-done((bf16[1,640,8192]{2,1,0:T(8,128)(2,1)S(1)}, bf16[1,640,8192]{2,1,0:T(8,128)(2,1)}, u32[]{:S(2)}) %copy-start) | copy-done | bytes 10485784
  4.7 1.1 %copy-done.1 = bf16[1,640,512]{2,1,0:T(8,128)(2,1)S(1)} copy-done((bf16[1,640,512]{2,1,0:T(8,128)(2,1)S(1)}, bf16[1,640,512]{2,1,0:T(8,128)(2,1)}, u32[]{:S(2)}) %copy-start.1) | copy-done | bytes 655384
  6.5 7.6 %shard_map.68 = (bf16[1,2,4,2,256,128]{5,4,3,2,1,0:T(8,128)(2,1)S(1)}, bf16[1,2,4,2,256,128]{5,4,3,2,1,0:T(8,128)(2,1)S(1)}, bf16[512,640]{1,0:T(8,128)(2,1)S(1)}) custom-call(s32[4]{0:T(128)S(1)} %pad_add_fusion.place, bf16[640,8192]{1,0:T(8,128)(2,1)S(1)} %bitcast.107, bf16[640,512]{1,0:T(8,128)(2,1)S(1)} %bitcast.110, f32[1,8192]{1,0:T(1,128)S(1)} %bitcast.111), custom_call_target="tpu_custom_call" | custom-call | flops 1342177280 | bytes 1048576 | tf_op jit(solution)/shard_map/pallas_call | solution.py:130
  14.2 6.0 %shard_map.70 = (bf16[2,2,4,2,256,128]{5,4,3,2,1,0:T(8,128)(2,1)S(1)}, bf16[2,2,4,2,256,128]{5,4,3,2,1,0:T(8,128)(2,1)S(1)}) custom-call(s32[4]{0:T(128)S(1)} %pad_add_fusion.place, bf16[640,8192]{1,0:T(8,128)(2,1)S(1)} %bitcast.108, bf16[512,640]{1,0:T(8,128)(2,1)S(1)} %get-tuple-element.9.grads, f32[1,8192]{1,0:T(1,128)S(1)} %bitcast.112), custom_call_target="tpu_custom_call" | custom-call | flops 2684354560 | bytes 1048576 | tf_op jit(solution)/shard_map/pallas_call | solution.py:130
  20.1 3.3 %collective-permute-start.1 = (bf16[2,2,4,2,256,128]{5,4,3,2,1,0:T(8,128)(2,1)S(1)}, bf16[2,2,4,2,256,128]{5,4,3,2,1,0:T(8,128)(2,1)S(1)}, u32[]{:S(2)}, u32[]{:S(2)}) collective-permute-start(bf16[2,2,4,2,256,128]{5,4,3,2,1,0:T(8,128)(2,1)S(1)} %get-tuple-element.13), channel_id=1, source_target_pairs={{0,64},{64,0},{1,65},{65,1},{2,66},{66,2},{3,67},{67,3},{4,68},{68... | collective-permute-start | bytes 6291464 | tf_op jit(solution)/shard_map/ppermute | solution.py:36
  23.5 5.2 %collective-permute-done.3 = bf16[1,2,4,2,256,128]{5,4,3,2,1,0:T(8,128)(2,1)S(1)} collective-permute-done((bf16[1,2,4,2,256,128]{5,4,3,2,1,0:T(8,128)(2,1)S(1)}, bf16[1,2,4,2,256,128]{5,4,3,2,1,0:T(8,128)(2,1)S(1)}, u32[]{:S(2)}, u32[]{:S(2)}) %collective-permute-start.3) | collective-permute-done | bytes 1048608 | tf_op jit(solution)/shard_map/ppermute | solution.py:36
  29.0 1.1 %collective-permute-start.11 = (bf16[4,2,256,128]{3,2,1,0:T(8,128)(2,1)S(1)}, bf16[4,2,256,128]{3,2,1,0:T(8,128)(2,1)S(1)}, u32[]{:S(2)}, u32[]{:S(2)}) collective-permute-start(bf16[4,2,256,128]{3,2,1,0:T(8,128)(2,1)S(1)} %get-tuple-element.30), channel_id=1, source_target_pairs={{0,1},{1,2},{2,3},{3,0},{64,67},{65,64},{66,65},{67,66},{4,5},{5,6... | collective-permute-start | bytes 1572872 | tf_op jit(solution)/shard_map/ppermute | solution.py:32
  30.1 2.5 %collective-permute-start.4 = (bf16[4,2,256,128]{3,2,1,0:T(8,128)(2,1)S(1)}, bf16[4,2,256,128]{3,2,1,0:T(8,128)(2,1)S(1)}, u32[]{:S(2)}, u32[]{:S(2)}) collective-permute-start(bf16[4,2,256,128]{3,2,1,0:T(8,128)(2,1)S(1)} %get-tuple-element.31), channel_id=1, source_target_pairs={{0,16},{16,32},{32,48},{48,0},{64,112},{80,64},{96,80},{112,96},{1... | collective-permute-start | bytes 1572872 | tf_op jit(solution)/shard_map/ppermute | solution.py:32
  32.6 3.3 %shard_map.69 = (bf16[1,2,4,2,256,128]{5,4,3,2,1,0:T(8,128)(2,1)S(1)}, bf16[1,2,4,2,256,128]{5,4,3,2,1,0:T(8,128)(2,1)S(1)}) custom-call(s32[4]{0:T(128)S(1)} %pad_add_fusion.place, bf16[640,8192]{1,0:T(8,128)(2,1)S(1)} %bitcast.109, bf16[512,640]{1,0:T(8,128)(2,1)S(1)} %get-tuple-element.9.grads, f32[1,8192]{1,0:T(1,128)S(1)} %bitcast.113), custom_call_target="tpu_custom_call" | custom-call | flops 1342177280 | bytes 1048576 | tf_op jit(solution)/shard_map/pallas_call | solution.py:130
  35.9 1.5 %collective-permute-done.11 = bf16[4,2,256,128]{3,2,1,0:T(8,128)(2,1)S(1)} collective-permute-done((bf16[4,2,256,128]{3,2,1,0:T(8,128)(2,1)S(1)}, bf16[4,2,256,128]{3,2,1,0:T(8,128)(2,1)S(1)}, u32[]{:S(2)}, u32[]{:S(2)}) %collective-permute-start.11) | collective-permute-done | bytes 524320 | tf_op jit(solution)/shard_map/ppermute | solution.py:32
  37.4 1.3 %collective-permute-done.4 = bf16[4,2,256,128]{3,2,1,0:T(8,128)(2,1)S(1)} collective-permute-done((bf16[4,2,256,128]{3,2,1,0:T(8,128)(2,1)S(1)}, bf16[4,2,256,128]{3,2,1,0:T(8,128)(2,1)S(1)}, u32[]{:S(2)}, u32[]{:S(2)}) %collective-permute-start.4) | collective-permute-done | bytes 524320 | tf_op jit(solution)/shard_map/ppermute | solution.py:32
  38.7 1.4 %fusion = (bf16[4,2,256,128]{3,2,1,0:T(8,128)(2,1)}, bf16[4,2,256,128]{3,2,1,0:T(8,128)(2,1)}) fusion(bf16[4,2,256,128]{3,2,1,0:T(8,128)(2,1)S(1)} %collective-permute-done.11, bf16[2,2,4,2,256,128]{5,4,3,2,1,0:T(8,128)(2,1)S(1)} %collective-permute-done.1, bf16[2,2,4,2,256,128]{5,4,3,2,1,0:T(8,128)(2,1)S(1)} %get-tuple-element.12, ...), kind=kLoop, calls=%fused_computation.1 | loop fusion | flops 3145728 | bytes 4194304 | tf_op jit(solution)/shard_map/convert_element_type | solution.py:44
  40.1 0.9 collective-permute-start.12
  41.1 1.3 %fusion.6 = (bf16[4,2,256,128]{3,2,1,0:T(8,128)(2,1)}, bf16[4,2,256,128]{3,2,1,0:T(8,128)(2,1)}) fusion(bf16[2,2,4,2,256,128]{5,4,3,2,1,0:T(8,128)(2,1)S(1)} %collective-permute-done.1, bf16[2,2,4,2,256,128]{5,4,3,2,1,0:T(8,128)(2,1)S(1)} %get-tuple-element.12), kind=kLoop, calls=%fused_computation.14 | loop fusion | flops 2097152 | bytes 3145728 | tf_op jit(solution)/shard_map/convert_element_type | solution.py:44
  42.9 3.1 %collective-permute-start.5 = (bf16[4,2,256,128]{3,2,1,0:T(8,128)(2,1)}, bf16[4,2,256,128]{3,2,1,0:T(8,128)(2,1)}, u32[]{:S(2)}, u32[]{:S(2)}) collective-permute-start(bf16[4,2,256,128]{3,2,1,0:T(8,128)(2,1)} %get-tuple-element.27), channel_id=1, source_target_pairs={{0,16},{16,32},{32,48},{48,0},{64,112},{80,64},{96,80},{112,96},{1... | collective-permute-start | bytes 1572872 | tf_op jit(solution)/shard_map/ppermute | solution.py:32
  46.1 4.0 %collective-permute-done.12 = bf16[4,2,256,128]{3,2,1,0:T(8,128)(2,1)} collective-permute-done((bf16[4,2,256,128]{3,2,1,0:T(8,128)(2,1)}, bf16[4,2,256,128]{3,2,1,0:T(8,128)(2,1)}, u32[]{:S(2)}, u32[]{:S(2)}) %collective-permute-start.12) | collective-permute-done | bytes 524320 | tf_op jit(solution)/shard_map/ppermute | solution.py:32
  50.1 7.2 %collective-permute-done.10 = bf16[4,2,256,128]{3,2,1,0:T(8,128)(2,1)} collective-permute-done((bf16[4,2,256,128]{3,2,1,0:T(8,128)(2,1)}, bf16[4,2,256,128]{3,2,1,0:T(8,128)(2,1)}, u32[]{:S(2)}, u32[]{:S(2)}) %collective-permute-start.10) | collective-permute-done | bytes 524320 | tf_op jit(solution)/shard_map/ppermute | solution.py:32
  57.3 3.8 %collective-permute-done.2 = bf16[4,2,256,128]{3,2,1,0:T(8,128)(2,1)} collective-permute-done((bf16[4,2,256,128]{3,2,1,0:T(8,128)(2,1)}, bf16[4,2,256,128]{3,2,1,0:T(8,128)(2,1)}, u32[]{:S(2)}, u32[]{:S(2)}) %collective-permute-start.2) | collective-permute-done | bytes 524320 | tf_op jit(solution)/shard_map/ppermute | solution.py:32
  61.1 2.2 %fusion.28 = (bf16[4,2,256,128]{3,2,1,0:T(8,128)(2,1)S(1)}, f32[4,2,256,128]{3,2,1,0:T(8,128)S(1)}, bf16[4,2,256,128]{3,2,1,0:T(8,128)(2,1)S(1)}, f32[4,2,256,128]{3,2,1,0:T(8,128)S(1)}) fusion(bf16[4,2,256,128]{3,2,1,0:T(8,128)(2,1)} %collective-permute-done.12, bf16[4,2,256,128]{3,2,1,0:T(8,128)(2,1)} %collective-permute-done.10, ...), kind=kLoop, calls=%fused_computation.60 | loop fusion | flops 4194304 | bytes 7340032 | tf_op jit(solution)/shard_map/convert.5
  63.4 1.8 %collective-permute-start.7 = (bf16[2,256,128]{2,1,0:T(8,128)(2,1)S(1)}, bf16[2,256,128]{2,1,0:T(8,128)(2,1)S(1)}, u32[]{:S(2)}, u32[]{:S(2)}) collective-permute-start(bf16[2,256,128]{2,1,0:T(8,128)(2,1)S(1)} %get-tuple-element.35), channel_id=1, source_target_pairs={{0,1},{1,2},{2,3},{3,0},{64,67},{65,64},{66,65},{67,66},{4,5},{5,6... | collective-permute-start | bytes 393224 | tf_op jit(solution)/shard_map/ppermute | solution.py:32
  65.2 1.4 %collective-permute-start.13 = (bf16[2,256,128]{2,1,0:T(8,128)(2,1)S(1)}, bf16[2,256,128]{2,1,0:T(8,128)(2,1)S(1)}, u32[]{:S(2)}, u32[]{:S(2)}) collective-permute-start(bf16[2,256,128]{2,1,0:T(8,128)(2,1)S(1)} %get-tuple-element.32), channel_id=1, source_target_pairs={{0,48},{16,0},{32,16},{48,32},{64,80},{80,96},{96,112},{112,64},{1... | collective-permute-start | bytes 393224 | tf_op jit(solution)/shard_map/ppermute | solution.py:32
  67.2 1.3 %collective-permute-start.15 = (bf16[2,256,128]{2,1,0:T(8,128)(2,1)S(1)}, bf16[2,256,128]{2,1,0:T(8,128)(2,1)S(1)}, u32[]{:S(2)}, u32[]{:S(2)}) collective-permute-start(bf16[2,256,128]{2,1,0:T(8,128)(2,1)S(1)} %fusion.11), channel_id=1, source_target_pairs={{0,16},{16,32},{32,48},{48,0},{64,112},{80,64},{96,80},{112,96},{1... | collective-permute-start | bytes 393224 | tf_op jit(solution)/shard_map/ppermute | solution.py:32
  68.6 2.2 %collective-permute-start.8 = (bf16[2,256,128]{2,1,0:T(8,128)(2,1)S(1)}, bf16[2,256,128]{2,1,0:T(8,128)(2,1)S(1)}, u32[]{:S(2)}, u32[]{:S(2)}) collective-permute-start(bf16[2,256,128]{2,1,0:T(8,128)(2,1)S(1)} %fusion.16), channel_id=1, source_target_pairs={{0,1},{1,2},{2,3},{3,0},{64,67},{65,64},{66,65},{67,66},{4,5},{5,6... | collective-permute-start | bytes 393224 | tf_op jit(solution)/shard_map/ppermute | solution.py:32
  71.0 1.2 %collective-permute-done.15 = bf16[2,256,128]{2,1,0:T(8,128)(2,1)S(1)} collective-permute-done((bf16[2,256,128]{2,1,0:T(8,128)(2,1)S(1)}, bf16[2,256,128]{2,1,0:T(8,128)(2,1)S(1)}, u32[]{:S(2)}, u32[]{:S(2)}) %collective-permute-start.15) | collective-permute-done | bytes 131104 | tf_op jit(solution)/shard_map/ppermute | solution.py:32
  72.3 4.8 %collective-permute-start.17 = (bf16[256,128]{1,0:T(8,128)(2,1)S(1)}, bf16[256,128]{1,0:T(8,128)(2,1)S(1)}, u32[]{:S(2)}, u32[]{:S(2)}) collective-permute-start(bf16[256,128]{1,0:T(8,128)(2,1)S(1)} %get-tuple-element.39), channel_id=1, source_target_pairs={{0,12},{4,0},{8,4},{12,8},{1,13},{5,1},{9,5},{13,9},{2,14},{6,2},{... | collective-permute-start | bytes 196616 | tf_op jit(solution)/shard_map/ppermute | solution.py:27
  77.2 0.9 collective-permute-start.9
  78.4 2.8 %collective-permute-done.16 = bf16[256,128]{1,0:T(8,128)(2,1)S(1)} collective-permute-done((bf16[256,128]{1,0:T(8,128)(2,1)S(1)}, bf16[256,128]{1,0:T(8,128)(2,1)S(1)}, u32[]{:S(2)}, u32[]{:S(2)}) %collective-permute-start.16) | collective-permute-done | bytes 65568 | tf_op jit(solution)/shard_map/ppermute | solution.py:27
  81.2 1.0 %collective-permute-done.9 = bf16[256,128]{1,0:T(8,128)(2,1)S(1)} collective-permute-done((bf16[256,128]{1,0:T(8,128)(2,1)S(1)}, bf16[256,128]{1,0:T(8,128)(2,1)S(1)}, u32[]{:S(2)}, u32[]{:S(2)}) %collective-permute-start.9) | collective-permute-done | bytes 65568 | tf_op jit(solution)/shard_map/ppermute | solution.py:27
  82.3 4.9 %collective-permute-start.18 = (bf16[2,128,128]{2,1,0:T(8,128)(2,1)S(1)}, bf16[2,128,128]{2,1,0:T(8,128)(2,1)S(1)}, u32[]{:S(2)}, u32[]{:S(2)}) collective-permute-start(bf16[2,128,128]{2,1,0:T(8,128)(2,1)S(1)} %add_convert_fusion.4), channel_id=1, source_target_pairs={{0,128},{128,0},{1,129},{129,1},{2,130},{130,2},{3,131},{131,3},{4... | collective-permute-start | bytes 196616 | tf_op jit(solution)/shard_map/ppermute | solution.py:36
  87.5 2.6 %collective-permute-done.18 = bf16[2,128,128]{2,1,0:T(8,128)(2,1)S(1)} collective-permute-done((bf16[2,128,128]{2,1,0:T(8,128)(2,1)S(1)}, bf16[2,128,128]{2,1,0:T(8,128)(2,1)S(1)}, u32[]{:S(2)}, u32[]{:S(2)}) %collective-permute-start.18) | collective-permute-done | bytes 65568 | tf_op jit(solution)/shard_map/ppermute | solution.py:36
  90.2 6.8 %collective-permute-start.19 = (f32[2,128,128]{2,1,0:T(8,128)S(1)}, f32[2,128,128]{2,1,0:T(8,128)S(1)}, u32[]{:S(2)}, u32[]{:S(2)}) collective-permute-start(f32[2,128,128]{2,1,0:T(8,128)S(1)} %get-tuple-element.37), channel_id=1, source_target_pairs={{0,64},{64,0},{1,65},{65,1},{2,66},{66,2},{3,67},{67,3},{4,68},{68... | collective-permute-start | bytes 393224 | tf_op jit(solution)/shard_map/ppermute | solution.py:36
  98.1 0.8 copy.14
  (49 shorter events, 4.9 us)
Async XLA Ops:
  0.7 4.0 %copy-start = (bf16[1,640,8192]{2,1,0:T(8,128)(2,1)S(1)}, bf16[1,640,8192]{2,1,0:T(8,128)(2,1)}, u32[]{:S(2)}) copy-start(bf16[1,640,8192]{2,1,0:T(8,128)(2,1)} %param.5) | copy-start | bytes 31457284
  4.7 1.1 %copy-start.1 = (bf16[1,640,512]{2,1,0:T(8,128)(2,1)S(1)}, bf16[1,640,512]{2,1,0:T(8,128)(2,1)}, u32[]{:S(2)}) copy-start(bf16[1,640,512]{2,1,0:T(8,128)(2,1)} %param.6) | copy-start | bytes 1966084
  5.8 0.8 copy-start.2
  20.1 18.6 %collective-permute-start.1 = (bf16[2,2,4,2,256,128]{5,4,3,2,1,0:T(8,128)(2,1)S(1)}, bf16[2,2,4,2,256,128]{5,4,3,2,1,0:T(8,128)(2,1)S(1)}, u32[]{:S(2)}, u32[]{:S(2)}) collective-permute-start(bf16[2,2,4,2,256,128]{5,4,3,2,1,0:T(8,128)(2,1)S(1)} %get-tuple-element.13), channel_id=1, source_target_pairs={{0,64},{64,0},{1,65},{65,1},{2,66},{66,2},{3,67},{67,3},{4,68},{68... | collective-permute-start | bytes 6291464 | tf_op jit(solution)/shard_map/ppermute | solution.py:36
  23.4 5.3 %collective-permute-start.3 = (bf16[1,2,4,2,256,128]{5,4,3,2,1,0:T(8,128)(2,1)S(1)}, bf16[1,2,4,2,256,128]{5,4,3,2,1,0:T(8,128)(2,1)S(1)}, u32[]{:S(2)}, u32[]{:S(2)}) collective-permute-start(bf16[1,2,4,2,256,128]{5,4,3,2,1,0:T(8,128)(2,1)S(1)} %get-tuple-element.15), channel_id=1, source_target_pairs={{0,64},{64,0},{1,65},{65,1},{2,66},{66,2},{3,67},{67,3},{4,68},{68... | collective-permute-start | bytes 3145736 | tf_op jit(solution)/shard_map/ppermute | solution.py:36
  29.0 8.4 %collective-permute-start.11 = (bf16[4,2,256,128]{3,2,1,0:T(8,128)(2,1)S(1)}, bf16[4,2,256,128]{3,2,1,0:T(8,128)(2,1)S(1)}, u32[]{:S(2)}, u32[]{:S(2)}) collective-permute-start(bf16[4,2,256,128]{3,2,1,0:T(8,128)(2,1)S(1)} %get-tuple-element.30), channel_id=1, source_target_pairs={{0,1},{1,2},{2,3},{3,0},{64,67},{65,64},{66,65},{67,66},{4,5},{5,6... | collective-permute-start | bytes 1572872 | tf_op jit(solution)/shard_map/ppermute | solution.py:32
  30.1 8.6 %collective-permute-start.4 = (bf16[4,2,256,128]{3,2,1,0:T(8,128)(2,1)S(1)}, bf16[4,2,256,128]{3,2,1,0:T(8,128)(2,1)S(1)}, u32[]{:S(2)}, u32[]{:S(2)}) collective-permute-start(bf16[4,2,256,128]{3,2,1,0:T(8,128)(2,1)S(1)} %get-tuple-element.31), channel_id=1, source_target_pairs={{0,16},{16,32},{32,48},{48,0},{64,112},{80,64},{96,80},{112,96},{1... | collective-permute-start | bytes 1572872 | tf_op jit(solution)/shard_map/ppermute | solution.py:32
  35.8 10.3 %collective-permute-start = (bf16[1,2,4,2,256,128]{5,4,3,2,1,0:T(8,128)(2,1)S(1)}, bf16[1,2,4,2,256,128]{5,4,3,2,1,0:T(8,128)(2,1)S(1)}, u32[]{:S(2)}, u32[]{:S(2)}) collective-permute-start(bf16[1,2,4,2,256,128]{5,4,3,2,1,0:T(8,128)(2,1)S(1)} %get-tuple-element.11), channel_id=1, source_target_pairs={{0,64},{64,0},{1,65},{65,1},{2,66},{66,2},{3,67},{67,3},{4,68},{68... | collective-permute-start | bytes 3145736 | tf_op jit(solution)/shard_map/ppermute | solution.py:36
  40.1 5.8 %copy-start.3 = (f32[128,128]{1,0:T(8,128)S(1)}, f32[128,128]{1,0:T(8,128)}, u32[]{:S(2)}) copy-start(f32[128,128]{1,0:T(8,128)} %param.9) | copy-start | bytes 196612
  40.1 10.0 %collective-permute-start.12 = (bf16[4,2,256,128]{3,2,1,0:T(8,128)(2,1)}, bf16[4,2,256,128]{3,2,1,0:T(8,128)(2,1)}, u32[]{:S(2)}, u32[]{:S(2)}) collective-permute-start(bf16[4,2,256,128]{3,2,1,0:T(8,128)(2,1)} %get-tuple-element.26), channel_id=1, source_target_pairs={{0,1},{1,2},{2,3},{3,0},{64,67},{65,64},{66,65},{67,66},{4,5},{5,6... | collective-permute-start | bytes 1572872 | tf_op jit(solution)/shard_map/ppermute | solution.py:32
  42.3 15.0 %collective-permute-start.10 = (bf16[4,2,256,128]{3,2,1,0:T(8,128)(2,1)}, bf16[4,2,256,128]{3,2,1,0:T(8,128)(2,1)}, u32[]{:S(2)}, u32[]{:S(2)}) collective-permute-start(bf16[4,2,256,128]{3,2,1,0:T(8,128)(2,1)} %get-tuple-element.24), channel_id=1, source_target_pairs={{0,3},{1,0},{2,1},{3,2},{64,65},{65,66},{66,67},{67,64},{4,7},{5,4... | collective-permute-start | bytes 1572872 | tf_op jit(solution)/shard_map/ppermute | solution.py:32
  42.9 14.4 %collective-permute-start.5 = (bf16[4,2,256,128]{3,2,1,0:T(8,128)(2,1)}, bf16[4,2,256,128]{3,2,1,0:T(8,128)(2,1)}, u32[]{:S(2)}, u32[]{:S(2)}) collective-permute-start(bf16[4,2,256,128]{3,2,1,0:T(8,128)(2,1)} %get-tuple-element.27), channel_id=1, source_target_pairs={{0,16},{16,32},{32,48},{48,0},{64,112},{80,64},{96,80},{112,96},{1... | collective-permute-start | bytes 1572872 | tf_op jit(solution)/shard_map/ppermute | solution.py:32
  46.0 15.1 %collective-permute-start.2 = (bf16[4,2,256,128]{3,2,1,0:T(8,128)(2,1)}, bf16[4,2,256,128]{3,2,1,0:T(8,128)(2,1)}, u32[]{:S(2)}, u32[]{:S(2)}) collective-permute-start(bf16[4,2,256,128]{3,2,1,0:T(8,128)(2,1)} %get-tuple-element.25), channel_id=1, source_target_pairs={{0,48},{16,0},{32,16},{48,32},{64,80},{80,96},{96,112},{112,64},{1... | collective-permute-start | bytes 1572872 | tf_op jit(solution)/shard_map/ppermute | solution.py:32
  63.3 3.9 %collective-permute-start.14 = (bf16[2,256,128]{2,1,0:T(8,128)(2,1)S(1)}, bf16[2,256,128]{2,1,0:T(8,128)(2,1)S(1)}, u32[]{:S(2)}, u32[]{:S(2)}) collective-permute-start(bf16[2,256,128]{2,1,0:T(8,128)(2,1)S(1)} %get-tuple-element.33), channel_id=1, source_target_pairs={{0,16},{16,32},{32,48},{48,0},{64,112},{80,64},{96,80},{112,96},{1... | collective-permute-start | bytes 393224 | tf_op jit(solution)/shard_map/ppermute | solution.py:32
  63.4 24.0 %copy-start.4 = (bf16[128,512]{1,0:T(8,128)(2,1)S(1)}, bf16[128,512]{1,0:T(8,128)(2,1)}, u32[]{:S(2)}) copy-start(bf16[128,512]{1,0:T(8,128)(2,1)} %param.8) | copy-start | bytes 393220
  63.4 5.1 %collective-permute-start.7 = (bf16[2,256,128]{2,1,0:T(8,128)(2,1)S(1)}, bf16[2,256,128]{2,1,0:T(8,128)(2,1)S(1)}, u32[]{:S(2)}, u32[]{:S(2)}) collective-permute-start(bf16[2,256,128]{2,1,0:T(8,128)(2,1)S(1)} %get-tuple-element.35), channel_id=1, source_target_pairs={{0,1},{1,2},{2,3},{3,0},{64,67},{65,64},{66,65},{67,66},{4,5},{5,6... | collective-permute-start | bytes 393224 | tf_op jit(solution)/shard_map/ppermute | solution.py:32
  65.2 11.9 %collective-permute-start.6 = (bf16[2,256,128]{2,1,0:T(8,128)(2,1)S(1)}, bf16[2,256,128]{2,1,0:T(8,128)(2,1)S(1)}, u32[]{:S(2)}, u32[]{:S(2)}) collective-permute-start(bf16[2,256,128]{2,1,0:T(8,128)(2,1)S(1)} %get-tuple-element.34), channel_id=1, source_target_pairs={{0,3},{1,0},{2,1},{3,2},{64,65},{65,66},{66,67},{67,64},{4,7},{5,4... | collective-permute-start | bytes 393224 | tf_op jit(solution)/shard_map/ppermute | solution.py:32
  65.2 5.8 %collective-permute-start.13 = (bf16[2,256,128]{2,1,0:T(8,128)(2,1)S(1)}, bf16[2,256,128]{2,1,0:T(8,128)(2,1)S(1)}, u32[]{:S(2)}, u32[]{:S(2)}) collective-permute-start(bf16[2,256,128]{2,1,0:T(8,128)(2,1)S(1)} %get-tuple-element.32), channel_id=1, source_target_pairs={{0,48},{16,0},{32,16},{48,32},{64,80},{80,96},{96,112},{112,64},{1... | collective-permute-start | bytes 393224 | tf_op jit(solution)/shard_map/ppermute | solution.py:32
  67.2 4.9 %collective-permute-start.15 = (bf16[2,256,128]{2,1,0:T(8,128)(2,1)S(1)}, bf16[2,256,128]{2,1,0:T(8,128)(2,1)S(1)}, u32[]{:S(2)}, u32[]{:S(2)}) collective-permute-start(bf16[2,256,128]{2,1,0:T(8,128)(2,1)S(1)} %fusion.11), channel_id=1, source_target_pairs={{0,16},{16,32},{32,48},{48,0},{64,112},{80,64},{96,80},{112,96},{1... | collective-permute-start | bytes 393224 | tf_op jit(solution)/shard_map/ppermute | solution.py:32
  68.6 8.5 %collective-permute-start.8 = (bf16[2,256,128]{2,1,0:T(8,128)(2,1)S(1)}, bf16[2,256,128]{2,1,0:T(8,128)(2,1)S(1)}, u32[]{:S(2)}, u32[]{:S(2)}) collective-permute-start(bf16[2,256,128]{2,1,0:T(8,128)(2,1)S(1)} %fusion.16), channel_id=1, source_target_pairs={{0,1},{1,2},{2,3},{3,0},{64,67},{65,64},{66,65},{67,66},{4,5},{5,6... | collective-permute-start | bytes 393224 | tf_op jit(solution)/shard_map/ppermute | solution.py:32
  72.3 6.2 %collective-permute-start.17 = (bf16[256,128]{1,0:T(8,128)(2,1)S(1)}, bf16[256,128]{1,0:T(8,128)(2,1)S(1)}, u32[]{:S(2)}, u32[]{:S(2)}) collective-permute-start(bf16[256,128]{1,0:T(8,128)(2,1)S(1)} %get-tuple-element.39), channel_id=1, source_target_pairs={{0,12},{4,0},{8,4},{12,8},{1,13},{5,1},{9,5},{13,9},{2,14},{6,2},{... | collective-permute-start | bytes 196616 | tf_op jit(solution)/shard_map/ppermute | solution.py:27
  77.1 4.1 %collective-permute-start.16 = (bf16[256,128]{1,0:T(8,128)(2,1)S(1)}, bf16[256,128]{1,0:T(8,128)(2,1)S(1)}, u32[]{:S(2)}, u32[]{:S(2)}) collective-permute-start(bf16[256,128]{1,0:T(8,128)(2,1)S(1)} %get-tuple-element.38), channel_id=1, source_target_pairs={{0,8},{4,12},{8,0},{12,4},{1,9},{5,13},{9,1},{13,5},{2,10},{6,14},... | collective-permute-start | bytes 196616 | tf_op jit(solution)/shard_map/ppermute | solution.py:27
  77.2 5.0 %collective-permute-start.9 = (bf16[256,128]{1,0:T(8,128)(2,1)S(1)}, bf16[256,128]{1,0:T(8,128)(2,1)S(1)}, u32[]{:S(2)}, u32[]{:S(2)}) collective-permute-start(bf16[256,128]{1,0:T(8,128)(2,1)S(1)} %fusion.23), channel_id=1, source_target_pairs={{0,4},{4,8},{8,12},{12,0},{1,5},{5,9},{9,13},{13,1},{2,6},{6,10},{... | collective-permute-start | bytes 196616 | tf_op jit(solution)/shard_map/ppermute | solution.py:27
  82.3 7.7 %collective-permute-start.18 = (bf16[2,128,128]{2,1,0:T(8,128)(2,1)S(1)}, bf16[2,128,128]{2,1,0:T(8,128)(2,1)S(1)}, u32[]{:S(2)}, u32[]{:S(2)}) collective-permute-start(bf16[2,128,128]{2,1,0:T(8,128)(2,1)S(1)} %add_convert_fusion.4), channel_id=1, source_target_pairs={{0,128},{128,0},{1,129},{129,1},{2,130},{130,2},{3,131},{131,3},{4... | collective-permute-start | bytes 196616 | tf_op jit(solution)/shard_map/ppermute | solution.py:36
  90.2 7.8 %collective-permute-start.19 = (f32[2,128,128]{2,1,0:T(8,128)S(1)}, f32[2,128,128]{2,1,0:T(8,128)S(1)}, u32[]{:S(2)}, u32[]{:S(2)}) collective-permute-start(f32[2,128,128]{2,1,0:T(8,128)S(1)} %get-tuple-element.37), channel_id=1, source_target_pairs={{0,64},{64,0},{1,65},{65,1},{2,66},{66,2},{3,67},{67,3},{4,68},{68... | collective-permute-start | bytes 393224 | tf_op jit(solution)/shard_map/ppermute | solution.py:36

commit v2 on v1

--- a/solution.py
+++ b/solution.py
@@ -12,7 +12,8 @@
 
 BLOCK = 128
 ROWS_AT_A_TIME = 64
-VMEM_LIMIT = 24 * 2**20
+FIRST_LIMIT = 38
+LATER_LIMIT = 24
 FSDP = ("x", "zl", "y")
 GROUP = ("zh", "core")
 
@@ -83,15 +84,25 @@
         lax.fori_loop(0, self.count, body, 0)
 
 
-def first_kernel(factor, place, tokens, keys, gain, send, own, grads, scaled):
+def first_kernel(factor, place, tokens, keys, gain, send, own, held, grads, scaled, load):
     count, width = tokens.shape
 
+    def rows_of(i):
+        return pl.ds(pl.multiple_of(i * ROWS_AT_A_TIME, ROWS_AT_A_TIME), ROWS_AT_A_TIME)
+
+    def read(i):
+        return pltpu.make_async_copy(tokens.at[rows_of(i)], held.at[rows_of(i)], load.at[i])
+
+    for i in range(count // ROWS_AT_A_TIME):
+        read(i).start()
+
     def squares(i, carry):
-        rows = pl.ds(pl.multiple_of(i * ROWS_AT_A_TIME, ROWS_AT_A_TIME), ROWS_AT_A_TIME)
+        read(i).wait()
+        rows = rows_of(i)
 
         def add(j, total):
             for k in range(8):
-                part = tokens[rows, pl.ds(pl.multiple_of((j * 8 + k) * BLOCK, BLOCK), BLOCK)].astype(jnp.float32)
+                part = held[rows, pl.ds(pl.multiple_of((j * 8 + k) * BLOCK, BLOCK), BLOCK)].astype(jnp.float32)
                 total = total + part * part
             return total
 
@@ -112,14 +123,14 @@
             square = scaled[t * BLOCK : (t + 1) * BLOCK, group * BLOCK : (group + 1) * BLOCK]
             grads[at, t * BLOCK : (t + 1) * BLOCK] = square.T.astype(jnp.bfloat16)
 
-    Tiles(place, (2,)).products(tokens, grads, gain, send, own)
+    Tiles(place, (2,)).products(held, grads, gain, send, own)
 
 
 def later_kernel(distances, place, tokens, grads, gain, send, own):
     Tiles(place, distances).products(tokens, grads, gain, send, own)
 
 
-def terms(kernel, distances, outs, scratch, place, tokens, grads, gain):
+def terms(kernel, distances, outs, scratch, tokens_in, limit, place, tokens, grads, gain):
     count = tokens.shape[0]
     cols = 4 * BLOCK
     part = jax.ShapeDtypeStruct((len(distances), 2, 4, 2, cols // 2, BLOCK), jnp.bfloat16)
@@ -130,23 +141,25 @@
     return pl.pallas_call(
         kernel,
         out_shape=outs,
-        in_specs=[in_smem, in_vmem, in_vmem, in_vmem],
+        in_specs=[in_smem, pl.BlockSpec(memory_space=tokens_in), in_vmem, in_vmem],
         out_specs=[in_vmem] * len(outs),
         scratch_shapes=scratch,
         cost_estimate=pl.CostEstimate(flops=flops, bytes_accessed=2**20, transcendentals=0),
-        compiler_params=pltpu.CompilerParams(vmem_limit_bytes=VMEM_LIMIT),
+        compiler_params=pltpu.CompilerParams(vmem_limit_bytes=limit * 2**20),
     )(place, tokens, grads, gain)
 
 
 def first_terms(place, tokens, keys, gain, factor):
     count, cols = keys.shape
-    grads = jax.ShapeDtypeStruct((cols, count), jnp.bfloat16)
-    scratch = [pltpu.VMEM((count, cols), jnp.float32)]
-    return terms(functools.partial(first_kernel, factor), (2,), [grads], scratch, place, tokens, keys, gain)
+    outs = [jax.ShapeDtypeStruct(tokens.shape, jnp.bfloat16), jax.ShapeDtypeStruct((cols, count), jnp.bfloat16)]
+    scratch = [pltpu.VMEM((count, cols), jnp.float32), pltpu.SemaphoreType.DMA((count // ROWS_AT_A_TIME,))]
+    kernel = functools.partial(first_kernel, factor)
+    return terms(kernel, (2,), outs, scratch, pl.ANY, FIRST_LIMIT, place, tokens, keys, gain)
 
 
 def later_terms(distances, place, tokens, grads, gain):
-    return terms(functools.partial(later_kernel, distances), distances, [], [], place, tokens, grads, gain)
+    kernel = functools.partial(later_kernel, distances)
+    return terms(kernel, distances, [], [], pltpu.VMEM, LATER_LIMIT, place, tokens, grads, gain)
 
 
 def ring_sum(terms, axis):
@@ -165,13 +178,13 @@
     gain = norm_gain[None, :]
     axes = ("x", "y")
 
-    send, own, grads = first_terms(place, tokens[0], keys_grad[0], gain, factor)
+    send, own, held, grads = first_terms(place, tokens[0], keys_grad[0], gain, factor)
     received = swap(send, "core")
     far = [None, None]
     for c in (0, 1):
         far[c] = onward(narrow(wide(own[0, c]) + wide(received[0, c])), axes[c], 1)
 
-    send, own = later_terms((1, 3), place, tokens[0], grads, gain)
+    send, own = later_terms((1, 3), place, held, grads, gain)
     received = swap(send, "core")
     sides = [[wide(own[i, c]) + wide(received[i, c]) for i in (0, 1)] for c in (0, 1)]
     back = [None, None]
@@ -182,7 +195,7 @@
     for c in (0, 1):
         front[c] = onward(narrow(sides[c][0] + wide(far[c])), axes[c], 1)
 
-    send, own = later_terms((0,), place, tokens[0], grads, gain)
+    send, own = later_terms((0,), place, held, grads, gain)
     received = swap(send, "core")
     sums = [wide(own[0, c]) + wide(received[0, c]) + wide(back[c]) + wide(front[c]) for c in (0, 1)]
 

time: 99.1 us -> 96.4 us (0.973)
  local copies, waits for them, and re-layouts: 7.71 us -> 3.73 us
  Pallas kernels: 16.8 us -> 18.2 us
    unnamed x14, local copies, waits for them, and re-layouts: 7.54 us -> 3.56 us
    pallas_call x3, Pallas kernels: 16.8 us -> 18.2 us  [terms(): pl.pallas_call(kernel, out_shape=outs, in_specs=[in_smem, pl.BlockSpec(me...]
    ppermute x5, starting transfers between devices: 15.2 us -> 14.1 us  [swap(): return lax.ppermute(block, axis, [(0, 1), (1, 0)])]
where the time goes in v2:
time: 96.4 us; the launch traced here: 96.2 us
  starting transfers between devices  35 us (36%)
  waiting for transfers between devices  32.7 us (34%)
  Pallas kernels  18.2 us (19%)
  other arithmetic  5.72 us (6%)
  local copies, waits for them, and re-layouts  3.73 us (4%)
    ppermute x12, waiting for transfers between devices, onward(): return lax.ppermute(block, ('core', axis), route)  19.6 us
    pallas_call x3, Pallas kernels, terms(): pl.pallas_call(kernel, out_shape=outs, in_specs=[in_smem, pl.BlockSpec(me...  18.2 us
    ppermute x12, starting transfers between devices, onward(): return lax.ppermute(block, ('core', axis), route)  15 us
    ppermute x5, starting transfers between devices, swap(): return lax.ppermute(block, axis, [(0, 1), (1, 0)])  14.1 us
    ppermute x5, waiting for transfers between devices, swap(): return lax.ppermute(block, axis, [(0, 1), (1, 0)])  8.41 us
    ppermute x3, starting transfers between devices, shift(): lax.ppermute(block, axis, [(i, (i + step) % count) for i in range(count)])  5.92 us
    ppermute x3, waiting for transfers between devices, shift(): lax.ppermute(block, axis, [(i, (i + step) % count) for i in range(count)])  4.63 us
    unnamed x14, local copies, waits for them, and re-layouts  3.56 us
  transfers between devices with their start and end apart: 20, of which 14 were waited for; matrix products, arithmetic and copies ran while one was open for 4% of the time, Pallas kernels for 3%

profile of v2, /device:TPU:1, one launch (start us, length us, event | category | flops | bytes accessed | tf_op | source)
XLA Modules:
  0.0 96.2 jit_solution(17030029610267728006)
XLA Ops:
  0.7 1.1 %copy-done = bf16[1,640,512]{2,1,0:T(8,128)(2,1)S(1)} copy-done((bf16[1,640,512]{2,1,0:T(8,128)(2,1)S(1)}, bf16[1,640,512]{2,1,0:T(8,128)(2,1)}, u32[]{:S(2)}) %copy-start) | copy-done | bytes 655384
  1.8 0.8 copy-done.1
  2.6 9.0 %shard_map.68 = (bf16[1,2,4,2,256,128]{5,4,3,2,1,0:T(8,128)(2,1)S(1)}, bf16[1,2,4,2,256,128]{5,4,3,2,1,0:T(8,128)(2,1)S(1)}, bf16[640,8192]{1,0:T(8,128)(2,1)S(1)}, bf16[512,640]{1,0:T(8,128)(2,1)S(1)}) custom-call(s32[4]{0:T(128)S(1)} %pad_add_fusion.place, bf16[640,8192]{1,0:T(8,128)(2,1)} %bitcast.111, bf16[640,512]{1,0:T(8,128)(2,1)S(1)} %bitcast.107, ...), custom_call_target="tpu_custom_call" | custom-call | flops 1342177280 | bytes 1048576 | tf_op jit(solution)/shard_map/pallas_call | solution.py:141
  11.5 6.0 %shard_map.70 = (bf16[2,2,4,2,256,128]{5,4,3,2,1,0:T(8,128)(2,1)S(1)}, bf16[2,2,4,2,256,128]{5,4,3,2,1,0:T(8,128)(2,1)S(1)}) custom-call(s32[4]{0:T(128)S(1)} %pad_add_fusion.place, bf16[640,8192]{1,0:T(8,128)(2,1)S(1)} %get-tuple-element.10.tokens, bf16[512,640]{1,0:T(8,128)(2,1)S(1)} %get-tuple-element.11.grads, f32[1,8192]{1,0:T(1,128)S(1)} %bitcast.109), custom_call_target="tpu_custom_call" | custom-call | flops 2684354560 | bytes 1048576 | tf_op jit(solution)/shard_map/pallas_call | solution.py:141
  17.5 3.3 %collective-permute-start.1 = (bf16[2,2,4,2,256,128]{5,4,3,2,1,0:T(8,128)(2,1)S(1)}, bf16[2,2,4,2,256,128]{5,4,3,2,1,0:T(8,128)(2,1)S(1)}, u32[]{:S(2)}, u32[]{:S(2)}) collective-permute-start(bf16[2,2,4,2,256,128]{5,4,3,2,1,0:T(8,128)(2,1)S(1)} %get-tuple-element.15), channel_id=1, source_target_pairs={{0,64},{64,0},{1,65},{65,1},{2,66},{66,2},{3,67},{67,3},{4,68},{68... | collective-permute-start | bytes 6291464 | tf_op jit(solution)/shard_map/ppermute | solution.py:37
  20.9 5.2 %collective-permute-done.3 = bf16[1,2,4,2,256,128]{5,4,3,2,1,0:T(8,128)(2,1)S(1)} collective-permute-done((bf16[1,2,4,2,256,128]{5,4,3,2,1,0:T(8,128)(2,1)S(1)}, bf16[1,2,4,2,256,128]{5,4,3,2,1,0:T(8,128)(2,1)S(1)}, u32[]{:S(2)}, u32[]{:S(2)}) %collective-permute-start.3) | collective-permute-done | bytes 1048608 | tf_op jit(solution)/shard_map/ppermute | solution.py:37
  26.4 1.1 %collective-permute-start.11 = (bf16[4,2,256,128]{3,2,1,0:T(8,128)(2,1)S(1)}, bf16[4,2,256,128]{3,2,1,0:T(8,128)(2,1)S(1)}, u32[]{:S(2)}, u32[]{:S(2)}) collective-permute-start(bf16[4,2,256,128]{3,2,1,0:T(8,128)(2,1)S(1)} %get-tuple-element.32), channel_id=1, source_target_pairs={{0,1},{1,2},{2,3},{3,0},{64,67},{65,64},{66,65},{67,66},{4,5},{5,6... | collective-permute-start | bytes 1572872 | tf_op jit(solution)/shard_map/ppermute | solution.py:33
  27.5 2.5 %collective-permute-start.4 = (bf16[4,2,256,128]{3,2,1,0:T(8,128)(2,1)S(1)}, bf16[4,2,256,128]{3,2,1,0:T(8,128)(2,1)S(1)}, u32[]{:S(2)}, u32[]{:S(2)}) collective-permute-start(bf16[4,2,256,128]{3,2,1,0:T(8,128)(2,1)S(1)} %get-tuple-element.33), channel_id=1, source_target_pairs={{0,16},{16,32},{32,48},{48,0},{64,112},{80,64},{96,80},{112,96},{1... | collective-permute-start | bytes 1572872 | tf_op jit(solution)/shard_map/ppermute | solution.py:33
  29.9 3.3 %shard_map.69 = (bf16[1,2,4,2,256,128]{5,4,3,2,1,0:T(8,128)(2,1)S(1)}, bf16[1,2,4,2,256,128]{5,4,3,2,1,0:T(8,128)(2,1)S(1)}) custom-call(s32[4]{0:T(128)S(1)} %pad_add_fusion.place, bf16[640,8192]{1,0:T(8,128)(2,1)S(1)} %get-tuple-element.10.tokens, bf16[512,640]{1,0:T(8,128)(2,1)S(1)} %get-tuple-element.11.grads, f32[1,8192]{1,0:T(1,128)S(1)} %bitcast.110), custom_call_target="tpu_custom_call" | custom-call | flops 1342177280 | bytes 1048576 | tf_op jit(solution)/shard_map/pallas_call | solution.py:141
  33.3 1.5 %collective-permute-done.11 = bf16[4,2,256,128]{3,2,1,0:T(8,128)(2,1)S(1)} collective-permute-done((bf16[4,2,256,128]{3,2,1,0:T(8,128)(2,1)S(1)}, bf16[4,2,256,128]{3,2,1,0:T(8,128)(2,1)S(1)}, u32[]{:S(2)}, u32[]{:S(2)}) %collective-permute-start.11) | collective-permute-done | bytes 524320 | tf_op jit(solution)/shard_map/ppermute | solution.py:33
  34.8 1.3 %collective-permute-done.4 = bf16[4,2,256,128]{3,2,1,0:T(8,128)(2,1)S(1)} collective-permute-done((bf16[4,2,256,128]{3,2,1,0:T(8,128)(2,1)S(1)}, bf16[4,2,256,128]{3,2,1,0:T(8,128)(2,1)S(1)}, u32[]{:S(2)}, u32[]{:S(2)}) %collective-permute-start.4) | collective-permute-done | bytes 524320 | tf_op jit(solution)/shard_map/ppermute | solution.py:33
  36.1 1.4 %fusion = (bf16[4,2,256,128]{3,2,1,0:T(8,128)(2,1)}, bf16[4,2,256,128]{3,2,1,0:T(8,128)(2,1)}) fusion(bf16[4,2,256,128]{3,2,1,0:T(8,128)(2,1)S(1)} %collective-permute-done.11, bf16[2,2,4,2,256,128]{5,4,3,2,1,0:T(8,128)(2,1)S(1)} %collective-permute-done.1, bf16[2,2,4,2,256,128]{5,4,3,2,1,0:T(8,128)(2,1)S(1)} %get-tuple-element.14, ...), kind=kLoop, calls=%fused_computation.1 | loop fusion | flops 3145728 | bytes 4194304 | tf_op jit(solution)/shard_map/convert_element_type | solution.py:45
  37.5 0.9 collective-permute-start.12
  38.4 1.3 %fusion.6 = (bf16[4,2,256,128]{3,2,1,0:T(8,128)(2,1)}, bf16[4,2,256,128]{3,2,1,0:T(8,128)(2,1)}) fusion(bf16[2,2,4,2,256,128]{5,4,3,2,1,0:T(8,128)(2,1)S(1)} %collective-permute-done.1, bf16[2,2,4,2,256,128]{5,4,3,2,1,0:T(8,128)(2,1)S(1)} %get-tuple-element.14), kind=kLoop, calls=%fused_computation.14 | loop fusion | flops 2097152 | bytes 3145728 | tf_op jit(solution)/shard_map/convert_element_type | solution.py:45
  40.2 3.1 %collective-permute-start.5 = (bf16[4,2,256,128]{3,2,1,0:T(8,128)(2,1)}, bf16[4,2,256,128]{3,2,1,0:T(8,128)(2,1)}, u32[]{:S(2)}, u32[]{:S(2)}) collective-permute-start(bf16[4,2,256,128]{3,2,1,0:T(8,128)(2,1)} %get-tuple-element.29), channel_id=1, source_target_pairs={{0,16},{16,32},{32,48},{48,0},{64,112},{80,64},{96,80},{112,96},{1... | collective-permute-start | bytes 1572872 | tf_op jit(solution)/shard_map/ppermute | solution.py:33
  43.5 4.0 %collective-permute-done.12 = bf16[4,2,256,128]{3,2,1,0:T(8,128)(2,1)} collective-permute-done((bf16[4,2,256,128]{3,2,1,0:T(8,128)(2,1)}, bf16[4,2,256,128]{3,2,1,0:T(8,128)(2,1)}, u32[]{:S(2)}, u32[]{:S(2)}) %collective-permute-start.12) | collective-permute-done | bytes 524320 | tf_op jit(solution)/shard_map/ppermute | solution.py:33
  47.5 7.2 %collective-permute-done.10 = bf16[4,2,256,128]{3,2,1,0:T(8,128)(2,1)} collective-permute-done((bf16[4,2,256,128]{3,2,1,0:T(8,128)(2,1)}, bf16[4,2,256,128]{3,2,1,0:T(8,128)(2,1)}, u32[]{:S(2)}, u32[]{:S(2)}) %collective-permute-start.10) | collective-permute-done | bytes 524320 | tf_op jit(solution)/shard_map/ppermute | solution.py:33
  54.7 3.8 %collective-permute-done.2 = bf16[4,2,256,128]{3,2,1,0:T(8,128)(2,1)} collective-permute-done((bf16[4,2,256,128]{3,2,1,0:T(8,128)(2,1)}, bf16[4,2,256,128]{3,2,1,0:T(8,128)(2,1)}, u32[]{:S(2)}, u32[]{:S(2)}) %collective-permute-start.2) | collective-permute-done | bytes 524320 | tf_op jit(solution)/shard_map/ppermute | solution.py:33
  58.5 2.2 %fusion.28 = (bf16[4,2,256,128]{3,2,1,0:T(8,128)(2,1)S(1)}, f32[4,2,256,128]{3,2,1,0:T(8,128)S(1)}, bf16[4,2,256,128]{3,2,1,0:T(8,128)(2,1)S(1)}, f32[4,2,256,128]{3,2,1,0:T(8,128)S(1)}) fusion(bf16[4,2,256,128]{3,2,1,0:T(8,128)(2,1)} %collective-permute-done.12, bf16[4,2,256,128]{3,2,1,0:T(8,128)(2,1)} %collective-permute-done.10, ...), kind=kLoop, calls=%fused_computation.60 | loop fusion | flops 4194304 | bytes 7340032 | tf_op jit(solution)/shard_map/convert.5
  60.8 1.8 %collective-permute-start.7 = (bf16[2,256,128]{2,1,0:T(8,128)(2,1)S(1)}, bf16[2,256,128]{2,1,0:T(8,128)(2,1)S(1)}, u32[]{:S(2)}, u32[]{:S(2)}) collective-permute-start(bf16[2,256,128]{2,1,0:T(8,128)(2,1)S(1)} %get-tuple-element.37), channel_id=1, source_target_pairs={{0,1},{1,2},{2,3},{3,0},{64,67},{65,64},{66,65},{67,66},{4,5},{5,6... | collective-permute-start | bytes 393224 | tf_op jit(solution)/shard_map/ppermute | solution.py:33
  62.6 1.4 %collective-permute-start.13 = (bf16[2,256,128]{2,1,0:T(8,128)(2,1)S(1)}, bf16[2,256,128]{2,1,0:T(8,128)(2,1)S(1)}, u32[]{:S(2)}, u32[]{:S(2)}) collective-permute-start(bf16[2,256,128]{2,1,0:T(8,128)(2,1)S(1)} %get-tuple-element.34), channel_id=1, source_target_pairs={{0,48},{16,0},{32,16},{48,32},{64,80},{80,96},{96,112},{112,64},{1... | collective-permute-start | bytes 393224 | tf_op jit(solution)/shard_map/ppermute | solution.py:33
  64.6 1.3 %collective-permute-start.15 = (bf16[2,256,128]{2,1,0:T(8,128)(2,1)S(1)}, bf16[2,256,128]{2,1,0:T(8,128)(2,1)S(1)}, u32[]{:S(2)}, u32[]{:S(2)}) collective-permute-start(bf16[2,256,128]{2,1,0:T(8,128)(2,1)S(1)} %fusion.11), channel_id=1, source_target_pairs={{0,16},{16,32},{32,48},{48,0},{64,112},{80,64},{96,80},{112,96},{1... | collective-permute-start | bytes 393224 | tf_op jit(solution)/shard_map/ppermute | solution.py:33
  65.9 2.3 %collective-permute-start.8 = (bf16[2,256,128]{2,1,0:T(8,128)(2,1)S(1)}, bf16[2,256,128]{2,1,0:T(8,128)(2,1)S(1)}, u32[]{:S(2)}, u32[]{:S(2)}) collective-permute-start(bf16[2,256,128]{2,1,0:T(8,128)(2,1)S(1)} %fusion.16), channel_id=1, source_target_pairs={{0,1},{1,2},{2,3},{3,0},{64,67},{65,64},{66,65},{67,66},{4,5},{5,6... | collective-permute-start | bytes 393224 | tf_op jit(solution)/shard_map/ppermute | solution.py:33
  68.4 1.2 %collective-permute-done.15 = bf16[2,256,128]{2,1,0:T(8,128)(2,1)S(1)} collective-permute-done((bf16[2,256,128]{2,1,0:T(8,128)(2,1)S(1)}, bf16[2,256,128]{2,1,0:T(8,128)(2,1)S(1)}, u32[]{:S(2)}, u32[]{:S(2)}) %collective-permute-start.15) | collective-permute-done | bytes 131104 | tf_op jit(solution)/shard_map/ppermute | solution.py:33
  69.6 5.5 %collective-permute-start.17 = (bf16[256,128]{1,0:T(8,128)(2,1)S(1)}, bf16[256,128]{1,0:T(8,128)(2,1)S(1)}, u32[]{:S(2)}, u32[]{:S(2)}) collective-permute-start(bf16[256,128]{1,0:T(8,128)(2,1)S(1)} %get-tuple-element.41), channel_id=1, source_target_pairs={{0,12},{4,0},{8,4},{12,8},{1,13},{5,1},{9,5},{13,9},{2,14},{6,2},{... | collective-permute-start | bytes 196616 | tf_op jit(solution)/shard_map/ppermute | solution.py:28
  75.6 0.8 collective-permute-done.17
  76.4 2.7 %collective-permute-done.16 = bf16[256,128]{1,0:T(8,128)(2,1)S(1)} collective-permute-done((bf16[256,128]{1,0:T(8,128)(2,1)S(1)}, bf16[256,128]{1,0:T(8,128)(2,1)S(1)}, u32[]{:S(2)}, u32[]{:S(2)}) %collective-permute-start.16) | collective-permute-done | bytes 65568 | tf_op jit(solution)/shard_map/ppermute | solution.py:28
  79.2 1.1 %collective-permute-done.9 = bf16[256,128]{1,0:T(8,128)(2,1)S(1)} collective-permute-done((bf16[256,128]{1,0:T(8,128)(2,1)S(1)}, bf16[256,128]{1,0:T(8,128)(2,1)S(1)}, u32[]{:S(2)}, u32[]{:S(2)}) %collective-permute-start.9) | collective-permute-done | bytes 65568 | tf_op jit(solution)/shard_map/ppermute | solution.py:28
  80.4 4.5 %collective-permute-start.18 = (bf16[2,128,128]{2,1,0:T(8,128)(2,1)S(1)}, bf16[2,128,128]{2,1,0:T(8,128)(2,1)S(1)}, u32[]{:S(2)}, u32[]{:S(2)}) collective-permute-start(bf16[2,128,128]{2,1,0:T(8,128)(2,1)S(1)} %add_convert_fusion.4), channel_id=1, source_target_pairs={{0,128},{128,0},{1,129},{129,1},{2,130},{130,2},{3,131},{131,3},{4... | collective-permute-start | bytes 196616 | tf_op jit(solution)/shard_map/ppermute | solution.py:37
  85.1 3.0 %collective-permute-done.18 = bf16[2,128,128]{2,1,0:T(8,128)(2,1)S(1)} collective-permute-done((bf16[2,128,128]{2,1,0:T(8,128)(2,1)S(1)}, bf16[2,128,128]{2,1,0:T(8,128)(2,1)S(1)}, u32[]{:S(2)}, u32[]{:S(2)}) %collective-permute-start.18) | collective-permute-done | bytes 65568 | tf_op jit(solution)/shard_map/ppermute | solution.py:37
  88.2 6.1 %collective-permute-start.19 = (f32[2,128,128]{2,1,0:T(8,128)S(1)}, f32[2,128,128]{2,1,0:T(8,128)S(1)}, u32[]{:S(2)}, u32[]{:S(2)}) collective-permute-start(f32[2,128,128]{2,1,0:T(8,128)S(1)} %get-tuple-element.39), channel_id=1, source_target_pairs={{0,64},{64,0},{1,65},{65,1},{2,66},{66,2},{3,67},{67,3},{4,68},{68... | collective-permute-start | bytes 393224 | tf_op jit(solution)/shard_map/ppermute | solution.py:37
  95.4 0.8 copy.14
  (49 shorter events, 4.2 us)
Async XLA Ops:
  0.7 1.1 %copy-start = (bf16[1,640,512]{2,1,0:T(8,128)(2,1)S(1)}, bf16[1,640,512]{2,1,0:T(8,128)(2,1)}, u32[]{:S(2)}) copy-start(bf16[1,640,512]{2,1,0:T(8,128)(2,1)} %param.6) | copy-start | bytes 1966084
  1.8 0.8 copy-start.1
  2.6 9.0 %copy-start.2 = (f32[8192]{0:T(1024)S(1)}, f32[8192]{0:T(1024)}, u32[]{:S(2)}) copy-start(f32[8192]{0:T(1024)} %param.7) | copy-start | bytes 98308
  17.5 18.6 %collective-permute-start.1 = (bf16[2,2,4,2,256,128]{5,4,3,2,1,0:T(8,128)(2,1)S(1)}, bf16[2,2,4,2,256,128]{5,4,3,2,1,0:T(8,128)(2,1)S(1)}, u32[]{:S(2)}, u32[]{:S(2)}) collective-permute-start(bf16[2,2,4,2,256,128]{5,4,3,2,1,0:T(8,128)(2,1)S(1)} %get-tuple-element.15), channel_id=1, source_target_pairs={{0,64},{64,0},{1,65},{65,1},{2,66},{66,2},{3,67},{67,3},{4,68},{68... | collective-permute-start | bytes 6291464 | tf_op jit(solution)/shard_map/ppermute | solution.py:37
  20.8 5.3 %collective-permute-start.3 = (bf16[1,2,4,2,256,128]{5,4,3,2,1,0:T(8,128)(2,1)S(1)}, bf16[1,2,4,2,256,128]{5,4,3,2,1,0:T(8,128)(2,1)S(1)}, u32[]{:S(2)}, u32[]{:S(2)}) collective-permute-start(bf16[1,2,4,2,256,128]{5,4,3,2,1,0:T(8,128)(2,1)S(1)} %get-tuple-element.17), channel_id=1, source_target_pairs={{0,64},{64,0},{1,65},{65,1},{2,66},{66,2},{3,67},{67,3},{4,68},{68... | collective-permute-start | bytes 3145736 | tf_op jit(solution)/shard_map/ppermute | solution.py:37
  26.4 8.4 %collective-permute-start.11 = (bf16[4,2,256,128]{3,2,1,0:T(8,128)(2,1)S(1)}, bf16[4,2,256,128]{3,2,1,0:T(8,128)(2,1)S(1)}, u32[]{:S(2)}, u32[]{:S(2)}) collective-permute-start(bf16[4,2,256,128]{3,2,1,0:T(8,128)(2,1)S(1)} %get-tuple-element.32), channel_id=1, source_target_pairs={{0,1},{1,2},{2,3},{3,0},{64,67},{65,64},{66,65},{67,66},{4,5},{5,6... | collective-permute-start | bytes 1572872 | tf_op jit(solution)/shard_map/ppermute | solution.py:33
  27.5 8.6 %collective-permute-start.4 = (bf16[4,2,256,128]{3,2,1,0:T(8,128)(2,1)S(1)}, bf16[4,2,256,128]{3,2,1,0:T(8,128)(2,1)S(1)}, u32[]{:S(2)}, u32[]{:S(2)}) collective-permute-start(bf16[4,2,256,128]{3,2,1,0:T(8,128)(2,1)S(1)} %get-tuple-element.33), channel_id=1, source_target_pairs={{0,16},{16,32},{32,48},{48,0},{64,112},{80,64},{96,80},{112,96},{1... | collective-permute-start | bytes 1572872 | tf_op jit(solution)/shard_map/ppermute | solution.py:33
  33.2 10.3 %collective-permute-start = (bf16[1,2,4,2,256,128]{5,4,3,2,1,0:T(8,128)(2,1)S(1)}, bf16[1,2,4,2,256,128]{5,4,3,2,1,0:T(8,128)(2,1)S(1)}, u32[]{:S(2)}, u32[]{:S(2)}) collective-permute-start(bf16[1,2,4,2,256,128]{5,4,3,2,1,0:T(8,128)(2,1)S(1)} %get-tuple-element.13), channel_id=1, source_target_pairs={{0,64},{64,0},{1,65},{65,1},{2,66},{66,2},{3,67},{67,3},{4,68},{68... | collective-permute-start | bytes 3145736 | tf_op jit(solution)/shard_map/ppermute | solution.py:37
  37.5 5.8 %copy-start.3 = (f32[128,128]{1,0:T(8,128)S(1)}, f32[128,128]{1,0:T(8,128)}, u32[]{:S(2)}) copy-start(f32[128,128]{1,0:T(8,128)} %param.9) | copy-start | bytes 196612
  37.5 10.0 %collective-permute-start.12 = (bf16[4,2,256,128]{3,2,1,0:T(8,128)(2,1)}, bf16[4,2,256,128]{3,2,1,0:T(8,128)(2,1)}, u32[]{:S(2)}, u32[]{:S(2)}) collective-permute-start(bf16[4,2,256,128]{3,2,1,0:T(8,128)(2,1)} %get-tuple-element.28), channel_id=1, source_target_pairs={{0,1},{1,2},{2,3},{3,0},{64,67},{65,64},{66,65},{67,66},{4,5},{5,6... | collective-permute-start | bytes 1572872 | tf_op jit(solution)/shard_map/ppermute | solution.py:33
  39.7 15.0 %collective-permute-start.10 = (bf16[4,2,256,128]{3,2,1,0:T(8,128)(2,1)}, bf16[4,2,256,128]{3,2,1,0:T(8,128)(2,1)}, u32[]{:S(2)}, u32[]{:S(2)}) collective-permute-start(bf16[4,2,256,128]{3,2,1,0:T(8,128)(2,1)} %get-tuple-element.26), channel_id=1, source_target_pairs={{0,3},{1,0},{2,1},{3,2},{64,65},{65,66},{66,67},{67,64},{4,7},{5,4... | collective-permute-start | bytes 1572872 | tf_op jit(solution)/shard_map/ppermute | solution.py:33
  40.2 14.4 %collective-permute-start.5 = (bf16[4,2,256,128]{3,2,1,0:T(8,128)(2,1)}, bf16[4,2,256,128]{3,2,1,0:T(8,128)(2,1)}, u32[]{:S(2)}, u32[]{:S(2)}) collective-permute-start(bf16[4,2,256,128]{3,2,1,0:T(8,128)(2,1)} %get-tuple-element.29), channel_id=1, source_target_pairs={{0,16},{16,32},{32,48},{48,0},{64,112},{80,64},{96,80},{112,96},{1... | collective-permute-start | bytes 1572872 | tf_op jit(solution)/shard_map/ppermute | solution.py:33
  43.3 15.1 %collective-permute-start.2 = (bf16[4,2,256,128]{3,2,1,0:T(8,128)(2,1)}, bf16[4,2,256,128]{3,2,1,0:T(8,128)(2,1)}, u32[]{:S(2)}, u32[]{:S(2)}) collective-permute-start(bf16[4,2,256,128]{3,2,1,0:T(8,128)(2,1)} %get-tuple-element.27), channel_id=1, source_target_pairs={{0,48},{16,0},{32,16},{48,32},{64,80},{80,96},{96,112},{112,64},{1... | collective-permute-start | bytes 1572872 | tf_op jit(solution)/shard_map/ppermute | solution.py:33
  60.7 3.9 %collective-permute-start.14 = (bf16[2,256,128]{2,1,0:T(8,128)(2,1)S(1)}, bf16[2,256,128]{2,1,0:T(8,128)(2,1)S(1)}, u32[]{:S(2)}, u32[]{:S(2)}) collective-permute-start(bf16[2,256,128]{2,1,0:T(8,128)(2,1)S(1)} %get-tuple-element.35), channel_id=1, source_target_pairs={{0,16},{16,32},{32,48},{48,0},{64,112},{80,64},{96,80},{112,96},{1... | collective-permute-start | bytes 393224 | tf_op jit(solution)/shard_map/ppermute | solution.py:33
  60.8 24.2 %copy-start.4 = (bf16[128,512]{1,0:T(8,128)(2,1)S(1)}, bf16[128,512]{1,0:T(8,128)(2,1)}, u32[]{:S(2)}) copy-start(bf16[128,512]{1,0:T(8,128)(2,1)} %param.8) | copy-start | bytes 393220
  60.8 5.1 %collective-permute-start.7 = (bf16[2,256,128]{2,1,0:T(8,128)(2,1)S(1)}, bf16[2,256,128]{2,1,0:T(8,128)(2,1)S(1)}, u32[]{:S(2)}, u32[]{:S(2)}) collective-permute-start(bf16[2,256,128]{2,1,0:T(8,128)(2,1)S(1)} %get-tuple-element.37), channel_id=1, source_target_pairs={{0,1},{1,2},{2,3},{3,0},{64,67},{65,64},{66,65},{67,66},{4,5},{5,6... | collective-permute-start | bytes 393224 | tf_op jit(solution)/shard_map/ppermute | solution.py:33
  62.6 12.5 %collective-permute-start.6 = (bf16[2,256,128]{2,1,0:T(8,128)(2,1)S(1)}, bf16[2,256,128]{2,1,0:T(8,128)(2,1)S(1)}, u32[]{:S(2)}, u32[]{:S(2)}) collective-permute-start(bf16[2,256,128]{2,1,0:T(8,128)(2,1)S(1)} %get-tuple-element.36), channel_id=1, source_target_pairs={{0,3},{1,0},{2,1},{3,2},{64,65},{65,66},{66,67},{67,64},{4,7},{5,4... | collective-permute-start | bytes 393224 | tf_op jit(solution)/shard_map/ppermute | solution.py:33
  62.6 5.8 %collective-permute-start.13 = (bf16[2,256,128]{2,1,0:T(8,128)(2,1)S(1)}, bf16[2,256,128]{2,1,0:T(8,128)(2,1)S(1)}, u32[]{:S(2)}, u32[]{:S(2)}) collective-permute-start(bf16[2,256,128]{2,1,0:T(8,128)(2,1)S(1)} %get-tuple-element.34), channel_id=1, source_target_pairs={{0,48},{16,0},{32,16},{48,32},{64,80},{80,96},{96,112},{112,64},{1... | collective-permute-start | bytes 393224 | tf_op jit(solution)/shard_map/ppermute | solution.py:33
  64.6 5.0 %collective-permute-start.15 = (bf16[2,256,128]{2,1,0:T(8,128)(2,1)S(1)}, bf16[2,256,128]{2,1,0:T(8,128)(2,1)S(1)}, u32[]{:S(2)}, u32[]{:S(2)}) collective-permute-start(bf16[2,256,128]{2,1,0:T(8,128)(2,1)S(1)} %fusion.11), channel_id=1, source_target_pairs={{0,16},{16,32},{32,48},{48,0},{64,112},{80,64},{96,80},{112,96},{1... | collective-permute-start | bytes 393224 | tf_op jit(solution)/shard_map/ppermute | solution.py:33
  65.9 9.2 %collective-permute-start.8 = (bf16[2,256,128]{2,1,0:T(8,128)(2,1)S(1)}, bf16[2,256,128]{2,1,0:T(8,128)(2,1)S(1)}, u32[]{:S(2)}, u32[]{:S(2)}) collective-permute-start(bf16[2,256,128]{2,1,0:T(8,128)(2,1)S(1)} %fusion.16), channel_id=1, source_target_pairs={{0,1},{1,2},{2,3},{3,0},{64,67},{65,64},{66,65},{67,66},{4,5},{5,6... | collective-permute-start | bytes 393224 | tf_op jit(solution)/shard_map/ppermute | solution.py:33
  69.6 6.8 %collective-permute-start.17 = (bf16[256,128]{1,0:T(8,128)(2,1)S(1)}, bf16[256,128]{1,0:T(8,128)(2,1)S(1)}, u32[]{:S(2)}, u32[]{:S(2)}) collective-permute-start(bf16[256,128]{1,0:T(8,128)(2,1)S(1)} %get-tuple-element.41), channel_id=1, source_target_pairs={{0,12},{4,0},{8,4},{12,8},{1,13},{5,1},{9,5},{13,9},{2,14},{6,2},{... | collective-permute-start | bytes 196616 | tf_op jit(solution)/shard_map/ppermute | solution.py:28
  75.1 4.1 %collective-permute-start.16 = (bf16[256,128]{1,0:T(8,128)(2,1)S(1)}, bf16[256,128]{1,0:T(8,128)(2,1)S(1)}, u32[]{:S(2)}, u32[]{:S(2)}) collective-permute-start(bf16[256,128]{1,0:T(8,128)(2,1)S(1)} %get-tuple-element.40), channel_id=1, source_target_pairs={{0,8},{4,12},{8,0},{12,4},{1,9},{5,13},{9,1},{13,5},{2,10},{6,14},... | collective-permute-start | bytes 196616 | tf_op jit(solution)/shard_map/ppermute | solution.py:28
  75.2 5.1 %collective-permute-start.9 = (bf16[256,128]{1,0:T(8,128)(2,1)S(1)}, bf16[256,128]{1,0:T(8,128)(2,1)S(1)}, u32[]{:S(2)}, u32[]{:S(2)}) collective-permute-start(bf16[256,128]{1,0:T(8,128)(2,1)S(1)} %fusion.23), channel_id=1, source_target_pairs={{0,4},{4,8},{8,12},{12,0},{1,5},{5,9},{9,13},{13,1},{2,6},{6,10},{... | collective-permute-start | bytes 196616 | tf_op jit(solution)/shard_map/ppermute | solution.py:28
  80.4 7.7 %collective-permute-start.18 = (bf16[2,128,128]{2,1,0:T(8,128)(2,1)S(1)}, bf16[2,128,128]{2,1,0:T(8,128)(2,1)S(1)}, u32[]{:S(2)}, u32[]{:S(2)}) collective-permute-start(bf16[2,128,128]{2,1,0:T(8,128)(2,1)S(1)} %add_convert_fusion.4), channel_id=1, source_target_pairs={{0,128},{128,0},{1,129},{129,1},{2,130},{130,2},{3,131},{131,3},{4... | collective-permute-start | bytes 196616 | tf_op jit(solution)/shard_map/ppermute | solution.py:37
  88.2 7.1 %collective-permute-start.19 = (f32[2,128,128]{2,1,0:T(8,128)S(1)}, f32[2,128,128]{2,1,0:T(8,128)S(1)}, u32[]{:S(2)}, u32[]{:S(2)}) collective-permute-start(f32[2,128,128]{2,1,0:T(8,128)S(1)} %get-tuple-element.39), channel_id=1, source_target_pairs={{0,64},{64,0},{1,65},{65,1},{2,66},{66,2},{3,67},{67,3},{4,68},{68... | collective-permute-start | bytes 393224 | tf_op jit(solution)/shard_map/ppermute | solution.py:37

commit v3 on v2

--- a/solution.py
+++ b/solution.py
@@ -163,10 +163,8 @@
 
 
 def ring_sum(terms, axis):
-    far = onward(narrow(terms[2]), axis, 1)
-    back = onward(narrow(terms[3]), axis, -1)
-    front = onward(narrow(terms[1] + wide(far)), axis, 1)
-    return terms[0] + wide(back) + wide(front)
+    others = [onward(terms[s], axis, s) for s in (2, 1, 3)]
+    return wide(terms[0]) + sum(wide(other) for other in others)
 
 
 def per_device(tokens, keys_grad, norm_gain, weight, momentum):
@@ -197,7 +195,7 @@
 
     send, own = later_terms((0,), place, held, grads, gain)
     received = swap(send, "core")
-    sums = [wide(own[0, c]) + wide(received[0, c]) + wide(back[c]) + wide(front[c]) for c in (0, 1)]
+    sums = [narrow(wide(own[0, c]) + wide(received[0, c]) + wide(back[c]) + wide(front[c])) for c in (0, 1)]
 
     sums = [ring_sum(sums[0], "y"), ring_sum(sums[1], "x")]
     lines = [sums[0][0], sums[0][1], sums[1][0], sums[1][1]]

time: 96.4 us -> 92.9 us (0.964)
  starting transfers between devices: 35 us -> 31.5 us
    another operation x2 -> x1, other arithmetic: 2.22 us -> 0.08 us
    convert_element_type x7 -> x6, other arithmetic: 3.17 us -> 5.23 us  [narrow(): return array.astype(jnp.bfloat16)]
    ppermute x5, starting transfers between devices: 14.1 us -> 12.3 us  [swap(): return lax.ppermute(block, axis, [(0, 1), (1, 0)])]
    ppermute x5, waiting for transfers between devices: 8.41 us -> 6.85 us  [swap(): return lax.ppermute(block, axis, [(0, 1), (1, 0)])]
    ppermute x12, waiting for transfers between devices: 19.6 us -> 21.2 us  [onward(): return lax.ppermute(block, ('core', axis), route)]
    ppermute x12, starting transfers between devices: 15 us -> 13.9 us  [onward(): return lax.ppermute(block, ('core', axis), route)]
  transfers between devices with their start and end apart: 20 -> 20, of which waited for: 14 -> 12; matrix products, arithmetic and copies ran while one was open for 4% -> 5% of each run, Pallas kernels for 3% -> 4%
where the time goes in v3:
time: 92.9 us; the launch traced here: 92.7 us
  waiting for transfers between devices  32.7 us (35%)
  starting transfers between devices  31.5 us (34%)
  Pallas kernels  18.2 us (20%)
  other arithmetic  5.66 us (6%)
  local copies, waits for them, and re-layouts  3.75 us (4%)
    ppermute x12, waiting for transfers between devices, onward(): return lax.ppermute(block, ('core', axis), route)  21.2 us
    pallas_call x3, Pallas kernels, terms(): pl.pallas_call(kernel, out_shape=outs, in_specs=[in_smem, pl.BlockSpec(me...  18.2 us
    ppermute x12, starting transfers between devices, onward(): return lax.ppermute(block, ('core', axis), route)  13.9 us
    ppermute x5, starting transfers between devices, swap(): return lax.ppermute(block, axis, [(0, 1), (1, 0)])  12.3 us
    ppermute x5, waiting for transfers between devices, swap(): return lax.ppermute(block, axis, [(0, 1), (1, 0)])  6.85 us
    ppermute x3, starting transfers between devices, shift(): lax.ppermute(block, axis, [(i, (i + step) % count) for i in range(count)])  5.32 us
    convert_element_type x6, other arithmetic, narrow(): return array.astype(jnp.bfloat16)  5.23 us
    ppermute x3, waiting for transfers between devices, shift(): lax.ppermute(block, axis, [(i, (i + step) % count) for i in range(count)])  4.63 us
  transfers between devices with their start and end apart: 20, of which 12 were waited for; matrix products, arithmetic and copies ran while one was open for 5% of the time, Pallas kernels for 4%

profile of v3, /device:TPU:1, one launch (start us, length us, event | category | flops | bytes accessed | tf_op | source)
XLA Modules:
  0.0 92.7 jit_solution(17967522515872972242)
XLA Ops:
  0.7 1.1 %copy-done = bf16[1,640,512]{2,1,0:T(8,128)(2,1)S(1)} copy-done((bf16[1,640,512]{2,1,0:T(8,128)(2,1)S(1)}, bf16[1,640,512]{2,1,0:T(8,128)(2,1)}, u32[]{:S(2)}) %copy-start) | copy-done | bytes 655384
  1.8 0.8 copy-done.1
  2.6 9.0 %shard_map.68 = (bf16[1,2,4,2,256,128]{5,4,3,2,1,0:T(8,128)(2,1)S(1)}, bf16[1,2,4,2,256,128]{5,4,3,2,1,0:T(8,128)(2,1)S(1)}, bf16[640,8192]{1,0:T(8,128)(2,1)S(1)}, bf16[512,640]{1,0:T(8,128)(2,1)S(1)}) custom-call(s32[4]{0:T(128)S(1)} %pad_add_fusion.place, bf16[640,8192]{1,0:T(8,128)(2,1)} %bitcast.101, bf16[640,512]{1,0:T(8,128)(2,1)S(1)} %bitcast.97, ...), custom_call_target="tpu_custom_call" | custom-call | flops 1342177280 | bytes 1048576 | tf_op jit(solution)/shard_map/pallas_call | solution.py:141
  11.5 6.0 %shard_map.70 = (bf16[2,2,4,2,256,128]{5,4,3,2,1,0:T(8,128)(2,1)S(1)}, bf16[2,2,4,2,256,128]{5,4,3,2,1,0:T(8,128)(2,1)S(1)}) custom-call(s32[4]{0:T(128)S(1)} %pad_add_fusion.place, bf16[640,8192]{1,0:T(8,128)(2,1)S(1)} %get-tuple-element.10.tokens, bf16[512,640]{1,0:T(8,128)(2,1)S(1)} %get-tuple-element.11.grads, f32[1,8192]{1,0:T(1,128)S(1)} %bitcast.99), custom_call_target="tpu_custom_call" | custom-call | flops 2684354560 | bytes 1048576 | tf_op jit(solution)/shard_map/pallas_call | solution.py:141
  17.5 3.3 %collective-permute-start.1 = (bf16[2,2,4,2,256,128]{5,4,3,2,1,0:T(8,128)(2,1)S(1)}, bf16[2,2,4,2,256,128]{5,4,3,2,1,0:T(8,128)(2,1)S(1)}, u32[]{:S(2)}, u32[]{:S(2)}) collective-permute-start(bf16[2,2,4,2,256,128]{5,4,3,2,1,0:T(8,128)(2,1)S(1)} %get-tuple-element.15), channel_id=1, source_target_pairs={{0,64},{64,0},{1,65},{65,1},{2,66},{66,2},{3,67},{67,3},{4,68},{68... | collective-permute-start | bytes 6291464 | tf_op jit(solution)/shard_map/ppermute | solution.py:37
  20.9 5.2 %collective-permute-done.3 = bf16[1,2,4,2,256,128]{5,4,3,2,1,0:T(8,128)(2,1)S(1)} collective-permute-done((bf16[1,2,4,2,256,128]{5,4,3,2,1,0:T(8,128)(2,1)S(1)}, bf16[1,2,4,2,256,128]{5,4,3,2,1,0:T(8,128)(2,1)S(1)}, u32[]{:S(2)}, u32[]{:S(2)}) %collective-permute-start.3) | collective-permute-done | bytes 1048608 | tf_op jit(solution)/shard_map/ppermute | solution.py:37
  26.4 1.1 %collective-permute-start.11 = (bf16[4,2,256,128]{3,2,1,0:T(8,128)(2,1)S(1)}, bf16[4,2,256,128]{3,2,1,0:T(8,128)(2,1)S(1)}, u32[]{:S(2)}, u32[]{:S(2)}) collective-permute-start(bf16[4,2,256,128]{3,2,1,0:T(8,128)(2,1)S(1)} %get-tuple-element.28), channel_id=1, source_target_pairs={{0,1},{1,2},{2,3},{3,0},{64,67},{65,64},{66,65},{67,66},{4,5},{5,6... | collective-permute-start | bytes 1572872 | tf_op jit(solution)/shard_map/ppermute | solution.py:33
  27.5 2.5 %collective-permute-start.4 = (bf16[4,2,256,128]{3,2,1,0:T(8,128)(2,1)S(1)}, bf16[4,2,256,128]{3,2,1,0:T(8,128)(2,1)S(1)}, u32[]{:S(2)}, u32[]{:S(2)}) collective-permute-start(bf16[4,2,256,128]{3,2,1,0:T(8,128)(2,1)S(1)} %get-tuple-element.29), channel_id=1, source_target_pairs={{0,16},{16,32},{32,48},{48,0},{64,112},{80,64},{96,80},{112,96},{1... | collective-permute-start | bytes 1572872 | tf_op jit(solution)/shard_map/ppermute | solution.py:33
  29.9 3.3 %shard_map.69 = (bf16[1,2,4,2,256,128]{5,4,3,2,1,0:T(8,128)(2,1)S(1)}, bf16[1,2,4,2,256,128]{5,4,3,2,1,0:T(8,128)(2,1)S(1)}) custom-call(s32[4]{0:T(128)S(1)} %pad_add_fusion.place, bf16[640,8192]{1,0:T(8,128)(2,1)S(1)} %get-tuple-element.10.tokens, bf16[512,640]{1,0:T(8,128)(2,1)S(1)} %get-tuple-element.11.grads, f32[1,8192]{1,0:T(1,128)S(1)} %bitcast.100), custom_call_target="tpu_custom_call" | custom-call | flops 1342177280 | bytes 1048576 | tf_op jit(solution)/shard_map/pallas_call | solution.py:141
  33.3 1.5 %collective-permute-done.11 = bf16[4,2,256,128]{3,2,1,0:T(8,128)(2,1)S(1)} collective-permute-done((bf16[4,2,256,128]{3,2,1,0:T(8,128)(2,1)S(1)}, bf16[4,2,256,128]{3,2,1,0:T(8,128)(2,1)S(1)}, u32[]{:S(2)}, u32[]{:S(2)}) %collective-permute-start.11) | collective-permute-done | bytes 524320 | tf_op jit(solution)/shard_map/ppermute | solution.py:33
  34.8 1.3 %collective-permute-done.4 = bf16[4,2,256,128]{3,2,1,0:T(8,128)(2,1)S(1)} collective-permute-done((bf16[4,2,256,128]{3,2,1,0:T(8,128)(2,1)S(1)}, bf16[4,2,256,128]{3,2,1,0:T(8,128)(2,1)S(1)}, u32[]{:S(2)}, u32[]{:S(2)}) %collective-permute-start.4) | collective-permute-done | bytes 524320 | tf_op jit(solution)/shard_map/ppermute | solution.py:33
  36.1 1.4 %fusion = (bf16[4,2,256,128]{3,2,1,0:T(8,128)(2,1)}, bf16[4,2,256,128]{3,2,1,0:T(8,128)(2,1)}) fusion(bf16[4,2,256,128]{3,2,1,0:T(8,128)(2,1)S(1)} %collective-permute-done.11, bf16[2,2,4,2,256,128]{5,4,3,2,1,0:T(8,128)(2,1)S(1)} %collective-permute-done.1, bf16[2,2,4,2,256,128]{5,4,3,2,1,0:T(8,128)(2,1)S(1)} %get-tuple-element.14, ...), kind=kLoop, calls=%fused_computation.1 | loop fusion | flops 3145728 | bytes 4194304 | tf_op jit(solution)/shard_map/convert_element_type | solution.py:45
  37.5 0.9 %collective-permute-start.12 = (bf16[4,2,256,128]{3,2,1,0:T(8,128)(2,1)}, bf16[4,2,256,128]{3,2,1,0:T(8,128)(2,1)}, u32[]{:S(2)}, u32[]{:S(2)}) collective-permute-start(bf16[4,2,256,128]{3,2,1,0:T(8,128)(2,1)} %get-tuple-element.24), channel_id=1, source_target_pairs={{0,1},{1,2},{2,3},{3,0},{64,67},{65,64},{66,65},{67,66},{4,5},{5,6... | collective-permute-start | bytes 1572872 | tf_op jit(solution)/shard_map/ppermute | solution.py:33
  38.4 1.3 %fusion.8 = (bf16[4,2,256,128]{3,2,1,0:T(8,128)(2,1)}, bf16[4,2,256,128]{3,2,1,0:T(8,128)(2,1)}) fusion(bf16[2,2,4,2,256,128]{5,4,3,2,1,0:T(8,128)(2,1)S(1)} %collective-permute-done.1, bf16[2,2,4,2,256,128]{5,4,3,2,1,0:T(8,128)(2,1)S(1)} %get-tuple-element.14), kind=kLoop, calls=%fused_computation.16 | loop fusion | flops 2097152 | bytes 3145728 | tf_op jit(solution)/shard_map/convert_element_type | solution.py:45
  39.7 0.5 collective-permute-start.10
  40.2 3.1 %collective-permute-start.5 = (bf16[4,2,256,128]{3,2,1,0:T(8,128)(2,1)}, bf16[4,2,256,128]{3,2,1,0:T(8,128)(2,1)}, u32[]{:S(2)}, u32[]{:S(2)}) collective-permute-start(bf16[4,2,256,128]{3,2,1,0:T(8,128)(2,1)} %get-tuple-element.25), channel_id=1, source_target_pairs={{0,16},{16,32},{32,48},{48,0},{64,112},{80,64},{96,80},{112,96},{1... | collective-permute-start | bytes 1572872 | tf_op jit(solution)/shard_map/ppermute | solution.py:33
  43.5 4.0 %collective-permute-done.12 = bf16[4,2,256,128]{3,2,1,0:T(8,128)(2,1)} collective-permute-done((bf16[4,2,256,128]{3,2,1,0:T(8,128)(2,1)}, bf16[4,2,256,128]{3,2,1,0:T(8,128)(2,1)}, u32[]{:S(2)}, u32[]{:S(2)}) %collective-permute-start.12) | collective-permute-done | bytes 524320 | tf_op jit(solution)/shard_map/ppermute | solution.py:33
  47.5 7.2 %collective-permute-done.10 = bf16[4,2,256,128]{3,2,1,0:T(8,128)(2,1)} collective-permute-done((bf16[4,2,256,128]{3,2,1,0:T(8,128)(2,1)}, bf16[4,2,256,128]{3,2,1,0:T(8,128)(2,1)}, u32[]{:S(2)}, u32[]{:S(2)}) %collective-permute-start.10) | collective-permute-done | bytes 524320 | tf_op jit(solution)/shard_map/ppermute | solution.py:33
  54.7 3.8 %collective-permute-done.2 = bf16[4,2,256,128]{3,2,1,0:T(8,128)(2,1)} collective-permute-done((bf16[4,2,256,128]{3,2,1,0:T(8,128)(2,1)}, bf16[4,2,256,128]{3,2,1,0:T(8,128)(2,1)}, u32[]{:S(2)}, u32[]{:S(2)}) %collective-permute-start.2) | collective-permute-done | bytes 524320 | tf_op jit(solution)/shard_map/ppermute | solution.py:33
  58.5 2.1 %fusion.2 = (bf16[4,2,256,128]{3,2,1,0:T(8,128)(2,1)S(1)}, bf16[4,2,256,128]{3,2,1,0:T(8,128)(2,1)S(1)}) fusion(bf16[4,2,256,128]{3,2,1,0:T(8,128)(2,1)} %collective-permute-done.12, bf16[4,2,256,128]{3,2,1,0:T(8,128)(2,1)} %collective-permute-done.10, bf16[1,2,4,2,256,128]{5,4,3,2,1,0:T(8,128)(2,1)S(1)} %collective-permute-done, ...), kind=kLoop, calls=%fused_computation.4 | loop fusion | flops 4194304 | bytes 5242880 | tf_op jit(solution)/shard_map/convert_element_type | solution.py:45
  60.8 2.7 %collective-permute-start.14 = (bf16[2,256,128]{2,1,0:T(8,128)(2,1)S(1)}, bf16[2,256,128]{2,1,0:T(8,128)(2,1)S(1)}, u32[]{:S(2)}, u32[]{:S(2)}) collective-permute-start(bf16[2,256,128]{2,1,0:T(8,128)(2,1)S(1)} %get-tuple-element.32), channel_id=1, source_target_pairs={{0,16},{16,32},{32,48},{48,0},{64,112},{80,64},{96,80},{112,96},{1... | collective-permute-start | bytes 393224 | tf_op jit(solution)/shard_map/ppermute | solution.py:33
  63.7 2.5 %collective-permute-start.7 = (bf16[2,256,128]{2,1,0:T(8,128)(2,1)S(1)}, bf16[2,256,128]{2,1,0:T(8,128)(2,1)S(1)}, u32[]{:S(2)}, u32[]{:S(2)}) collective-permute-start(bf16[2,256,128]{2,1,0:T(8,128)(2,1)S(1)} %get-tuple-element.35), channel_id=1, source_target_pairs={{0,1},{1,2},{2,3},{3,0},{64,67},{65,64},{66,65},{67,66},{4,5},{5,6... | collective-permute-start | bytes 393224 | tf_op jit(solution)/shard_map/ppermute | solution.py:33
  66.4 3.4 %collective-permute-done.13 = bf16[2,256,128]{2,1,0:T(8,128)(2,1)S(1)} collective-permute-done((bf16[2,256,128]{2,1,0:T(8,128)(2,1)S(1)}, bf16[2,256,128]{2,1,0:T(8,128)(2,1)S(1)}, u32[]{:S(2)}, u32[]{:S(2)}) %collective-permute-start.13) | collective-permute-done | bytes 131104 | tf_op jit(solution)/shard_map/ppermute | solution.py:33
  70.0 4.9 %collective-permute-start.17 = (bf16[256,128]{1,0:T(8,128)(2,1)S(1)}, bf16[256,128]{1,0:T(8,128)(2,1)S(1)}, u32[]{:S(2)}, u32[]{:S(2)}) collective-permute-start(bf16[256,128]{1,0:T(8,128)(2,1)S(1)} %get-tuple-element.39), channel_id=1, source_target_pairs={{0,12},{4,0},{8,4},{12,8},{1,13},{5,1},{9,5},{13,9},{2,14},{6,2},{... | collective-permute-start | bytes 196616 | tf_op jit(solution)/shard_map/ppermute | solution.py:28
  75.4 0.8 collective-permute-done.17
  76.2 3.1 %collective-permute-done.16 = bf16[256,128]{1,0:T(8,128)(2,1)S(1)} collective-permute-done((bf16[256,128]{1,0:T(8,128)(2,1)S(1)}, bf16[256,128]{1,0:T(8,128)(2,1)S(1)}, u32[]{:S(2)}, u32[]{:S(2)}) %collective-permute-start.16) | collective-permute-done | bytes 65568 | tf_op jit(solution)/shard_map/ppermute | solution.py:28
  79.3 0.7 collective-permute-done.9
  80.2 5.5 %collective-permute-start.18 = (bf16[2,128,128]{2,1,0:T(8,128)(2,1)S(1)}, bf16[2,128,128]{2,1,0:T(8,128)(2,1)S(1)}, u32[]{:S(2)}, u32[]{:S(2)}) collective-permute-start(bf16[2,128,128]{2,1,0:T(8,128)(2,1)S(1)} %add_convert_fusion.4), channel_id=1, source_target_pairs={{0,128},{128,0},{1,129},{129,1},{2,130},{130,2},{3,131},{131,3},{4... | collective-permute-start | bytes 196616 | tf_op jit(solution)/shard_map/ppermute | solution.py:37
  86.0 1.4 %collective-permute-done.18 = bf16[2,128,128]{2,1,0:T(8,128)(2,1)S(1)} collective-permute-done((bf16[2,128,128]{2,1,0:T(8,128)(2,1)S(1)}, bf16[2,128,128]{2,1,0:T(8,128)(2,1)S(1)}, u32[]{:S(2)}, u32[]{:S(2)}) %collective-permute-start.18) | collective-permute-done | bytes 65568 | tf_op jit(solution)/shard_map/ppermute | solution.py:37
  87.5 3.3 %collective-permute-start.19 = (f32[2,128,128]{2,1,0:T(8,128)S(1)}, f32[2,128,128]{2,1,0:T(8,128)S(1)}, u32[]{:S(2)}, u32[]{:S(2)}) collective-permute-start(f32[2,128,128]{2,1,0:T(8,128)S(1)} %get-tuple-element.37), channel_id=1, source_target_pairs={{0,64},{64,0},{1,65},{65,1},{2,66},{66,2},{3,67},{67,3},{4,68},{68... | collective-permute-start | bytes 393224 | tf_op jit(solution)/shard_map/ppermute | solution.py:37
  90.8 0.7 copy.15
  91.9 0.8 copy.14
  (47 shorter events, 2.7 us)
Async XLA Ops:
  0.7 1.1 %copy-start = (bf16[1,640,512]{2,1,0:T(8,128)(2,1)S(1)}, bf16[1,640,512]{2,1,0:T(8,128)(2,1)}, u32[]{:S(2)}) copy-start(bf16[1,640,512]{2,1,0:T(8,128)(2,1)} %param.6) | copy-start | bytes 1966084
  1.8 0.8 copy-start.1
  2.6 9.0 %copy-start.2 = (f32[8192]{0:T(1024)S(1)}, f32[8192]{0:T(1024)}, u32[]{:S(2)}) copy-start(f32[8192]{0:T(1024)} %param.7) | copy-start | bytes 98308
  17.5 18.6 %collective-permute-start.1 = (bf16[2,2,4,2,256,128]{5,4,3,2,1,0:T(8,128)(2,1)S(1)}, bf16[2,2,4,2,256,128]{5,4,3,2,1,0:T(8,128)(2,1)S(1)}, u32[]{:S(2)}, u32[]{:S(2)}) collective-permute-start(bf16[2,2,4,2,256,128]{5,4,3,2,1,0:T(8,128)(2,1)S(1)} %get-tuple-element.15), channel_id=1, source_target_pairs={{0,64},{64,0},{1,65},{65,1},{2,66},{66,2},{3,67},{67,3},{4,68},{68... | collective-permute-start | bytes 6291464 | tf_op jit(solution)/shard_map/ppermute | solution.py:37
  20.8 5.3 %collective-permute-start.3 = (bf16[1,2,4,2,256,128]{5,4,3,2,1,0:T(8,128)(2,1)S(1)}, bf16[1,2,4,2,256,128]{5,4,3,2,1,0:T(8,128)(2,1)S(1)}, u32[]{:S(2)}, u32[]{:S(2)}) collective-permute-start(bf16[1,2,4,2,256,128]{5,4,3,2,1,0:T(8,128)(2,1)S(1)} %get-tuple-element.17), channel_id=1, source_target_pairs={{0,64},{64,0},{1,65},{65,1},{2,66},{66,2},{3,67},{67,3},{4,68},{68... | collective-permute-start | bytes 3145736 | tf_op jit(solution)/shard_map/ppermute | solution.py:37
  26.4 8.4 %collective-permute-start.11 = (bf16[4,2,256,128]{3,2,1,0:T(8,128)(2,1)S(1)}, bf16[4,2,256,128]{3,2,1,0:T(8,128)(2,1)S(1)}, u32[]{:S(2)}, u32[]{:S(2)}) collective-permute-start(bf16[4,2,256,128]{3,2,1,0:T(8,128)(2,1)S(1)} %get-tuple-element.28), channel_id=1, source_target_pairs={{0,1},{1,2},{2,3},{3,0},{64,67},{65,64},{66,65},{67,66},{4,5},{5,6... | collective-permute-start | bytes 1572872 | tf_op jit(solution)/shard_map/ppermute | solution.py:33
  27.5 8.6 %collective-permute-start.4 = (bf16[4,2,256,128]{3,2,1,0:T(8,128)(2,1)S(1)}, bf16[4,2,256,128]{3,2,1,0:T(8,128)(2,1)S(1)}, u32[]{:S(2)}, u32[]{:S(2)}) collective-permute-start(bf16[4,2,256,128]{3,2,1,0:T(8,128)(2,1)S(1)} %get-tuple-element.29), channel_id=1, source_target_pairs={{0,16},{16,32},{32,48},{48,0},{64,112},{80,64},{96,80},{112,96},{1... | collective-permute-start | bytes 1572872 | tf_op jit(solution)/shard_map/ppermute | solution.py:33
  33.2 10.3 %collective-permute-start = (bf16[1,2,4,2,256,128]{5,4,3,2,1,0:T(8,128)(2,1)S(1)}, bf16[1,2,4,2,256,128]{5,4,3,2,1,0:T(8,128)(2,1)S(1)}, u32[]{:S(2)}, u32[]{:S(2)}) collective-permute-start(bf16[1,2,4,2,256,128]{5,4,3,2,1,0:T(8,128)(2,1)S(1)} %get-tuple-element.13), channel_id=1, source_target_pairs={{0,64},{64,0},{1,65},{65,1},{2,66},{66,2},{3,67},{67,3},{4,68},{68... | collective-permute-start | bytes 3145736 | tf_op jit(solution)/shard_map/ppermute | solution.py:37
  37.5 5.8 %copy-start.3 = (f32[128,128]{1,0:T(8,128)S(1)}, f32[128,128]{1,0:T(8,128)}, u32[]{:S(2)}) copy-start(f32[128,128]{1,0:T(8,128)} %param.9) | copy-start | bytes 196612
  37.5 10.0 %collective-permute-start.12 = (bf16[4,2,256,128]{3,2,1,0:T(8,128)(2,1)}, bf16[4,2,256,128]{3,2,1,0:T(8,128)(2,1)}, u32[]{:S(2)}, u32[]{:S(2)}) collective-permute-start(bf16[4,2,256,128]{3,2,1,0:T(8,128)(2,1)} %get-tuple-element.24), channel_id=1, source_target_pairs={{0,1},{1,2},{2,3},{3,0},{64,67},{65,64},{66,65},{67,66},{4,5},{5,6... | collective-permute-start | bytes 1572872 | tf_op jit(solution)/shard_map/ppermute | solution.py:33
  39.7 15.0 %collective-permute-start.10 = (bf16[4,2,256,128]{3,2,1,0:T(8,128)(2,1)}, bf16[4,2,256,128]{3,2,1,0:T(8,128)(2,1)}, u32[]{:S(2)}, u32[]{:S(2)}) collective-permute-start(bf16[4,2,256,128]{3,2,1,0:T(8,128)(2,1)} %get-tuple-element.22), channel_id=1, source_target_pairs={{0,3},{1,0},{2,1},{3,2},{64,65},{65,66},{66,67},{67,64},{4,7},{5,4... | collective-permute-start | bytes 1572872 | tf_op jit(solution)/shard_map/ppermute | solution.py:33
  40.2 14.4 %collective-permute-start.5 = (bf16[4,2,256,128]{3,2,1,0:T(8,128)(2,1)}, bf16[4,2,256,128]{3,2,1,0:T(8,128)(2,1)}, u32[]{:S(2)}, u32[]{:S(2)}) collective-permute-start(bf16[4,2,256,128]{3,2,1,0:T(8,128)(2,1)} %get-tuple-element.25), channel_id=1, source_target_pairs={{0,16},{16,32},{32,48},{48,0},{64,112},{80,64},{96,80},{112,96},{1... | collective-permute-start | bytes 1572872 | tf_op jit(solution)/shard_map/ppermute | solution.py:33
  43.3 15.1 %collective-permute-start.2 = (bf16[4,2,256,128]{3,2,1,0:T(8,128)(2,1)}, bf16[4,2,256,128]{3,2,1,0:T(8,128)(2,1)}, u32[]{:S(2)}, u32[]{:S(2)}) collective-permute-start(bf16[4,2,256,128]{3,2,1,0:T(8,128)(2,1)} %get-tuple-element.23), channel_id=1, source_target_pairs={{0,48},{16,0},{32,16},{48,32},{64,80},{80,96},{96,112},{112,64},{1... | collective-permute-start | bytes 1572872 | tf_op jit(solution)/shard_map/ppermute | solution.py:33
  60.6 25.2 %copy-start.4 = (bf16[128,512]{1,0:T(8,128)(2,1)S(1)}, bf16[128,512]{1,0:T(8,128)(2,1)}, u32[]{:S(2)}) copy-start(bf16[128,512]{1,0:T(8,128)(2,1)} %param.8) | copy-start | bytes 393220
  60.7 5.5 %collective-permute-start.15 = (bf16[2,256,128]{2,1,0:T(8,128)(2,1)S(1)}, bf16[2,256,128]{2,1,0:T(8,128)(2,1)S(1)}, u32[]{:S(2)}, u32[]{:S(2)}) collective-permute-start(bf16[2,256,128]{2,1,0:T(8,128)(2,1)S(1)} %get-tuple-element.31), channel_id=1, source_target_pairs={{0,48},{16,0},{32,16},{48,32},{64,80},{80,96},{96,112},{112,64},{1... | collective-permute-start | bytes 393224 | tf_op jit(solution)/shard_map/ppermute | solution.py:33
  60.8 5.7 %collective-permute-start.14 = (bf16[2,256,128]{2,1,0:T(8,128)(2,1)S(1)}, bf16[2,256,128]{2,1,0:T(8,128)(2,1)S(1)}, u32[]{:S(2)}, u32[]{:S(2)}) collective-permute-start(bf16[2,256,128]{2,1,0:T(8,128)(2,1)S(1)} %get-tuple-element.32), channel_id=1, source_target_pairs={{0,16},{16,32},{32,48},{48,0},{64,112},{80,64},{96,80},{112,96},{1... | collective-permute-start | bytes 393224 | tf_op jit(solution)/shard_map/ppermute | solution.py:33
  63.4 6.5 %collective-permute-start.13 = (bf16[2,256,128]{2,1,0:T(8,128)(2,1)S(1)}, bf16[2,256,128]{2,1,0:T(8,128)(2,1)S(1)}, u32[]{:S(2)}, u32[]{:S(2)}) collective-permute-start(bf16[2,256,128]{2,1,0:T(8,128)(2,1)S(1)} %get-tuple-element.30), channel_id=1, source_target_pairs={{0,32},{16,48},{32,0},{48,16},{64,96},{80,112},{96,64},{112,80},{1... | collective-permute-start | bytes 393224 | tf_op jit(solution)/shard_map/ppermute | solution.py:33
  63.5 11.4 %collective-permute-start.8 = (bf16[2,256,128]{2,1,0:T(8,128)(2,1)S(1)}, bf16[2,256,128]{2,1,0:T(8,128)(2,1)S(1)}, u32[]{:S(2)}, u32[]{:S(2)}) collective-permute-start(bf16[2,256,128]{2,1,0:T(8,128)(2,1)S(1)} %get-tuple-element.34), channel_id=1, source_target_pairs={{0,3},{1,0},{2,1},{3,2},{64,65},{65,66},{66,67},{67,64},{4,7},{5,4... | collective-permute-start | bytes 393224 | tf_op jit(solution)/shard_map/ppermute | solution.py:33
  63.7 11.2 %collective-permute-start.7 = (bf16[2,256,128]{2,1,0:T(8,128)(2,1)S(1)}, bf16[2,256,128]{2,1,0:T(8,128)(2,1)S(1)}, u32[]{:S(2)}, u32[]{:S(2)}) collective-permute-start(bf16[2,256,128]{2,1,0:T(8,128)(2,1)S(1)} %get-tuple-element.35), channel_id=1, source_target_pairs={{0,1},{1,2},{2,3},{3,0},{64,67},{65,64},{66,65},{67,66},{4,5},{5,6... | collective-permute-start | bytes 393224 | tf_op jit(solution)/shard_map/ppermute | solution.py:33
  66.2 8.7 %collective-permute-start.6 = (bf16[2,256,128]{2,1,0:T(8,128)(2,1)S(1)}, bf16[2,256,128]{2,1,0:T(8,128)(2,1)S(1)}, u32[]{:S(2)}, u32[]{:S(2)}) collective-permute-start(bf16[2,256,128]{2,1,0:T(8,128)(2,1)S(1)} %get-tuple-element.33), channel_id=1, source_target_pairs={{0,2},{1,3},{2,0},{3,1},{64,66},{65,67},{66,64},{67,65},{4,6},{5,7... | collective-permute-start | bytes 393224 | tf_op jit(solution)/shard_map/ppermute | solution.py:33
  70.0 6.2 %collective-permute-start.17 = (bf16[256,128]{1,0:T(8,128)(2,1)S(1)}, bf16[256,128]{1,0:T(8,128)(2,1)S(1)}, u32[]{:S(2)}, u32[]{:S(2)}) collective-permute-start(bf16[256,128]{1,0:T(8,128)(2,1)S(1)} %get-tuple-element.39), channel_id=1, source_target_pairs={{0,12},{4,0},{8,4},{12,8},{1,13},{5,1},{9,5},{13,9},{2,14},{6,2},{... | collective-permute-start | bytes 196616 | tf_op jit(solution)/shard_map/ppermute | solution.py:28
  74.9 4.5 %collective-permute-start.16 = (bf16[256,128]{1,0:T(8,128)(2,1)S(1)}, bf16[256,128]{1,0:T(8,128)(2,1)S(1)}, u32[]{:S(2)}, u32[]{:S(2)}) collective-permute-start(bf16[256,128]{1,0:T(8,128)(2,1)S(1)} %get-tuple-element.38), channel_id=1, source_target_pairs={{0,8},{4,12},{8,0},{12,4},{1,9},{5,13},{9,1},{13,5},{2,10},{6,14},... | collective-permute-start | bytes 196616 | tf_op jit(solution)/shard_map/ppermute | solution.py:28
  75.0 5.1 %collective-permute-start.9 = (bf16[256,128]{1,0:T(8,128)(2,1)S(1)}, bf16[256,128]{1,0:T(8,128)(2,1)S(1)}, u32[]{:S(2)}, u32[]{:S(2)}) collective-permute-start(bf16[256,128]{1,0:T(8,128)(2,1)S(1)} %fusion.17), channel_id=1, source_target_pairs={{0,4},{4,8},{8,12},{12,0},{1,5},{5,9},{9,13},{13,1},{2,6},{6,10},{... | collective-permute-start | bytes 196616 | tf_op jit(solution)/shard_map/ppermute | solution.py:28
  80.2 7.2 %collective-permute-start.18 = (bf16[2,128,128]{2,1,0:T(8,128)(2,1)S(1)}, bf16[2,128,128]{2,1,0:T(8,128)(2,1)S(1)}, u32[]{:S(2)}, u32[]{:S(2)}) collective-permute-start(bf16[2,128,128]{2,1,0:T(8,128)(2,1)S(1)} %add_convert_fusion.4), channel_id=1, source_target_pairs={{0,128},{128,0},{1,129},{129,1},{2,130},{130,2},{3,131},{131,3},{4... | collective-permute-start | bytes 196616 | tf_op jit(solution)/shard_map/ppermute | solution.py:37
  87.5 4.3 %collective-permute-start.19 = (f32[2,128,128]{2,1,0:T(8,128)S(1)}, f32[2,128,128]{2,1,0:T(8,128)S(1)}, u32[]{:S(2)}, u32[]{:S(2)}) collective-permute-start(f32[2,128,128]{2,1,0:T(8,128)S(1)} %get-tuple-element.37), channel_id=1, source_target_pairs={{0,64},{64,0},{1,65},{65,1},{2,66},{66,2},{3,67},{67,3},{4,68},{68... | collective-permute-start | bytes 393224 | tf_op jit(solution)/shard_map/ppermute | solution.py:37

commit v4 on v3

--- a/solution.py
+++ b/solution.py
@@ -46,16 +46,18 @@
 
 
 class Tiles:
-    def __init__(self, place, distances):
+    def __init__(self, place, distances, colours=(0, 1)):
         self.x, self.zl, self.y, self.core = (place[i] for i in range(4))
-        self.distances = distances
-        self.count = 4 * len(distances)
+        self.distances, self.colours = distances, colours
+        self.count = 2 * len(colours) * len(distances)
 
     def parts(self, turn):
-        return turn // 4, (turn // 2) % 2, turn % 2
+        count = len(self.colours)
+        return turn // (2 * count), (turn // 2) % count, turn % 2
 
     def column(self, turn, block):
         at, colour, low = self.parts(turn)
+        colour = colour + self.colours[0]
         distance = self.distances[0] + 2 * at
         along = jnp.where(colour == 0, self.x, self.y)
         along = lax.rem(along + 4 + jnp.where(self.core == 0, distance, -distance), 4)
@@ -76,7 +78,7 @@
             rows = full.shape[0] // 2
             for k in range(4):
                 block = (full[:, k * BLOCK : (k + 1) * BLOCK] * gain[:, columns[k]]).astype(jnp.bfloat16)
-                there = self.second(colour, k)
+                there = self.second(colour + self.colours[0], k)
                 send[len(self.distances) - 1 - at, colour, lax.rem(4 - there, 4), low] = block[:rows]
                 own[at, colour, there, low] = block[rows:]
             return carry
@@ -126,18 +128,18 @@
     Tiles(place, (2,)).products(held, grads, gain, send, own)
 
 
-def later_kernel(distances, place, tokens, grads, gain, send, own):
-    Tiles(place, distances).products(tokens, grads, gain, send, own)
-
-
-def terms(kernel, distances, outs, scratch, tokens_in, limit, place, tokens, grads, gain):
+def later_kernel(distances, colours, place, tokens, grads, gain, send, own):
+    Tiles(place, distances, colours).products(tokens, grads, gain, send, own)
+
+
+def terms(kernel, distances, colours, outs, scratch, tokens_in, limit, place, tokens, grads, gain):
     count = tokens.shape[0]
     cols = 4 * BLOCK
-    part = jax.ShapeDtypeStruct((len(distances), 2, 4, 2, cols // 2, BLOCK), jnp.bfloat16)
+    part = jax.ShapeDtypeStruct((len(distances), len(colours), 4, 2, cols // 2, BLOCK), jnp.bfloat16)
     in_vmem = pl.BlockSpec(memory_space=pltpu.VMEM)
     in_smem = pl.BlockSpec(memory_space=pltpu.SMEM)
     outs = [part, part] + outs
-    flops = 2 * len(distances) * 16 * BLOCK * count * cols
+    flops = 2 * len(distances) * len(colours) * 8 * BLOCK * count * cols
     return pl.pallas_call(
         kernel,
         out_shape=outs,
@@ -154,12 +156,12 @@
     outs = [jax.ShapeDtypeStruct(tokens.shape, jnp.bfloat16), jax.ShapeDtypeStruct((cols, count), jnp.bfloat16)]
     scratch = [pltpu.VMEM((count, cols), jnp.float32), pltpu.SemaphoreType.DMA((count // ROWS_AT_A_TIME,))]
     kernel = functools.partial(first_kernel, factor)
-    return terms(kernel, (2,), outs, scratch, pl.ANY, FIRST_LIMIT, place, tokens, keys, gain)
-
-
-def later_terms(distances, place, tokens, grads, gain):
-    kernel = functools.partial(later_kernel, distances)
-    return terms(kernel, distances, [], [], pltpu.VMEM, LATER_LIMIT, place, tokens, grads, gain)
+    return terms(kernel, (2,), (0, 1), outs, scratch, pl.ANY, FIRST_LIMIT, place, tokens, keys, gain)
+
+
+def later_terms(distances, colours, place, tokens, grads, gain):
+    kernel = functools.partial(later_kernel, distances, colours)
+    return terms(kernel, distances, colours, [], [], pltpu.VMEM, LATER_LIMIT, place, tokens, grads, gain)
 
 
 def ring_sum(terms, axis):
@@ -182,18 +184,18 @@
     for c in (0, 1):
         far[c] = onward(narrow(wide(own[0, c]) + wide(received[0, c])), axes[c], 1)
 
-    send, own = later_terms((1, 3), place, held, grads, gain)
-    received = swap(send, "core")
-    sides = [[wide(own[i, c]) + wide(received[i, c]) for i in (0, 1)] for c in (0, 1)]
-    back = [None, None]
+    sides, back = [None, None], [None, None]
     for c in (0, 1):
+        send, own = later_terms((1, 3), (c,), place, held, grads, gain)
+        received = swap(send, "core")
+        sides[c] = [wide(own[i, 0]) + wide(received[i, 0]) for i in (0, 1)]
         back[c] = onward(narrow(sides[c][1]), axes[c], -1)
 
     front = [None, None]
     for c in (0, 1):
         front[c] = onward(narrow(sides[c][0] + wide(far[c])), axes[c], 1)
 
-    send, own = later_terms((0,), place, held, grads, gain)
+    send, own = later_terms((0,), (0, 1), place, held, grads, gain)
     received = swap(send, "core")
     sums = [narrow(wide(own[0, c]) + wide(received[0, c]) + wide(back[c]) + wide(front[c])) for c in (0, 1)]
 

time: 92.9 us -> 88.3 us (0.950)
  waiting for transfers between devices: 32.7 us -> 19.5 us
  starting transfers between devices: 31.5 us -> 38.4 us
  other arithmetic: 5.66 us -> 6.83 us
    ppermute x12, waiting for transfers between devices: 21.2 us -> 13 us  [onward(): return lax.ppermute(block, ('core', axis), route)]
    ppermute x5 -> x6, waiting for transfers between devices: 6.85 us -> 2.02 us  [swap(): return lax.ppermute(block, axis, [(0, 1), (1, 0)])]
    ppermute x5 -> x6, starting transfers between devices: 12.3 us -> 15.9 us  [swap(): return lax.ppermute(block, axis, [(0, 1), (1, 0)])]
    ppermute x12, starting transfers between devices: 13.9 us -> 16.8 us  [onward(): return lax.ppermute(block, ('core', axis), route)]
    convert_element_type x6 -> x8, other arithmetic: 5.23 us -> 6.4 us  [narrow(): return array.astype(jnp.bfloat16)]
    pallas_call x3 -> x4, Pallas kernels: 18.2 us -> 18.7 us  [terms(): pl.pallas_call(kernel, out_shape=outs, in_specs=[in_smem, pl.BlockSpec(me...]
    unnamed x14 -> x12, local copies, waits for them, and re-layouts: 3.56 us -> 3.56 us
  transfers between devices with their start and end apart: 20 -> 21, of which waited for: 12 -> 9; matrix products, arithmetic and copies ran while one was open for 5% -> 6% of each run, Pallas kernels for 4% -> 11%
where the time goes in v4:
time: 88.3 us; the launch traced here: 88 us
  starting transfers between devices  38.4 us (43%)
  waiting for transfers between devices  19.5 us (22%)
  Pallas kernels  18.7 us (21%)
  other arithmetic  6.83 us (8%)
  local copies, waits for them, and re-layouts  3.75 us (4%)
    pallas_call x4, Pallas kernels, terms(): pl.pallas_call(kernel, out_shape=outs, in_specs=[in_smem, pl.BlockSpec(me...  18.7 us
    ppermute x12, starting transfers between devices, onward(): return lax.ppermute(block, ('core', axis), route)  16.8 us
    ppermute x6, starting transfers between devices, swap(): return lax.ppermute(block, axis, [(0, 1), (1, 0)])  15.9 us
    ppermute x12, waiting for transfers between devices, onward(): return lax.ppermute(block, ('core', axis), route)  13 us
    convert_element_type x8, other arithmetic, narrow(): return array.astype(jnp.bfloat16)  6.4 us
    ppermute x3, starting transfers between devices, shift(): lax.ppermute(block, axis, [(i, (i + step) % count) for i in range(count)])  5.69 us
    ppermute x3, waiting for transfers between devices, shift(): lax.ppermute(block, axis, [(i, (i + step) % count) for i in range(count)])  4.47 us
    unnamed x12, local copies, waits for them, and re-layouts  3.56 us
  transfers between devices with their start and end apart: 21, of which 9 were waited for; matrix products, arithmetic and copies ran while one was open for 6% of the time, Pallas kernels for 11%

profile of v4, /device:TPU:1, one launch (start us, length us, event | category | flops | bytes accessed | tf_op | source)
XLA Modules:
  0.0 88.0 jit_solution(11506862737532361510)
XLA Ops:
  0.7 1.1 %copy-done = bf16[1,640,512]{2,1,0:T(8,128)(2,1)S(1)} copy-done((bf16[1,640,512]{2,1,0:T(8,128)(2,1)S(1)}, bf16[1,640,512]{2,1,0:T(8,128)(2,1)}, u32[]{:S(2)}) %copy-start) | copy-done | bytes 655384
  1.8 0.8 copy-done.1
  2.6 8.9 %shard_map.68 = (bf16[1,2,4,2,256,128]{5,4,3,2,1,0:T(8,128)(2,1)S(1)}, bf16[1,2,4,2,256,128]{5,4,3,2,1,0:T(8,128)(2,1)S(1)}, bf16[640,8192]{1,0:T(8,128)(2,1)S(1)}, bf16[512,640]{1,0:T(8,128)(2,1)S(1)}) custom-call(s32[4]{0:T(128)S(1)} %pad_add_fusion.place, bf16[640,8192]{1,0:T(8,128)(2,1)} %bitcast.102, bf16[640,512]{1,0:T(8,128)(2,1)S(1)} %bitcast.97, ...), custom_call_target="tpu_custom_call" | custom-call | flops 1342177280 | bytes 1048576 | tf_op jit(solution)/shard_map/pallas_call | solution.py:143
  11.5 3.3 %collective-permute-start.3 = (bf16[1,2,4,2,256,128]{5,4,3,2,1,0:T(8,128)(2,1)S(1)}, bf16[1,2,4,2,256,128]{5,4,3,2,1,0:T(8,128)(2,1)S(1)}, u32[]{:S(2)}, u32[]{:S(2)}) collective-permute-start(bf16[1,2,4,2,256,128]{5,4,3,2,1,0:T(8,128)(2,1)S(1)} %get-tuple-element.19), channel_id=1, source_target_pairs={{0,64},{64,0},{1,65},{65,1},{2,66},{66,2},{3,67},{67,3},{4,68},{68... | collective-permute-start | bytes 3145736 | tf_op jit(solution)/shard_map/ppermute | solution.py:37
  14.8 3.2 %shard_map.71 = (bf16[2,1,4,2,256,128]{5,4,3,2,1,0:T(8,128)(2,1)S(1)}, bf16[2,1,4,2,256,128]{5,4,3,2,1,0:T(8,128)(2,1)S(1)}) custom-call(s32[4]{0:T(128)S(1)} %pad_add_fusion.place, bf16[640,8192]{1,0:T(8,128)(2,1)S(1)} %get-tuple-element.12.tokens, bf16[512,640]{1,0:T(8,128)(2,1)S(1)} %get-tuple-element.13.grads, f32[1,8192]{1,0:T(1,128)S(1)} %bitcast.99), custom_call_target="tpu_custom_call" | custom-call | flops 1342177280 | bytes 1048576 | tf_op jit(solution)/shard_map/pallas_call | solution.py:143
  18.2 3.3 %shard_map.70 = (bf16[2,1,4,2,256,128]{5,4,3,2,1,0:T(8,128)(2,1)S(1)}, bf16[2,1,4,2,256,128]{5,4,3,2,1,0:T(8,128)(2,1)S(1)}) custom-call(s32[4]{0:T(128)S(1)} %pad_add_fusion.place, bf16[640,8192]{1,0:T(8,128)(2,1)S(1)} %get-tuple-element.12.tokens, bf16[512,640]{1,0:T(8,128)(2,1)S(1)} %get-tuple-element.13.grads, f32[1,8192]{1,0:T(1,128)S(1)} %bitcast.100), custom_call_target="tpu_custom_call" | custom-call | flops 1342177280 | bytes 1048576 | tf_op jit(solution)/shard_map/pallas_call | solution.py:143
  22.0 3.2 %shard_map.69 = (bf16[1,2,4,2,256,128]{5,4,3,2,1,0:T(8,128)(2,1)S(1)}, bf16[1,2,4,2,256,128]{5,4,3,2,1,0:T(8,128)(2,1)S(1)}) custom-call(s32[4]{0:T(128)S(1)} %pad_add_fusion.place, bf16[640,8192]{1,0:T(8,128)(2,1)S(1)} %get-tuple-element.12.tokens, bf16[512,640]{1,0:T(8,128)(2,1)S(1)} %get-tuple-element.13.grads, f32[1,8192]{1,0:T(1,128)S(1)} %bitcast.101), custom_call_target="tpu_custom_call" | custom-call | flops 1342177280 | bytes 1048576 | tf_op jit(solution)/shard_map/pallas_call | solution.py:143
  25.7 1.1 %collective-permute-start.12 = (bf16[4,2,256,128]{3,2,1,0:T(8,128)(2,1)S(1)}, bf16[4,2,256,128]{3,2,1,0:T(8,128)(2,1)S(1)}, u32[]{:S(2)}, u32[]{:S(2)}) collective-permute-start(bf16[4,2,256,128]{3,2,1,0:T(8,128)(2,1)S(1)} %get-tuple-element.28), channel_id=1, source_target_pairs={{0,1},{1,2},{2,3},{3,0},{64,67},{65,64},{66,65},{67,66},{4,5},{5,6... | collective-permute-start | bytes 1572872 | tf_op jit(solution)/shard_map/ppermute | solution.py:33
  26.8 0.9 %fusion.8 = bf16[4,2,256,128]{3,2,1,0:T(8,128)(2,1)} fusion(bf16[2,1,4,2,256,128]{5,4,3,2,1,0:T(8,128)(2,1)S(1)} %collective-permute-done.10, bf16[2,1,4,2,256,128]{5,4,3,2,1,0:T(8,128)(2,1)S(1)} %get-tuple-element.20), kind=kLoop, calls=%fused_computation.16 | loop fusion | flops 1048576 | bytes 1572864 | tf_op jit(solution)/shard_map/convert_element_type | solution.py:45
  28.2 2.1 %collective-permute-start.4 = (bf16[4,2,256,128]{3,2,1,0:T(8,128)(2,1)S(1)}, bf16[4,2,256,128]{3,2,1,0:T(8,128)(2,1)S(1)}, u32[]{:S(2)}, u32[]{:S(2)}) collective-permute-start(bf16[4,2,256,128]{3,2,1,0:T(8,128)(2,1)S(1)} %get-tuple-element.29), channel_id=1, source_target_pairs={{0,16},{16,32},{32,48},{48,0},{64,112},{80,64},{96,80},{112,96},{1... | collective-permute-start | bytes 1572872 | tf_op jit(solution)/shard_map/ppermute | solution.py:33
  30.2 0.9 %fusion.6 = bf16[4,2,256,128]{3,2,1,0:T(8,128)(2,1)} fusion(bf16[2,1,4,2,256,128]{5,4,3,2,1,0:T(8,128)(2,1)S(1)} %collective-permute-done.1, bf16[2,1,4,2,256,128]{5,4,3,2,1,0:T(8,128)(2,1)S(1)} %get-tuple-element.16), kind=kLoop, calls=%fused_computation.14 | loop fusion | flops 1048576 | bytes 1572864 | tf_op jit(solution)/shard_map/convert_element_type | solution.py:45
  31.2 6.5 %collective-permute-done.12 = bf16[4,2,256,128]{3,2,1,0:T(8,128)(2,1)S(1)} collective-permute-done((bf16[4,2,256,128]{3,2,1,0:T(8,128)(2,1)S(1)}, bf16[4,2,256,128]{3,2,1,0:T(8,128)(2,1)S(1)}, u32[]{:S(2)}, u32[]{:S(2)}) %collective-permute-start.12) | collective-permute-done | bytes 524320 | tf_op jit(solution)/shard_map/ppermute | solution.py:33
  37.7 1.0 %fusion = bf16[4,2,256,128]{3,2,1,0:T(8,128)(2,1)} fusion(bf16[4,2,256,128]{3,2,1,0:T(8,128)(2,1)S(1)} %collective-permute-done.12, bf16[2,1,4,2,256,128]{5,4,3,2,1,0:T(8,128)(2,1)S(1)} %collective-permute-done.10, bf16[2,1,4,2,256,128]{5,4,3,2,1,0:T(8,128)(2,1)S(1)} %get-tuple-element.20), kind=kLoop, calls=%fused_computation.1 | loop fusion | flops 1572864 | bytes 2097152 | tf_op jit(solution)/shard_map/convert_element_type | solution.py:45
  39.1 1.0 %fusion.3 = bf16[4,2,256,128]{3,2,1,0:T(8,128)(2,1)} fusion(bf16[4,2,256,128]{3,2,1,0:T(8,128)(2,1)S(1)} %collective-permute-done.4, bf16[2,1,4,2,256,128]{5,4,3,2,1,0:T(8,128)(2,1)S(1)} %collective-permute-done.1, bf16[2,1,4,2,256,128]{5,4,3,2,1,0:T(8,128)(2,1)S(1)} %get-tuple-element.16), kind=kLoop, calls=%fused_computation.6 | loop fusion | flops 1572864 | bytes 2097152 | tf_op jit(solution)/shard_map/convert_element_type | solution.py:45
  40.1 4.2 %collective-permute-start.5 = (bf16[4,2,256,128]{3,2,1,0:T(8,128)(2,1)}, bf16[4,2,256,128]{3,2,1,0:T(8,128)(2,1)}, u32[]{:S(2)}, u32[]{:S(2)}) collective-permute-start(bf16[4,2,256,128]{3,2,1,0:T(8,128)(2,1)} %fusion.3), channel_id=1, source_target_pairs={{0,16},{16,32},{32,48},{48,0},{64,112},{80,64},{96,80},{112,96},{1... | collective-permute-start | bytes 1572872 | tf_op jit(solution)/shard_map/ppermute | solution.py:33
  44.4 1.4 %collective-permute-done.2 = bf16[4,2,256,128]{3,2,1,0:T(8,128)(2,1)} collective-permute-done((bf16[4,2,256,128]{3,2,1,0:T(8,128)(2,1)}, bf16[4,2,256,128]{3,2,1,0:T(8,128)(2,1)}, u32[]{:S(2)}, u32[]{:S(2)}) %collective-permute-start.2) | collective-permute-done | bytes 524320 | tf_op jit(solution)/shard_map/ppermute | solution.py:33
  45.8 1.5 %collective-permute-done.13 = bf16[4,2,256,128]{3,2,1,0:T(8,128)(2,1)} collective-permute-done((bf16[4,2,256,128]{3,2,1,0:T(8,128)(2,1)}, bf16[4,2,256,128]{3,2,1,0:T(8,128)(2,1)}, u32[]{:S(2)}, u32[]{:S(2)}) %collective-permute-start.13) | collective-permute-done | bytes 524320 | tf_op jit(solution)/shard_map/ppermute | solution.py:33
  47.3 3.3 %collective-permute-done.5 = bf16[4,2,256,128]{3,2,1,0:T(8,128)(2,1)} collective-permute-done((bf16[4,2,256,128]{3,2,1,0:T(8,128)(2,1)}, bf16[4,2,256,128]{3,2,1,0:T(8,128)(2,1)}, u32[]{:S(2)}, u32[]{:S(2)}) %collective-permute-start.5) | collective-permute-done | bytes 524320 | tf_op jit(solution)/shard_map/ppermute | solution.py:33
  50.7 2.1 %fusion.2 = (bf16[4,2,256,128]{3,2,1,0:T(8,128)(2,1)S(1)}, bf16[4,2,256,128]{3,2,1,0:T(8,128)(2,1)S(1)}) fusion(bf16[4,2,256,128]{3,2,1,0:T(8,128)(2,1)} %collective-permute-done.13, bf16[4,2,256,128]{3,2,1,0:T(8,128)(2,1)} %collective-permute-done.11, bf16[1,2,4,2,256,128]{5,4,3,2,1,0:T(8,128)(2,1)S(1)} %collective-permute-done, ...), kind=kLoop, calls=%fused_computation.4 | loop fusion | flops 4194304 | bytes 5242880 | tf_op jit(solution)/shard_map/convert_element_type | solution.py:45
  52.9 1.0 %collective-permute-start.16 = (bf16[2,256,128]{2,1,0:T(8,128)(2,1)S(1)}, bf16[2,256,128]{2,1,0:T(8,128)(2,1)S(1)}, u32[]{:S(2)}, u32[]{:S(2)}) collective-permute-start(bf16[2,256,128]{2,1,0:T(8,128)(2,1)S(1)} %get-tuple-element.31), channel_id=1, source_target_pairs={{0,48},{16,0},{32,16},{48,32},{64,80},{80,96},{96,112},{112,64},{1... | collective-permute-start | bytes 393224 | tf_op jit(solution)/shard_map/ppermute | solution.py:33
  53.9 2.5 %collective-permute-start.15 = (bf16[2,256,128]{2,1,0:T(8,128)(2,1)S(1)}, bf16[2,256,128]{2,1,0:T(8,128)(2,1)S(1)}, u32[]{:S(2)}, u32[]{:S(2)}) collective-permute-start(bf16[2,256,128]{2,1,0:T(8,128)(2,1)S(1)} %get-tuple-element.32), channel_id=1, source_target_pairs={{0,16},{16,32},{32,48},{48,0},{64,112},{80,64},{96,80},{112,96},{1... | collective-permute-start | bytes 393224 | tf_op jit(solution)/shard_map/ppermute | solution.py:33
  56.3 0.9 %collective-permute-start.14 = (bf16[2,256,128]{2,1,0:T(8,128)(2,1)S(1)}, bf16[2,256,128]{2,1,0:T(8,128)(2,1)S(1)}, u32[]{:S(2)}, u32[]{:S(2)}) collective-permute-start(bf16[2,256,128]{2,1,0:T(8,128)(2,1)S(1)} %get-tuple-element.30), channel_id=1, source_target_pairs={{0,32},{16,48},{32,0},{48,16},{64,96},{80,112},{96,64},{112,80},{1... | collective-permute-start | bytes 393224 | tf_op jit(solution)/shard_map/ppermute | solution.py:33
  57.4 3.0 %collective-permute-start.7 = (bf16[2,256,128]{2,1,0:T(8,128)(2,1)S(1)}, bf16[2,256,128]{2,1,0:T(8,128)(2,1)S(1)}, u32[]{:S(2)}, u32[]{:S(2)}) collective-permute-start(bf16[2,256,128]{2,1,0:T(8,128)(2,1)S(1)} %get-tuple-element.35), channel_id=1, source_target_pairs={{0,1},{1,2},{2,3},{3,0},{64,67},{65,64},{66,65},{67,66},{4,5},{5,6... | collective-permute-start | bytes 393224 | tf_op jit(solution)/shard_map/ppermute | solution.py:33
  60.4 1.1 %collective-permute-start.6 = (bf16[2,256,128]{2,1,0:T(8,128)(2,1)S(1)}, bf16[2,256,128]{2,1,0:T(8,128)(2,1)S(1)}, u32[]{:S(2)}, u32[]{:S(2)}) collective-permute-start(bf16[2,256,128]{2,1,0:T(8,128)(2,1)S(1)} %get-tuple-element.33), channel_id=1, source_target_pairs={{0,2},{1,3},{2,0},{3,1},{64,66},{65,67},{66,64},{67,65},{4,6},{5,7... | collective-permute-start | bytes 393224 | tf_op jit(solution)/shard_map/ppermute | solution.py:33
  61.8 4.4 %collective-permute-start.18 = (bf16[256,128]{1,0:T(8,128)(2,1)S(1)}, bf16[256,128]{1,0:T(8,128)(2,1)S(1)}, u32[]{:S(2)}, u32[]{:S(2)}) collective-permute-start(bf16[256,128]{1,0:T(8,128)(2,1)S(1)} %get-tuple-element.39), channel_id=1, source_target_pairs={{0,12},{4,0},{8,4},{12,8},{1,13},{5,1},{9,5},{13,9},{2,14},{6,2},{... | collective-permute-start | bytes 196616 | tf_op jit(solution)/shard_map/ppermute | solution.py:28
  66.3 1.3 %collective-permute-start.9 = (bf16[256,128]{1,0:T(8,128)(2,1)S(1)}, bf16[256,128]{1,0:T(8,128)(2,1)S(1)}, u32[]{:S(2)}, u32[]{:S(2)}) collective-permute-start(bf16[256,128]{1,0:T(8,128)(2,1)S(1)} %fusion.17), channel_id=1, source_target_pairs={{0,4},{4,8},{8,12},{12,0},{1,5},{5,9},{9,13},{13,1},{2,6},{6,10},{... | collective-permute-start | bytes 196616 | tf_op jit(solution)/shard_map/ppermute | solution.py:28
  67.6 2.9 %collective-permute-done.17 = bf16[256,128]{1,0:T(8,128)(2,1)S(1)} collective-permute-done((bf16[256,128]{1,0:T(8,128)(2,1)S(1)}, bf16[256,128]{1,0:T(8,128)(2,1)S(1)}, u32[]{:S(2)}, u32[]{:S(2)}) %collective-permute-start.17) | collective-permute-done | bytes 65568 | tf_op jit(solution)/shard_map/ppermute | solution.py:28
  70.5 1.6 %collective-permute-done.9 = bf16[256,128]{1,0:T(8,128)(2,1)S(1)} collective-permute-done((bf16[256,128]{1,0:T(8,128)(2,1)S(1)}, bf16[256,128]{1,0:T(8,128)(2,1)S(1)}, u32[]{:S(2)}, u32[]{:S(2)}) %collective-permute-start.9) | collective-permute-done | bytes 65568 | tf_op jit(solution)/shard_map/ppermute | solution.py:28
  72.2 6.3 %collective-permute-start.19 = (bf16[2,128,128]{2,1,0:T(8,128)(2,1)S(1)}, bf16[2,128,128]{2,1,0:T(8,128)(2,1)S(1)}, u32[]{:S(2)}, u32[]{:S(2)}) collective-permute-start(bf16[2,128,128]{2,1,0:T(8,128)(2,1)S(1)} %add_convert_fusion.4), channel_id=1, source_target_pairs={{0,128},{128,0},{1,129},{129,1},{2,130},{130,2},{3,131},{131,3},{4... | collective-permute-start | bytes 196616 | tf_op jit(solution)/shard_map/ppermute | solution.py:37
  78.7 1.8 %collective-permute-done.19 = bf16[2,128,128]{2,1,0:T(8,128)(2,1)S(1)} collective-permute-done((bf16[2,128,128]{2,1,0:T(8,128)(2,1)S(1)}, bf16[2,128,128]{2,1,0:T(8,128)(2,1)S(1)}, u32[]{:S(2)}, u32[]{:S(2)}) %collective-permute-start.19) | collective-permute-done | bytes 65568 | tf_op jit(solution)/shard_map/ppermute | solution.py:37
  80.6 5.5 %collective-permute-start.20 = (f32[2,128,128]{2,1,0:T(8,128)S(1)}, f32[2,128,128]{2,1,0:T(8,128)S(1)}, u32[]{:S(2)}, u32[]{:S(2)}) collective-permute-start(f32[2,128,128]{2,1,0:T(8,128)S(1)} %get-tuple-element.37), channel_id=1, source_target_pairs={{0,64},{64,0},{1,65},{65,1},{2,66},{66,2},{3,67},{67,3},{4,68},{68... | collective-permute-start | bytes 393224 | tf_op jit(solution)/shard_map/ppermute | solution.py:37
  87.2 0.8 copy.14
  (50 shorter events, 4.0 us)
Async XLA Ops:
  0.7 1.1 %copy-start = (bf16[1,640,512]{2,1,0:T(8,128)(2,1)S(1)}, bf16[1,640,512]{2,1,0:T(8,128)(2,1)}, u32[]{:S(2)}) copy-start(bf16[1,640,512]{2,1,0:T(8,128)(2,1)} %param.6) | copy-start | bytes 1966084
  1.8 0.8 copy-start.1
  11.5 13.9 %collective-permute-start.3 = (bf16[1,2,4,2,256,128]{5,4,3,2,1,0:T(8,128)(2,1)S(1)}, bf16[1,2,4,2,256,128]{5,4,3,2,1,0:T(8,128)(2,1)S(1)}, u32[]{:S(2)}, u32[]{:S(2)}) collective-permute-start(bf16[1,2,4,2,256,128]{5,4,3,2,1,0:T(8,128)(2,1)S(1)} %get-tuple-element.19), channel_id=1, source_target_pairs={{0,64},{64,0},{1,65},{65,1},{2,66},{66,2},{3,67},{67,3},{4,68},{68... | collective-permute-start | bytes 3145736 | tf_op jit(solution)/shard_map/ppermute | solution.py:37
  18.0 8.8 %collective-permute-start.10 = (bf16[2,1,4,2,256,128]{5,4,3,2,1,0:T(8,128)(2,1)S(1)}, bf16[2,1,4,2,256,128]{5,4,3,2,1,0:T(8,128)(2,1)S(1)}, u32[]{:S(2)}, u32[]{:S(2)}) collective-permute-start(bf16[2,1,4,2,256,128]{5,4,3,2,1,0:T(8,128)(2,1)S(1)} %get-tuple-element.21), channel_id=1, source_target_pairs={{0,64},{64,0},{1,65},{65,1},{2,66},{66,2},{3,67},{67,3},{4,68},{68... | collective-permute-start | bytes 3145736 | tf_op jit(solution)/shard_map/ppermute | solution.py:37
  21.4 22.8 %copy-start.2 = (f32[128,128]{1,0:T(8,128)S(1)}, f32[128,128]{1,0:T(8,128)}, u32[]{:S(2)}) copy-start(f32[128,128]{1,0:T(8,128)} %param.9) | copy-start | bytes 196612
  21.4 8.8 %collective-permute-start.1 = (bf16[2,1,4,2,256,128]{5,4,3,2,1,0:T(8,128)(2,1)S(1)}, bf16[2,1,4,2,256,128]{5,4,3,2,1,0:T(8,128)(2,1)S(1)}, u32[]{:S(2)}, u32[]{:S(2)}) collective-permute-start(bf16[2,1,4,2,256,128]{5,4,3,2,1,0:T(8,128)(2,1)S(1)} %get-tuple-element.17), channel_id=1, source_target_pairs={{0,64},{64,0},{1,65},{65,1},{2,66},{66,2},{3,67},{67,3},{4,68},{68... | collective-permute-start | bytes 3145736 | tf_op jit(solution)/shard_map/ppermute | solution.py:37
  25.3 53.3 %copy-start.3 = (bf16[128,512]{1,0:T(8,128)(2,1)S(1)}, bf16[128,512]{1,0:T(8,128)(2,1)}, u32[]{:S(2)}) copy-start(bf16[128,512]{1,0:T(8,128)(2,1)} %param.8) | copy-start | bytes 393220
  25.3 19.1 %collective-permute-start = (bf16[1,2,4,2,256,128]{5,4,3,2,1,0:T(8,128)(2,1)S(1)}, bf16[1,2,4,2,256,128]{5,4,3,2,1,0:T(8,128)(2,1)S(1)}, u32[]{:S(2)}, u32[]{:S(2)}) collective-permute-start(bf16[1,2,4,2,256,128]{5,4,3,2,1,0:T(8,128)(2,1)S(1)} %get-tuple-element.15), channel_id=1, source_target_pairs={{0,64},{64,0},{1,65},{65,1},{2,66},{66,2},{3,67},{67,3},{4,68},{68... | collective-permute-start | bytes 3145736 | tf_op jit(solution)/shard_map/ppermute | solution.py:37
  25.7 12.0 %collective-permute-start.12 = (bf16[4,2,256,128]{3,2,1,0:T(8,128)(2,1)S(1)}, bf16[4,2,256,128]{3,2,1,0:T(8,128)(2,1)S(1)}, u32[]{:S(2)}, u32[]{:S(2)}) collective-permute-start(bf16[4,2,256,128]{3,2,1,0:T(8,128)(2,1)S(1)} %get-tuple-element.28), channel_id=1, source_target_pairs={{0,1},{1,2},{2,3},{3,0},{64,67},{65,64},{66,65},{67,66},{4,5},{5,6... | collective-permute-start | bytes 1572872 | tf_op jit(solution)/shard_map/ppermute | solution.py:33
  27.7 16.6 %collective-permute-start.11 = (bf16[4,2,256,128]{3,2,1,0:T(8,128)(2,1)}, bf16[4,2,256,128]{3,2,1,0:T(8,128)(2,1)}, u32[]{:S(2)}, u32[]{:S(2)}) collective-permute-start(bf16[4,2,256,128]{3,2,1,0:T(8,128)(2,1)} %fusion.8), channel_id=1, source_target_pairs={{0,3},{1,0},{2,1},{3,2},{64,65},{65,66},{66,67},{67,64},{4,7},{5,4... | collective-permute-start | bytes 1572872 | tf_op jit(solution)/shard_map/ppermute | solution.py:33
  28.2 10.9 %collective-permute-start.4 = (bf16[4,2,256,128]{3,2,1,0:T(8,128)(2,1)S(1)}, bf16[4,2,256,128]{3,2,1,0:T(8,128)(2,1)S(1)}, u32[]{:S(2)}, u32[]{:S(2)}) collective-permute-start(bf16[4,2,256,128]{3,2,1,0:T(8,128)(2,1)S(1)} %get-tuple-element.29), channel_id=1, source_target_pairs={{0,16},{16,32},{32,48},{48,0},{64,112},{80,64},{96,80},{112,96},{1... | collective-permute-start | bytes 1572872 | tf_op jit(solution)/shard_map/ppermute | solution.py:33
  31.2 14.7 %collective-permute-start.2 = (bf16[4,2,256,128]{3,2,1,0:T(8,128)(2,1)}, bf16[4,2,256,128]{3,2,1,0:T(8,128)(2,1)}, u32[]{:S(2)}, u32[]{:S(2)}) collective-permute-start(bf16[4,2,256,128]{3,2,1,0:T(8,128)(2,1)} %fusion.6), channel_id=1, source_target_pairs={{0,48},{16,0},{32,16},{48,32},{64,80},{80,96},{96,112},{112,64},{1... | collective-permute-start | bytes 1572872 | tf_op jit(solution)/shard_map/ppermute | solution.py:33
  38.7 8.6 %collective-permute-start.13 = (bf16[4,2,256,128]{3,2,1,0:T(8,128)(2,1)}, bf16[4,2,256,128]{3,2,1,0:T(8,128)(2,1)}, u32[]{:S(2)}, u32[]{:S(2)}) collective-permute-start(bf16[4,2,256,128]{3,2,1,0:T(8,128)(2,1)} %fusion), channel_id=1, source_target_pairs={{0,1},{1,2},{2,3},{3,0},{64,67},{65,64},{66,65},{67,66},{4,5},{5,6... | collective-permute-start | bytes 1572872 | tf_op jit(solution)/shard_map/ppermute | solution.py:33
  40.1 10.6 %collective-permute-start.5 = (bf16[4,2,256,128]{3,2,1,0:T(8,128)(2,1)}, bf16[4,2,256,128]{3,2,1,0:T(8,128)(2,1)}, u32[]{:S(2)}, u32[]{:S(2)}) collective-permute-start(bf16[4,2,256,128]{3,2,1,0:T(8,128)(2,1)} %fusion.3), channel_id=1, source_target_pairs={{0,16},{16,32},{32,48},{48,0},{64,112},{80,64},{96,80},{112,96},{1... | collective-permute-start | bytes 1572872 | tf_op jit(solution)/shard_map/ppermute | solution.py:33
  52.9 7.6 %collective-permute-start.16 = (bf16[2,256,128]{2,1,0:T(8,128)(2,1)S(1)}, bf16[2,256,128]{2,1,0:T(8,128)(2,1)S(1)}, u32[]{:S(2)}, u32[]{:S(2)}) collective-permute-start(bf16[2,256,128]{2,1,0:T(8,128)(2,1)S(1)} %get-tuple-element.31), channel_id=1, source_target_pairs={{0,48},{16,0},{32,16},{48,32},{64,80},{80,96},{96,112},{112,64},{1... | collective-permute-start | bytes 393224 | tf_op jit(solution)/shard_map/ppermute | solution.py:33
  53.9 7.7 %collective-permute-start.15 = (bf16[2,256,128]{2,1,0:T(8,128)(2,1)S(1)}, bf16[2,256,128]{2,1,0:T(8,128)(2,1)S(1)}, u32[]{:S(2)}, u32[]{:S(2)}) collective-permute-start(bf16[2,256,128]{2,1,0:T(8,128)(2,1)S(1)} %get-tuple-element.32), channel_id=1, source_target_pairs={{0,16},{16,32},{32,48},{48,0},{64,112},{80,64},{96,80},{112,96},{1... | collective-permute-start | bytes 393224 | tf_op jit(solution)/shard_map/ppermute | solution.py:33
  56.3 5.3 %collective-permute-start.14 = (bf16[2,256,128]{2,1,0:T(8,128)(2,1)S(1)}, bf16[2,256,128]{2,1,0:T(8,128)(2,1)S(1)}, u32[]{:S(2)}, u32[]{:S(2)}) collective-permute-start(bf16[2,256,128]{2,1,0:T(8,128)(2,1)S(1)} %get-tuple-element.30), channel_id=1, source_target_pairs={{0,32},{16,48},{32,0},{48,16},{64,96},{80,112},{96,64},{112,80},{1... | collective-permute-start | bytes 393224 | tf_op jit(solution)/shard_map/ppermute | solution.py:33
  57.3 8.9 %collective-permute-start.8 = (bf16[2,256,128]{2,1,0:T(8,128)(2,1)S(1)}, bf16[2,256,128]{2,1,0:T(8,128)(2,1)S(1)}, u32[]{:S(2)}, u32[]{:S(2)}) collective-permute-start(bf16[2,256,128]{2,1,0:T(8,128)(2,1)S(1)} %get-tuple-element.34), channel_id=1, source_target_pairs={{0,3},{1,0},{2,1},{3,2},{64,65},{65,66},{66,67},{67,64},{4,7},{5,4... | collective-permute-start | bytes 393224 | tf_op jit(solution)/shard_map/ppermute | solution.py:33
  57.4 8.8 %collective-permute-start.7 = (bf16[2,256,128]{2,1,0:T(8,128)(2,1)S(1)}, bf16[2,256,128]{2,1,0:T(8,128)(2,1)S(1)}, u32[]{:S(2)}, u32[]{:S(2)}) collective-permute-start(bf16[2,256,128]{2,1,0:T(8,128)(2,1)S(1)} %get-tuple-element.35), channel_id=1, source_target_pairs={{0,1},{1,2},{2,3},{3,0},{64,67},{65,64},{66,65},{67,66},{4,5},{5,6... | collective-permute-start | bytes 393224 | tf_op jit(solution)/shard_map/ppermute | solution.py:33
  60.4 5.7 %collective-permute-start.6 = (bf16[2,256,128]{2,1,0:T(8,128)(2,1)S(1)}, bf16[2,256,128]{2,1,0:T(8,128)(2,1)S(1)}, u32[]{:S(2)}, u32[]{:S(2)}) collective-permute-start(bf16[2,256,128]{2,1,0:T(8,128)(2,1)S(1)} %get-tuple-element.33), channel_id=1, source_target_pairs={{0,2},{1,3},{2,0},{3,1},{64,66},{65,67},{66,64},{67,65},{4,6},{5,7... | collective-permute-start | bytes 393224 | tf_op jit(solution)/shard_map/ppermute | solution.py:33
  61.8 5.8 %collective-permute-start.18 = (bf16[256,128]{1,0:T(8,128)(2,1)S(1)}, bf16[256,128]{1,0:T(8,128)(2,1)S(1)}, u32[]{:S(2)}, u32[]{:S(2)}) collective-permute-start(bf16[256,128]{1,0:T(8,128)(2,1)S(1)} %get-tuple-element.39), channel_id=1, source_target_pairs={{0,12},{4,0},{8,4},{12,8},{1,13},{5,1},{9,5},{13,9},{2,14},{6,2},{... | collective-permute-start | bytes 196616 | tf_op jit(solution)/shard_map/ppermute | solution.py:28
  66.2 4.3 %collective-permute-start.17 = (bf16[256,128]{1,0:T(8,128)(2,1)S(1)}, bf16[256,128]{1,0:T(8,128)(2,1)S(1)}, u32[]{:S(2)}, u32[]{:S(2)}) collective-permute-start(bf16[256,128]{1,0:T(8,128)(2,1)S(1)} %get-tuple-element.38), channel_id=1, source_target_pairs={{0,8},{4,12},{8,0},{12,4},{1,9},{5,13},{9,1},{13,5},{2,10},{6,14},... | collective-permute-start | bytes 196616 | tf_op jit(solution)/shard_map/ppermute | solution.py:28
  66.3 5.8 %collective-permute-start.9 = (bf16[256,128]{1,0:T(8,128)(2,1)S(1)}, bf16[256,128]{1,0:T(8,128)(2,1)S(1)}, u32[]{:S(2)}, u32[]{:S(2)}) collective-permute-start(bf16[256,128]{1,0:T(8,128)(2,1)S(1)} %fusion.17), channel_id=1, source_target_pairs={{0,4},{4,8},{8,12},{12,0},{1,5},{5,9},{9,13},{13,1},{2,6},{6,10},{... | collective-permute-start | bytes 196616 | tf_op jit(solution)/shard_map/ppermute | solution.py:28
  72.2 8.4 %collective-permute-start.19 = (bf16[2,128,128]{2,1,0:T(8,128)(2,1)S(1)}, bf16[2,128,128]{2,1,0:T(8,128)(2,1)S(1)}, u32[]{:S(2)}, u32[]{:S(2)}) collective-permute-start(bf16[2,128,128]{2,1,0:T(8,128)(2,1)S(1)} %add_convert_fusion.4), channel_id=1, source_target_pairs={{0,128},{128,0},{1,129},{129,1},{2,130},{130,2},{3,131},{131,3},{4... | collective-permute-start | bytes 196616 | tf_op jit(solution)/shard_map/ppermute | solution.py:37
  80.6 6.5 %collective-permute-start.20 = (f32[2,128,128]{2,1,0:T(8,128)S(1)}, f32[2,128,128]{2,1,0:T(8,128)S(1)}, u32[]{:S(2)}, u32[]{:S(2)}) collective-permute-start(f32[2,128,128]{2,1,0:T(8,128)S(1)} %get-tuple-element.37), channel_id=1, source_target_pairs={{0,64},{64,0},{1,65},{65,1},{2,66},{66,2},{3,67},{67,3},{4,68},{68... | collective-permute-start | bytes 393224 | tf_op jit(solution)/shard_map/ppermute | solution.py:37
